TPU v7x, 128 devices: a whole 4x4x4 slice. The times are simulated.
128 devices in a mesh: up: 16 (over y_lo, x, core), dn: 8 (over y_hi, z).
Axes of the slice: x: 4, y: 4 (y_hi: 2, y_lo: 2; y = y_hi * 2 + y_lo), z: 4, core: 2. Of those that a mesh axis runs over, the one named last changes fastest.
Arguments:
- start_vector: bfloat16 [13312, 13312], P('up', 'dn'), may hold values from -6 to 6
- hop_tiles: bfloat16 [104, 5, 128, 128], replicated, may hold values from -0.5 to 0.5
- tile_columns: int32 [104, 5], replicated, may hold values from 0 to 103, as said below
- tile_signs: int32 [104, 5], replicated, may hold values from 0 to 1
- occupation: int32 [16, 13312], replicated, may hold values from 0 to 1, as said below
Outputs:
- next_vector: bfloat16 [13312, 13312], P('up', 'dn')
- alphas: float32 [2], replicated
- betas: float32 [2], replicated
Inputs may be any that keep to these rules, and one draw needn't show every extreme that they name: Each row of tile_columns names 5 different tile columns. Every column of occupation holds exactly 8 ones.
All inputs are finite; a program needn't handle non-finite values.
Results may differ from a plain program's by a relative error of at most 0.0065.
Values may be sent and summed in bfloat16 or wider, within the bound.
No kernel may reach another device: no remote copies, remote signals or barrier semaphores. Data moves between devices by JAX's collectives and lax.ppermute only.
A program may use at most 192 MiB of HBM per device.

v0:
```python
import functools

import jax
import jax.numpy as jnp
from jax import lax
from jax.sharding import Mesh
from jax.sharding import PartitionSpec as P

STEPS = 2
UP = ("up_0", "up_1", "up_2")
DN = ("dn_0", "dn_1")
UP_DN = ("up_0", "up_1", "up_2", "dn_0", "dn_1")


coupling = 4.0


def split_up(value, dim, peers):
    before, after = (value.shape[:dim], value.shape[dim + 1 :])
    return jnp.moveaxis(value.reshape(*before, peers, -1, *after), dim, 0)


def joined_along(pieces, dim):
    pieces = jnp.moveaxis(pieces, 0, dim)
    shape = pieces.shape
    return pieces.reshape(*shape[:dim], shape[dim] * shape[dim + 1], *shape[dim + 2 :])


def moved_by_axis(pieces, axes, order):
    inside = pieces.shape[1:]
    whole = pieces.reshape(*(lax.axis_size(a) for a in axes), *inside)
    for k in order:
        whole = lax.all_to_all(whole, axes[k], k, k, tiled=True)
    return whole.reshape(-1, *inside)


def exchange_by_chip(value, groups, order, split_dim, concat_dim):
    peers = lax.axis_size(groups[0]) * lax.axis_size(groups[1])
    pieces = split_up(value, split_dim, peers)
    return joined_along(moved_by_axis(pieces, groups, order), concat_dim)


def edges_of(length, count):
    step = length // count
    if step >= 8:
        step -= step % 8
    return [step * k for k in range(1, count)]


def cut_exchange(value, axis, pieces, split_dim, concat_dim):
    blocks = split_up(value, split_dim, lax.axis_size(axis))
    cut = max(range(1, max(2, blocks.ndim - 1)), key=lambda d: blocks.shape[d])
    gathered = []
    for piece in jnp.split(blocks, edges_of(blocks.shape[cut], pieces), axis=cut):
        if piece.size:
            gathered.append(lax.all_to_all(piece, axis, split_axis=0, concat_axis=0, tiled=True))
    return joined_along(jnp.concatenate(gathered, axis=cut), concat_dim)


def one_axis_at_a_time(value, axes):
    return functools.reduce(lax.psum, axes, value)


def hop_lead(matrix, signed, tile_columns):
    layout = matrix.shape
    tile_width = signed.shape[-1]
    cube = matrix.reshape(layout[0] // tile_width, tile_width, -1)
    picked = cube[tile_columns]
    result = jnp.einsum("ikab,ikbm->iam", signed, picked, preferred_element_type=jnp.float32)
    return result.reshape(layout).astype(jnp.bfloat16)


def body(start_vector, hop_tiles, tile_columns, tile_signs, occupation):
    signed = hop_tiles * (1 - 2 * tile_signs).astype(jnp.bfloat16)[:, :, None, None]
    rows_local, cols_local = start_vector.shape
    count_up = lax.axis_size(UP)
    count_down = lax.axis_size(DN)
    row_start = lax.axis_index(UP) * rows_local
    col_start = lax.axis_index(DN) * cols_local
    block_rows, block_cols = start_vector.shape
    occ_rows = lax.dynamic_slice_in_dim(occupation, row_start, block_rows, 1).astype(jnp.bfloat16)
    occ_cols = lax.dynamic_slice_in_dim(occupation, col_start, block_cols, 1).astype(jnp.bfloat16)
    diagonal = coupling * jnp.einsum(
        "sa,sb->ab", occ_rows, occ_cols, preferred_element_type=jnp.float32
    )
    vector = start_vector.astype(jnp.float32)
    total = one_axis_at_a_time(jnp.sum(vector * vector), UP_DN)
    vector = vector / jnp.maximum(jnp.sqrt(total), 1.0)
    length = total / jnp.maximum(total, 1.0)
    previous = jnp.zeros_like(vector)
    beta_value = jnp.float32(0.0)
    alpha_list = []
    beta_list = []
    for iteration in range(STEPS):
        rounded = vector.astype(jnp.bfloat16)
        cube = rounded.reshape(block_rows, count_up, block_cols // count_up)
        up_part = lax.all_to_all(cube, UP, split_axis=1, concat_axis=0, tiled=True)
        up_whole = up_part.reshape(up_part.shape[0], up_part.shape[2])
        up_hopped = hop_lead(up_whole, signed, tile_columns).reshape(up_part.shape)
        moved = exchange_by_chip(up_hopped, (("up_0", "up_1"), "up_2"), (1, 0), 0, 1)
        hopped_up = moved.reshape(block_rows, block_cols)
        flipped = rounded.T.reshape(block_cols, count_down, block_rows // count_down)
        part = lax.all_to_all(flipped, DN, split_axis=1, concat_axis=0, tiled=True)
        whole = part.reshape(part.shape[0], part.shape[2])
        hopped = hop_lead(whole, signed, tile_columns).reshape(part.shape)
        returned = cut_exchange(hopped, DN, 2, 0, 1)
        hopped_down = returned.reshape(block_cols, block_rows).T
        work = (
            hopped_up.astype(jnp.float32)
            + hopped_down.astype(jnp.float32)
            + diagonal * vector
            - beta_value * previous
        )
        intersect, square = (
            one_axis_at_a_time(jnp.sum(work * vector), UP_DN),
            one_axis_at_a_time(jnp.sum(work * work), UP_DN),
        )
        work = work - intersect * vector
        residual = square - 2.0 * intersect * intersect + intersect * intersect * length
        beta_value = jnp.sqrt(jnp.maximum(residual, 1.0))
        length = residual / jnp.maximum(residual, 1.0)
        previous = vector
        vector = work / beta_value
        alpha_list.append(intersect)
        beta_list.append(beta_value)
    final = vector.astype(jnp.bfloat16)
    return (final, jnp.stack(alpha_list), jnp.stack(beta_list))


def solution(mesh):
    torus = Mesh(mesh.devices.reshape(2, 4, 2, 2, 4), ("up_0", "up_1", "up_2", "dn_0", "dn_1"))
    return jax.shard_map(
        body,
        mesh=torus,
        in_specs=(P(UP, DN), P(), P(), P(), P()),
        out_specs=(P(UP, DN), P(), P()),
        check_vma=False,
    )
```

profile of v0, /device:TPU:24, one launch (start us, length us, event | category | flops | bytes accessed | tf_op | source)
XLA Modules:
  0.0 686.6 jit_solution(5031893322592115355)
XLA Ops:
  10.0 11.1 %psum.176 = f32[]{:T(128)} all-reduce(f32[]{:T(128)} %psum.175), channel_id=1, replica_groups=mesh['up_0'=2,'up_1'=4,'up_2'=2,'dn_0'=2,'dn_1'=4] {'up_1'}, use_global_device_ids=true, to_apply=%region_2.0 | all-reduce | flops 1 | bytes 8 | tf_op jit(solution)/shard_map/psum | solution.py:61
  24.2 7.1 %psum.178 = f32[]{:T(128)} all-reduce(f32[]{:T(128)} %psum.177), channel_id=1, replica_groups=mesh['up_0'=2,'up_1'=4,'up_2'=2,'dn_0'=2,'dn_1'=4] {'dn_0'}, use_global_device_ids=true, to_apply=%region_4.0 | all-reduce | flops 1 | bytes 8 | tf_op jit(solution)/shard_map/psum | solution.py:61
  31.2 12.4 %psum.179 = f32[]{:T(128)} all-reduce(f32[]{:T(128)} %psum.178), channel_id=1, replica_groups=mesh['up_0'=2,'up_1'=4,'up_2'=2,'dn_0'=2,'dn_1'=4] {'dn_1'}, use_global_device_ids=true, to_apply=%region_5.0 | all-reduce | flops 1 | bytes 8 | tf_op jit(solution)/shard_map/psum | solution.py:61
  59.0 24.2 %all-to-all-done.3 = bf16[1664,8,104]{0,2,1:T(8,128)(2,1)S(1)} async-done(((bf16[1664,8,104]{0,2,1:T(8,128)(2,1)}), bf16[1664,8,104]{0,2,1:T(8,128)(2,1)S(1)}, u32[]{:S(2)}, u32[]{:S(2)}) %all-to-all-start.3) | async-done | bytes 2768928 | tf_op jit(solution)/shard_map/all_to_all | solution.py:103
  99.0 20.0 %gather_fusion.1 = bf16[520,128,104]{1,2,0:T(8,128)(2,1)} fusion(bf16[104,128,104]{1,2,0:T(8,128)(2,1)S(1)} %copy.67, s32[1024]{0:T(1024)S(1)} %pad_clamp_fusion), kind=kCustom, calls=%fused_computation.1 | custom fusion | bytes 27691040 | tf_op jit(solution)/shard_map/gather | solution.py:68
  118.9 13.1 %bitcast_convert_fusion.2 = bf16[104,128,104]{1,2,0:T(8,128)(2,1)S(1)} fusion(bf16[104,5,128,104]{2,3,1,0:T(8,128)(2,1)} %bitcast.104, bf16[104,5,128,128]{3,2,1,0:T(8,128)(2,1)} %param.6, bf16[104,5]{1,0:T(8,128)(2,1)S(1)} %copy.57), kind=kOutput, calls=%fused_computation.26 | convolution fusion | flops 1781997568 | bytes 33653776 | tf_op jit(solution)/shard_map/ikab,ikbm->iam/dot_general | solution.py:69
  151.2 20.0 %gather_fusion = bf16[520,128,104]{1,2,0:T(8,128)(2,1)} fusion(bf16[104,128,104]{1,2,0:T(8,128)(2,1)S(1)} %copy.61, s32[1024]{0:T(1024)S(1)} %pad_clamp_fusion), kind=kCustom, calls=%fused_computation | custom fusion | bytes 27691040 | tf_op jit(solution)/shard_map/gather | solution.py:68
  171.1 13.0 %bitcast_convert_fusion.3 = bf16[104,128,104]{1,2,0:T(8,128)(2,1)S(1)} fusion(bf16[104,5,128,104]{2,3,1,0:T(8,128)(2,1)} %bitcast.105, bf16[104,5,128,128]{3,2,1,0:T(8,128)(2,1)} %param.6, bf16[104,5]{1,0:T(8,128)(2,1)S(1)} %copy.57), kind=kOutput, calls=%fused_computation.27 | convolution fusion | flops 1781997568 | bytes 33653776 | tf_op jit(solution)/shard_map/ikab,ikbm->iam/dot_general | solution.py:69
  186.1 6.4 convert_element_type.125
  207.5 17.0 %all-to-all-done.4 = bf16[8,832,1,104]{1,3,2,0:T(8,128)(2,1)} async-done(((bf16[8,832,1,104]{1,3,2,0:T(8,128)(2,1)}), bf16[8,832,1,104]{1,3,2,0:T(8,128)(2,1)}, u32[]{:S(2)}, u32[]{:S(2)}) %all-to-all-start.4) | async-done | bytes 1384480 | tf_op jit(solution)/shard_map/all_to_all | solution.py:56
  235.0 14.6 %all-to-all-done.5 = bf16[8,832,1,104]{1,3,2,0:T(8,128)(2,1)} async-done(((bf16[8,832,1,104]{1,3,2,0:T(8,128)(2,1)}), bf16[8,832,1,104]{1,3,2,0:T(8,128)(2,1)}, u32[]{:S(2)}, u32[]{:S(2)}) %all-to-all-start.5) | async-done | bytes 1384480 | tf_op jit(solution)/shard_map/all_to_all | solution.py:56
  261.7 28.5 %all-to-all-done.2 = bf16[8,2,832,1,104]{2,1,4,3,0:T(2,128)(2,1)S(1)} async-done(((bf16[8,2,832,1,104]{2,1,4,3,0:T(2,128)(2,1)}), bf16[8,2,832,1,104]{2,1,4,3,0:T(2,128)(2,1)S(1)}, u32[]{:S(2)}, u32[]{:S(2)}) %all-to-all-start.2) | async-done | bytes 2768928 | tf_op jit(solution)/shard_map/all_to_all | solution.py:33
  293.7 7.2 %copy.71 = f32[832,1664]{1,0:T(8,128)} copy(f32[832,1664]{0,1:T(8,128)} %bitcast.101) | data formatting | bytes 11075584 | tf_op jit(solution)/shard_map/convert_element_type | solution.py:109
  300.9 11.1 %multiply_reduce_fusion.3 = (f32[]{:T(128)}, f32[]{:T(128)}, f32[832,1664]{1,0:T(8,128)}, f32[832,1664]{1,0:T(8,128)}) fusion(f32[]{:T(128)S(6)} %max.13, bf16[832,1664]{1,0:T(8,128)(2,1)S(1)} %copy-done, f32[832,1664]{1,0:T(8,128)} %copy.71, f32[8,1664,1,104]{1,3,2,0:T(8,128)} %maximum_convert_fusion, s32[16,13312]{1,0:T(8,128)} %param.9, ...), kind=kOutput, calls=%fused_computation.33 | convolution fusion | flops 58186752 | bytes 25083924 | tf_op jit(solution)/shard_map/sa,sb->ab/dot_general | solution.py:83
  317.6 17.9 %all-reduce.3 = (f32[]{:T(128)}, f32[]{:T(128)}) all-reduce(f32[]{:T(128)} %get-tuple-element.25, f32[]{:T(128)} %get-tuple-element.26), channel_id=1, replica_groups=mesh['up_0'=2,'up_1'=4,'up_2'=2,'dn_0'=2,'dn_1'=4] {'up_1'}, use_global_device_ids=true, to_apply=%region_14.0 | all-reduce | flops 2 | bytes 16 | tf_op jit(solution)/shard_map/psum | solution.py:61
  338.6 7.1 %all-reduce.5 = (f32[]{:T(128)}, f32[]{:T(128)}) all-reduce(f32[]{:T(128)} %get-tuple-element.21, f32[]{:T(128)} %get-tuple-element.22), channel_id=1, replica_groups=mesh['up_0'=2,'up_1'=4,'up_2'=2,'dn_0'=2,'dn_1'=4] {'dn_0'}, use_global_device_ids=true, to_apply=%region_16.0 | all-reduce | flops 2 | bytes 16 | tf_op jit(solution)/shard_map/psum | solution.py:61
  345.7 11.1 %all-reduce.1 = (f32[]{:T(128)}, f32[]{:T(128)}) all-reduce(f32[]{:T(128)} %get-tuple-element.17, f32[]{:T(128)} %get-tuple-element.18), channel_id=1, replica_groups=mesh['up_0'=2,'up_1'=4,'up_2'=2,'dn_0'=2,'dn_1'=4] {'dn_1'}, use_global_device_ids=true, to_apply=%region_17.0 | all-reduce | flops 2 | bytes 16 | tf_op jit(solution)/shard_map/psum | solution.py:61
  360.2 7.6 %fusion.28 = (bf16[832,1664]{1,0:T(8,128)(2,1)}, f32[832,1664]{1,0:T(8,128)}) fusion(f32[]{:T(128)} %sqrt.10, f32[832,1664]{1,0:T(8,128)} %get-tuple-element.30, f32[]{:T(128)S(6)} %max.13, bf16[832,1664]{1,0:T(8,128)(2,1)S(1)} %copy-done, f32[]{:T(128)} %get-tuple-element.10), kind=kLoop, calls=%fused_computation.48 | loop fusion | flops 8306688 | bytes 16613388 | tf_op jit(solution)/shard_map/convert_element_type | solution.py:95
  376.7 26.4 %all-to-all-done.9 = bf16[1664,8,104]{0,2,1:T(8,128)(2,1)} async-done(((bf16[1664,8,104]{0,2,1:T(8,128)(2,1)}), bf16[1664,8,104]{0,2,1:T(8,128)(2,1)}, u32[]{:S(2)}, u32[]{:S(2)}) %all-to-all-start.9) | async-done | bytes 2768928 | tf_op jit(solution)/shard_map/all_to_all | solution.py:103
  416.6 20.0 %gather_fusion.3 = bf16[520,128,104]{1,2,0:T(8,128)(2,1)} fusion(bf16[104,128,104]{1,2,0:T(8,128)(2,1)S(1)} %copy.80, s32[1024]{0:T(1024)S(1)} %pad_clamp_fusion), kind=kCustom, calls=%fused_computation.3 | custom fusion | bytes 27691040 | tf_op jit(solution)/shard_map/gather | solution.py:68
  436.5 13.1 %bitcast_convert_fusion = bf16[104,128,104]{1,2,0:T(8,128)(2,1)S(1)} fusion(bf16[104,5,128,104]{2,3,1,0:T(8,128)(2,1)} %bitcast.106, bf16[104,5,128,128]{3,2,1,0:T(8,128)(2,1)} %param.6, bf16[104,5]{1,0:T(8,128)(2,1)S(1)} %copy.57), kind=kOutput, calls=%fused_computation.24 | convolution fusion | flops 1781997568 | bytes 33653776 | tf_op jit(solution)/shard_map/ikab,ikbm->iam/dot_general | solution.py:69
  468.6 20.0 %gather_fusion.2 = bf16[520,128,104]{1,2,0:T(8,128)(2,1)} fusion(bf16[104,128,104]{1,2,0:T(8,128)(2,1)S(1)} %copy.74, s32[1024]{0:T(1024)S(1)} %pad_clamp_fusion), kind=kCustom, calls=%fused_computation.2 | custom fusion | bytes 27691040 | tf_op jit(solution)/shard_map/gather | solution.py:68
  488.6 13.1 %bitcast_convert_fusion.1 = bf16[104,128,104]{1,2,0:T(8,128)(2,1)S(1)} fusion(bf16[104,5,128,104]{2,3,1,0:T(8,128)(2,1)} %bitcast.103, bf16[104,5,128,128]{3,2,1,0:T(8,128)(2,1)} %param.6, bf16[104,5]{1,0:T(8,128)(2,1)S(1)} %copy.57), kind=kOutput, calls=%fused_computation.25 | convolution fusion | flops 1781997568 | bytes 33653776 | tf_op jit(solution)/shard_map/ikab,ikbm->iam/dot_general | solution.py:69
  524.9 17.0 %all-to-all-done.10 = bf16[8,832,1,104]{1,3,2,0:T(8,128)(2,1)} async-done(((bf16[8,832,1,104]{1,3,2,0:T(8,128)(2,1)}), bf16[8,832,1,104]{1,3,2,0:T(8,128)(2,1)}, u32[]{:S(2)}, u32[]{:S(2)}) %all-to-all-start.10) | async-done | bytes 1384480 | tf_op jit(solution)/shard_map/all_to_all | solution.py:56
  552.4 14.6 %all-to-all-done.11 = bf16[8,832,1,104]{1,3,2,0:T(8,128)(2,1)} async-done(((bf16[8,832,1,104]{1,3,2,0:T(8,128)(2,1)}), bf16[8,832,1,104]{1,3,2,0:T(8,128)(2,1)}, u32[]{:S(2)}, u32[]{:S(2)}) %all-to-all-start.11) | async-done | bytes 1384480 | tf_op jit(solution)/shard_map/all_to_all | solution.py:56
  577.8 29.8 %all-to-all-done.8 = bf16[8,2,832,1,104]{2,1,4,3,0:T(2,128)(2,1)S(1)} async-done(((bf16[8,2,832,1,104]{2,1,4,3,0:T(2,128)(2,1)}), bf16[8,2,832,1,104]{2,1,4,3,0:T(2,128)(2,1)S(1)}, u32[]{:S(2)}, u32[]{:S(2)}) %all-to-all-start.8) | async-done | bytes 2768928 | tf_op jit(solution)/shard_map/all_to_all | solution.py:33
  611.1 7.2 %copy.84 = f32[832,1664]{1,0:T(8,128)} copy(f32[832,1664]{0,1:T(8,128)} %bitcast.102) | data formatting | bytes 11075584 | tf_op jit(solution)/shard_map/convert_element_type | solution.py:109
  618.3 11.7 %multiply_reduce_fusion.1 = (f32[]{:T(128)}, f32[]{:T(128)}, f32[832,1664]{1,0:T(8,128)}) fusion(f32[832,1664]{1,0:T(8,128)} %get-tuple-element.29, f32[]{:T(128)S(6)} %max.13, bf16[832,1664]{1,0:T(8,128)(2,1)S(1)} %copy-done.1, f32[]{:T(128)} %sqrt.10, f32[832,1664]{1,0:T(8,128)} %get-tuple-element.35, f32[832,1664]{1,0:T(8,128)} %copy.84, ...), kind=kLoop, calls=%fused_computation.30 | loop fusion | flops 16613374 | bytes 30457872 | tf_op jit(solution)/shard_map/reduce_sum | solution.py:115
  635.6 17.9 %all-reduce.2 = (f32[]{:T(128)}, f32[]{:T(128)}) all-reduce(f32[]{:T(128)} %get-tuple-element.23, f32[]{:T(128)} %get-tuple-element.24), channel_id=1, replica_groups=mesh['up_0'=2,'up_1'=4,'up_2'=2,'dn_0'=2,'dn_1'=4] {'up_1'}, use_global_device_ids=true, to_apply=%region_26.0 | all-reduce | flops 2 | bytes 16 | tf_op jit(solution)/shard_map/psum | solution.py:61
  656.6 7.1 %all-reduce.4 = (f32[]{:T(128)}, f32[]{:T(128)}) all-reduce(f32[]{:T(128)} %get-tuple-element.19, f32[]{:T(128)} %get-tuple-element.20), channel_id=1, replica_groups=mesh['up_0'=2,'up_1'=4,'up_2'=2,'dn_0'=2,'dn_1'=4] {'dn_0'}, use_global_device_ids=true, to_apply=%region_28.0 | all-reduce | flops 2 | bytes 16 | tf_op jit(solution)/shard_map/psum | solution.py:61
  663.7 11.0 %all-reduce = (f32[]{:T(128)}, f32[]{:T(128)}) all-reduce(f32[]{:T(128)} %get-tuple-element.15, f32[]{:T(128)} %get-tuple-element.16), channel_id=1, replica_groups=mesh['up_0'=2,'up_1'=4,'up_2'=2,'dn_0'=2,'dn_1'=4] {'dn_1'}, use_global_device_ids=true, to_apply=%region_29.0 | all-reduce | flops 2 | bytes 16 | tf_op jit(solution)/shard_map/psum | solution.py:61
  677.6 7.0 %divide_convert_fusion = bf16[832,1664]{1,0:T(8,128)(2,1)} fusion(f32[832,1664]{1,0:T(8,128)} %get-tuple-element.27, f32[832,1664]{1,0:T(8,128)} %get-tuple-element.29, f32[]{:T(128)} %sqrt.11, f32[]{:T(128)} %get-tuple-element.8), kind=kLoop, calls=%fused_computation.28 | loop fusion | flops 5537792 | bytes 13844488 | tf_op jit(solution)/shard_map/convert_element_type | solution.py:126
  (76 shorter events, 212.2 us)
Async XLA Ops:
  48.1 10.6 %copy-start.4 = (s32[104,5]{0,1:T(8,128)S(1)}, s32[104,5]{0,1:T(8,128)}, u32[]{:S(2)}) copy-start(s32[104,5]{0,1:T(8,128)} %param.7) | copy-start | bytes 6244
  48.1 10.9 %copy-start.3 = (s32[104,5]{0,1:T(8,128)S(1)}, s32[104,5]{0,1:T(8,128)}, u32[]{:S(2)}) copy-start(s32[104,5]{0,1:T(8,128)} %param.8) | copy-start | bytes 6244
  48.1 35.1 %all-to-all-start.3 = ((bf16[1664,8,104]{0,2,1:T(8,128)(2,1)}), bf16[1664,8,104]{0,2,1:T(8,128)(2,1)S(1)}, u32[]{:S(2)}, u32[]{:S(2)}) async-start(bf16[1664,8,104]{0,2,1:T(8,128)(2,1)} %bitcast.10), calls=%async_computation.3 | async-start | bytes 5537792 | tf_op jit(solution)/shard_map/all_to_all | solution.py:103
  83.2 59.1 %all-to-all-start = ((bf16[832,16,104]{0,2,1:T(8,128)(2,1)}), bf16[832,16,104]{0,2,1:T(8,128)(2,1)}, u32[]{:S(2)}, u32[]{:S(2)}) async-start(bf16[832,16,104]{0,2,1:T(8,128)(2,1)} %bitcast), calls=%async_computation | async-start | bytes 5963776 | tf_op jit(solution)/shard_map/all_to_all | solution.py:97
  199.0 25.4 %all-to-all-start.4 = ((bf16[8,832,1,104]{1,3,2,0:T(8,128)(2,1)}), bf16[8,832,1,104]{1,3,2,0:T(8,128)(2,1)}, u32[]{:S(2)}, u32[]{:S(2)}) async-start(bf16[8,832,1,104]{1,3,2,0:T(8,128)(2,1)} %copy.69), calls=%async_computation.4 | async-start | bytes 2981888 | tf_op jit(solution)/shard_map/all_to_all | solution.py:56
  224.5 25.1 %all-to-all-start.5 = ((bf16[8,832,1,104]{1,3,2,0:T(8,128)(2,1)}), bf16[8,832,1,104]{1,3,2,0:T(8,128)(2,1)}, u32[]{:S(2)}, u32[]{:S(2)}) async-start(bf16[8,832,1,104]{1,3,2,0:T(8,128)(2,1)} %copy.70), calls=%async_computation.5 | async-start | bytes 2981888 | tf_op jit(solution)/shard_map/all_to_all | solution.py:56
  249.6 40.6 %all-to-all-start.2 = ((bf16[8,2,832,1,104]{2,1,4,3,0:T(2,128)(2,1)}), bf16[8,2,832,1,104]{2,1,4,3,0:T(2,128)(2,1)S(1)}, u32[]{:S(2)}, u32[]{:S(2)}) async-start(bf16[8,2,832,1,104]{2,1,4,3,0:T(2,128)(2,1)} %copy.64), calls=%async_computation.2 | async-start | bytes 5963776 | tf_op jit(solution)/shard_map/all_to_all | solution.py:33
  293.7 7.2 %copy-start = (bf16[832,1664]{1,0:T(8,128)(2,1)S(1)}, bf16[832,1664]{1,0:T(8,128)(2,1)}, u32[]{:S(2)}) copy-start(bf16[832,1664]{1,0:T(8,128)(2,1)} %param.5) | copy-start | bytes 8306692
  367.8 5.4 copy-start.2
  367.8 35.3 %all-to-all-start.9 = ((bf16[1664,8,104]{0,2,1:T(8,128)(2,1)}), bf16[1664,8,104]{0,2,1:T(8,128)(2,1)}, u32[]{:S(2)}, u32[]{:S(2)}) async-start(bf16[1664,8,104]{0,2,1:T(8,128)(2,1)} %bitcast.100), calls=%async_computation.9 | async-start | bytes 5537792 | tf_op jit(solution)/shard_map/all_to_all | solution.py:103
  403.1 56.7 %all-to-all-start.6 = ((bf16[832,16,104]{0,2,1:T(8,128)(2,1)}), bf16[832,16,104]{0,2,1:T(8,128)(2,1)}, u32[]{:S(2)}, u32[]{:S(2)}) async-start(bf16[832,16,104]{0,2,1:T(8,128)(2,1)} %bitcast.107), calls=%async_computation.6 | async-start | bytes 5963776 | tf_op jit(solution)/shard_map/all_to_all | solution.py:97
  516.5 25.4 %all-to-all-start.10 = ((bf16[8,832,1,104]{1,3,2,0:T(8,128)(2,1)}), bf16[8,832,1,104]{1,3,2,0:T(8,128)(2,1)}, u32[]{:S(2)}, u32[]{:S(2)}) async-start(bf16[8,832,1,104]{1,3,2,0:T(8,128)(2,1)} %copy.82), calls=%async_computation.10 | async-start | bytes 2981888 | tf_op jit(solution)/shard_map/all_to_all | solution.py:56
  541.9 25.1 %all-to-all-start.11 = ((bf16[8,832,1,104]{1,3,2,0:T(8,128)(2,1)}), bf16[8,832,1,104]{1,3,2,0:T(8,128)(2,1)}, u32[]{:S(2)}, u32[]{:S(2)}) async-start(bf16[8,832,1,104]{1,3,2,0:T(8,128)(2,1)} %copy.83), calls=%async_computation.11 | async-start | bytes 2981888 | tf_op jit(solution)/shard_map/all_to_all | solution.py:56
  567.0 40.6 %all-to-all-start.8 = ((bf16[8,2,832,1,104]{2,1,4,3,0:T(2,128)(2,1)}), bf16[8,2,832,1,104]{2,1,4,3,0:T(2,128)(2,1)S(1)}, u32[]{:S(2)}, u32[]{:S(2)}) async-start(bf16[8,2,832,1,104]{2,1,4,3,0:T(2,128)(2,1)} %copy.77), calls=%async_computation.8 | async-start | bytes 5963776 | tf_op jit(solution)/shard_map/all_to_all | solution.py:33
  611.1 7.2 %copy-start.1 = (bf16[832,1664]{1,0:T(8,128)(2,1)S(1)}, bf16[832,1664]{1,0:T(8,128)(2,1)}, u32[]{:S(2)}) copy-start(bf16[832,1664]{1,0:T(8,128)(2,1)} %param.5) | copy-start | bytes 8306692
where the time goes:
time: 692 us; the launch traced here: 687 us
  local copies, waits for them, and re-layouts  193 us (28%)
  waiting for transfers between devices  172 us (25%)
  blocking collectives  141 us (20%)
  matrix products  63.4 us (9%)
  starting transfers between devices  55.9 us (8%)
  other arithmetic  52.2 us (8%)
  between operations  9.48 us (1%)
    psum x15, blocking collectives, one_axis_at_a_time(): return functools.reduce(lax.psum, axes, value)  128 us
    gather x4, local copies, waits for them, and re-layouts, hop_lead(): picked = cube[tile_columns]  79.9 us
    all_to_all x4, waiting for transfers between devices, cut_exchange(): lax.all_to_all(piece, axis, split_axis=0, concat_axis=0, tiled=True)  63.1 us
    all_to_all x2, waiting for transfers between devices, moved_by_axis(): whole = lax.all_to_all(whole, axes[k], k, k, tiled=True)  58.3 us
    dot_general x4, matrix products, hop_lead(): jnp.einsum('ikab,ikbm->iam', signed, picked, preferred_element_type=jnp.f...  52.3 us
    all_to_all x2, waiting for transfers between devices, body(): part = lax.all_to_all(flipped, DN, split_axis=1, concat_axis=0, tiled=True)  50.6 us
    convert_element_type x10, local copies, waits for them, and re-layouts, hop_lead(): return result.reshape(layout).astype(jnp.bfloat16)  31.5 us
    another operation x8, local copies, waits for them, and re-layouts, hop_lead(): cube = matrix.reshape(layout[0] // tile_width, tile_width, -1)  27.8 us
  transfers between devices with their start and end apart: 10, of which 8 were waited for; matrix products, arithmetic and copies ran while one was open for 20% of the time, Pallas kernels for 0%

commit v1 on v0

v1 whole, which is shorter than its diff:
```python
import jax
import jax.numpy as jnp
from jax import lax
from jax.experimental import pallas as pl
from jax.experimental.pallas import tpu as pltpu
from jax.sharding import Mesh
from jax.sharding import PartitionSpec as P

UP = ("up_0", "up_1", "up_2")
DN = ("dn_0", "dn_1")
ALL = UP + DN
coupling = 4.0

f32 = jnp.float32
bf16 = jnp.bfloat16

T = 128
NT = 104
KT = 5
G = 13
STEPS = NT // G
W = 104
NU = 16
ND = 8
VMEM = 58 * 1024 * 1024


def params():
    return pltpu.CompilerParams(dimension_semantics=("arbitrary",), vmem_limit_bytes=VMEM)


def whole(shape):
    zeros = (0,) * len(shape)
    return pl.BlockSpec(shape, lambda i, *_: zeros, pipeline_mode=pl.Buffered(1))


def tile_spec():
    return pl.BlockSpec((G, KT, T, T), lambda i, *_: (i, 0, 0, 0))


def lane_of(shape):
    return lax.broadcasted_iota(jnp.int32, shape, len(shape) - 1)


def pieces_of(x):
    hi = x.astype(bf16).astype(f32)
    mid = (x - hi).astype(bf16).astype(f32)
    return hi, mid, x - hi - mid


def total_of(x):
    return jnp.sum(jnp.sum(x, axis=0, keepdims=True), axis=1, keepdims=True)


def fold8(x):
    return jnp.sum(x.reshape(x.shape[0] // 8, 8, x.shape[1]), axis=0)


def hop_nat(i, g, idx_ref, tiles_ref, xs):
    row = i * G + g
    left = jnp.concatenate([tiles_ref[g, k] for k in range(KT)], axis=1)
    right = jnp.concatenate([xs[idx_ref[row * KT + k]] for k in range(KT)], axis=0)
    return jnp.dot(left, right, preferred_element_type=f32)


def hop_turned(i, g, idx_ref, tiles_ref, xs):
    row = i * G + g
    right = jnp.concatenate([tiles_ref[g, k] for k in range(KT)], axis=1)
    left = jnp.concatenate([xs[idx_ref[row * KT + k]] for k in range(KT)], axis=1)
    return lax.dot_general(left, right, (((1,), (1,)), ((), ())), preferred_element_type=f32)


def first_up_kernel(idx_ref, a_ref, tiles_ref, occ_rows_ref, occ_cols_ref, p_ref, sums_ref, xs, acc):
    i = pl.program_id(0)

    @pl.when(i == 0)
    def _():
        acc[...] = jnp.zeros_like(acc)

        def put(j, c):
            x = a_ref[j]
            xs[j] = x
            xs[NT + j] = -x
            return c

        lax.fori_loop(0, NT, put, 0)

    for g in range(G):
        row = i * G + g
        p = hop_nat(i, g, idx_ref, tiles_ref, xs).astype(bf16)
        p_ref[row] = p
        a = xs[row].astype(f32)
        diag = coupling * jnp.dot(occ_rows_ref[pl.ds(row * T, T), :], occ_cols_ref[...], preferred_element_type=f32)
        acc[0] += fold8((p.astype(f32) + diag * a) * a)
        acc[1] += fold8(a * a)

    @pl.when(i == STEPS - 1)
    def _():
        energy = total_of(acc[0])
        norm = total_of(acc[1])
        center = (energy / jnp.maximum(norm, 1e-30)).astype(bf16)
        sub = lax.broadcasted_iota(jnp.int32, (8, T), 0)
        sums_ref[...] = jnp.where(sub == 0, energy, jnp.where(sub == 1, norm, center.astype(f32)))
        fill = jnp.broadcast_to(center, (T, T))
        pad = lane_of((T, T)) >= W

        def put(j, c):
            p_ref[j] = jnp.where(pad, fill, p_ref[j])
            return c

        lax.fori_loop(0, NT, put, 0)


def second_up_kernel(idx_ref, a_ref, p_in_ref, tiles_ref, occ_rows_ref, occ_cols_ref, sums_ref, dots_ref, q_ref, xs, extra):
    i = pl.program_id(0)

    @pl.when(i == 0)
    def _():
        energy = sums_ref[0:1, :] + dots_ref[0:1, :]
        norm = sums_ref[1:2, :]
        lane = lane_of((1, T))
        row = jnp.zeros((1, T), f32)
        for k, piece in enumerate(pieces_of(energy) + pieces_of(norm)):
            row = jnp.where(lane == W + k, piece, row)
        extra[...] = jnp.broadcast_to(row, extra.shape)
        center = sums_ref[2:3, :]

        def put(j, c):
            a = a_ref[j].astype(f32)
            diag = coupling * jnp.dot(occ_rows_ref[pl.ds(pl.multiple_of(j * T, T), T), :], occ_cols_ref[...], preferred_element_type=f32)
            x = jnp.where(lane < W, p_in_ref[j].astype(f32) + (diag - center) * a, 0.0).astype(bf16)
            xs[j] = x
            xs[NT + j] = -x
            return c

        lax.fori_loop(0, NT, put, 0)

    pad = lane_of((T, T)) >= W
    for g in range(G):
        q = hop_nat(i, g, idx_ref, tiles_ref, xs)
        q_ref[g] = jnp.where(pad, extra[0:1, :], q).astype(bf16)


def first_down_kernel(idx_ref, a_ref, tiles_ref, r_ref, dots_ref, xs, acc):
    i = pl.program_id(0)

    @pl.when(i == 0)
    def _():
        acc[...] = jnp.zeros_like(acc)

        def put(d, c):
            for o in range(G):
                x = a_ref[d, :, o * T : (o + 1) * T]
                xs[d * G + o] = x
                xs[NT + d * G + o] = -x
            return c

        lax.fori_loop(0, ND, put, 0)

    for g in range(G):
        r = hop_turned(i, g, idx_ref, tiles_ref, xs).astype(bf16)
        r_ref[0, :, g * T : (g + 1) * T] = r
        acc[...] += fold8(r.astype(f32) * xs[i * G + g].astype(f32))

    @pl.when(i == STEPS - 1)
    def _():
        dots_ref[...] = jnp.broadcast_to(total_of(acc[...]), dots_ref.shape)


def pieces_in(o):
    found = []
    for u in range(NU):
        lo, hi = max(u * W, o * T), min((u + 1) * W, (o + 1) * T)
        if lo < hi:
            found.append((u, hi - o * T))
    return found


def assembled(rolled, o, lane):
    found = pieces_in(o)
    value = rolled[found[-1][0]]
    for u, end in reversed(found[:-1]):
        value = jnp.where(lane < end, rolled[u], value)
    return value


def second_down_kernel(idx_ref, a_ref, r_ref, p_ref, tiles_ref, occ_rows_ref, occ_cols_ref, w_ref, t_ref, xs, acc):
    i = pl.program_id(0)

    @pl.when(i == 0)
    def _():
        acc[...] = jnp.zeros_like(acc)
        lane = lane_of((1, T))

        def first(d, c):
            rolled, centers = {}, {}
            done = 0
            for o in range(G):
                for u, _end in pieces_in(o):
                    if u in rolled:
                        continue
                    x = p_ref[u * ND + d].astype(f32)
                    centers[u] = jnp.sum(jnp.where(lane == W, x[0:1, :], 0.0), axis=1, keepdims=True)
                    shift = (u * W) % T
                    rolled[u] = pltpu.roll(x, shift, 1) if shift else x
                p = assembled(rolled, o, lane)
                center = assembled(centers, o, lane)
                lanes = slice(o * T, (o + 1) * T)
                a = a_ref[d, :, lanes].astype(f32)
                r = r_ref[d, :, lanes].astype(f32)
                diag = coupling * jnp.dot(occ_rows_ref[...], occ_cols_ref[d, :, lanes], preferred_element_type=f32)
                w = p + r + diag * a
                w_ref[d, :, lanes] = w
                t_ref[d, :, lanes] = center * p + diag * w
                xs[d * G + o] = p.astype(bf16)
                acc[0] += fold8(w * a)
                acc[1] += fold8(a * a)
            return c

        lax.fori_loop(0, ND, first, 0)
        center = total_of(acc[0]) / jnp.maximum(total_of(acc[1]), 1e-30)

        def second(d, c):
            for o in range(G):
                lanes = slice(o * T, (o + 1) * T)
                a = a_ref[d, :, lanes].astype(f32)
                r = r_ref[d, :, lanes].astype(f32)
                x = (w_ref[d, :, lanes] + xs[d * G + o].astype(f32) - center * a).astype(bf16)
                xs[d * G + o] = x
                xs[NT + d * G + o] = -x
                t_ref[d, :, lanes] += center * r
            return c

        lax.fori_loop(0, ND, second, 0)

    for g in range(G):
        t_ref[i, :, g * T : (g + 1) * T] += hop_turned(i, g, idx_ref, tiles_ref, xs)


def joined_kernel(a_ref, w_ref, t_ref, q_ref, g_ref, sums_ref, acc, scal):
    i = pl.program_id(0)
    lane = lane_of((1, T))

    @pl.when(i == 0)
    def _():
        acc[...] = jnp.zeros_like(acc)

        def add(s, c):
            return c + q_ref[s, 0:8, :].astype(f32)

        row = lax.fori_loop(0, NU * ND, add, jnp.zeros((8, T), f32))[0:1, :]
        energy = jnp.sum(jnp.where((lane >= W) & (lane < W + 3), row, 0.0), axis=1, keepdims=True)
        norm = jnp.sum(jnp.where((lane >= W + 3) & (lane < W + 6), row, 0.0), axis=1, keepdims=True)
        alpha = energy / jnp.maximum(norm, 1.0)
        scal[...] = jnp.where(lane_of(scal.shape) == 0, alpha, norm)

    alpha = scal[0:1, 0:1]
    rolled = {}
    for o in range(G):
        for u, _end in pieces_in(o):
            if u in rolled:
                continue
            x = q_ref[u * ND + i].astype(f32)
            shift = (u * W) % T
            rolled[u] = pltpu.roll(x, shift, 1) if shift else x
        lanes = slice(o * T, (o + 1) * T)
        q = assembled(rolled, o, lane)
        a = a_ref[0, :, lanes].astype(f32)
        w = w_ref[0, :, lanes]
        g = q + t_ref[0, :, lanes]
        g_ref[0, :, lanes] = g
        u = w - alpha * a
        h = g - alpha * (w + u)
        acc[0] += fold8(u * u)
        acc[1] += fold8(u * a)
        acc[2] += fold8(h * h)
        acc[3] += fold8(h * u)
        acc[4] += fold8(h * a)

    @pl.when(i == ND - 1)
    def _():
        row = jnp.where(lane == 5, scal[0:1, 0:1], jnp.where(lane == 6, scal[0:1, 1:2], 0.0))
        for k in range(5):
            row = jnp.where(lane == k, total_of(acc[k]), row)
        sums_ref[...] = jnp.broadcast_to(row, sums_ref.shape)


def final_kernel(coef_ref, a_ref, w_ref, g_ref, v_ref):
    ca, cw, cg = coef_ref[0], coef_ref[1], coef_ref[2]
    v_ref[...] = (cg * g_ref[...] + cw * w_ref[...] + ca * a_ref[...].astype(f32)).astype(bf16)


def body(start_vector, hop_tiles, tile_columns, tile_signs, occupation):
    rows, cols = start_vector.shape
    index = (tile_columns + NT * tile_signs).astype(jnp.int32).reshape(-1)
    up = lax.axis_index(UP)
    down = lax.axis_index(DN)
    occ = occupation.astype(bf16)
    occ_rows = occ.T
    a_cols = lax.dynamic_slice_in_dim(occ, down * cols + up * W, W, 1)
    a_cols = jnp.pad(a_cols, ((0, 0), (0, T - W)))
    b_rows = lax.dynamic_slice_in_dim(occ_rows, up * rows + down * W, W, 0)
    b_cols = jnp.moveaxis(occ.reshape(occ.shape[0], ND, cols), 1, 0)

    parts = [jnp.pad(start_vector[:, k * W : (k + 1) * W], ((0, 0), (0, T - W))) for k in range(NU)]
    a_up = lax.all_to_all(jnp.stack(parts), UP, 0, 0, tiled=True).reshape(NT, T, T)
    a_up, start_later = lax.optimization_barrier((a_up, start_vector))
    a_dn = lax.all_to_all(start_later.reshape(ND, W, cols), DN, 0, 0, tiled=True)

    hop_flops = 2 * NT * KT * T * T * T
    tile_bytes = NT * KT * T * T * 2
    cost = pl.CostEstimate(flops=hop_flops, bytes_accessed=tile_bytes + 8 * 2**20, transcendentals=0)
    nat = (NT, T, T)
    wide = (ND, W, cols)
    xs_nat = pltpu.VMEM((2 * NT, T, T), bf16)
    xs_turned = pltpu.VMEM((2 * NT, W, T), bf16)

    p, sums = pl.pallas_call(
        first_up_kernel,
        grid_spec=pltpu.PrefetchScalarGridSpec(
            num_scalar_prefetch=1,
            grid=(STEPS,),
            in_specs=[whole(nat), tile_spec(), whole(occ_rows.shape), whole(a_cols.shape)],
            out_specs=[whole(nat), whole((8, T))],
            scratch_shapes=[xs_nat, pltpu.VMEM((2, 8, T), f32)],
        ),
        out_shape=[jax.ShapeDtypeStruct(nat, bf16), jax.ShapeDtypeStruct((8, T), f32)],
        compiler_params=params(),
        cost_estimate=cost,
        name="first_up",
    )(index, a_up, hop_tiles, occ_rows, a_cols)

    p_dn = lax.all_to_all(p.reshape(NU * ND, W, T), ALL, 0, 0, tiled=True)

    r, dots = pl.pallas_call(
        first_down_kernel,
        grid_spec=pltpu.PrefetchScalarGridSpec(
            num_scalar_prefetch=1,
            grid=(STEPS,),
            in_specs=[whole(wide), tile_spec()],
            out_specs=[pl.BlockSpec((1, W, cols), lambda i, *_: (i, 0, 0)), whole((8, T))],
            scratch_shapes=[xs_turned, pltpu.VMEM((8, T), f32)],
        ),
        out_shape=[jax.ShapeDtypeStruct(wide, bf16), jax.ShapeDtypeStruct((8, T), f32)],
        compiler_params=params(),
        cost_estimate=cost,
        name="first_down",
    )(index, a_dn, hop_tiles)

    q = pl.pallas_call(
        second_up_kernel,
        grid_spec=pltpu.PrefetchScalarGridSpec(
            num_scalar_prefetch=1,
            grid=(STEPS,),
            in_specs=[
                whole(nat),
                whole(nat),
                tile_spec(),
                whole(occ_rows.shape),
                whole(a_cols.shape),
                whole((8, T)),
                whole((8, T)),
            ],
            out_specs=pl.BlockSpec((G, T, T), lambda i, *_: (i, 0, 0)),
            scratch_shapes=[xs_nat, pltpu.VMEM((8, T), f32)],
        ),
        out_shape=jax.ShapeDtypeStruct(nat, bf16),
        compiler_params=params(),
        cost_estimate=cost,
        name="second_up",
    )(index, a_up, p, hop_tiles, occ_rows, a_cols, sums, dots)

    p_dn, q = lax.optimization_barrier((p_dn, q))
    q_dn = lax.all_to_all(q.reshape(NU * ND, W, T), ALL, 0, 0, tiled=True)

    w, t = pl.pallas_call(
        second_down_kernel,
        grid_spec=pltpu.PrefetchScalarGridSpec(
            num_scalar_prefetch=1,
            grid=(STEPS,),
            in_specs=[
                whole(wide),
                whole(wide),
                whole((NU * ND, W, T)),
                tile_spec(),
                whole(b_rows.shape),
                whole(b_cols.shape),
            ],
            out_specs=[whole(wide), whole(wide)],
            scratch_shapes=[xs_turned, pltpu.VMEM((2, 8, T), f32)],
        ),
        out_shape=[jax.ShapeDtypeStruct(wide, f32), jax.ShapeDtypeStruct(wide, f32)],
        compiler_params=params(),
        cost_estimate=cost,
        name="second_down",
    )(index, a_dn, r, p_dn, hop_tiles, b_rows, b_cols)

    block = pl.BlockSpec((1, W, cols), lambda i, *_: (i, 0, 0))
    g, partial = pl.pallas_call(
        joined_kernel,
        grid=(ND,),
        in_specs=[block, block, block, whole((NU * ND, W, T))],
        out_specs=[block, whole((NU * ND, T))],
        out_shape=[jax.ShapeDtypeStruct(wide, f32), jax.ShapeDtypeStruct((NU * ND, T), f32)],
        scratch_shapes=[pltpu.VMEM((5, 8, T), f32), pltpu.VMEM((8, T), f32)],
        compiler_params=params(),
        name="joined",
    )(a_dn, w, t, q_dn)

    shared = lax.all_to_all(partial, ALL, 0, 0, tiled=True)
    uu, ua, hh, hu, ha, _alpha, _norm = [jnp.sum(shared[:, k]) for k in range(7)]
    alpha1 = partial[0, 5]
    norm = partial[0, 6]
    scale2 = 1.0 / jnp.maximum(norm, 1.0)
    square1 = jnp.maximum(scale2 * uu, 1.0)
    beta1 = jnp.sqrt(square1)
    ratio2 = scale2 / square1
    alpha2 = ratio2 * (hu + alpha1 * uu - square1 * ua)
    shift = alpha2 - alpha1
    nn = hh + square1 * square1 * norm + shift * shift * uu - 2.0 * square1 * ha - 2.0 * shift * hu + 2.0 * square1 * shift * ua
    square2 = jnp.maximum(ratio2 * nn, 1.0)
    beta2 = jnp.sqrt(square2)
    cg = jnp.sqrt(ratio2) / beta2
    cw = -cg * (alpha1 + alpha2)
    ca = cg * (alpha1 * alpha2 - square1)
    coef = jnp.stack([ca, cw, cg])

    v = pl.pallas_call(
        final_kernel,
        grid_spec=pltpu.PrefetchScalarGridSpec(
            num_scalar_prefetch=1,
            grid=(ND,),
            in_specs=[block, block, block],
            out_specs=block,
        ),
        out_shape=jax.ShapeDtypeStruct(wide, bf16),
        compiler_params=params(),
        name="final",
    )(coef, a_dn, w, g)
    final = lax.all_to_all(v, DN, 0, 0, tiled=True).reshape(rows, cols)
    return final, jnp.stack([alpha1, alpha2]), jnp.stack([beta1, beta2])


def solution(mesh):
    torus = Mesh(mesh.devices.reshape(2, 4, 2, 2, 4), ALL)
    return jax.shard_map(
        body,
        mesh=torus,
        in_specs=(P(UP, DN), P(), P(), P(), P()),
        out_specs=(P(UP, DN), P(), P()),
        check_vma=False,
    )
```

time: 692 us -> 307 us (0.44)
  local copies, waits for them, and re-layouts: 193 us -> 32.1 us
  blocking collectives: 141 us -> 0 us
  Pallas kernels: 0 us -> 110 us
  waiting for transfers between devices: 172 us -> 93.6 us
  matrix products: 63.4 us -> 0 us
  other arithmetic: 52.2 us -> 13.2 us
  starting transfers between devices: 55.9 us -> 44.6 us
    psum x15 -> x0, blocking collectives: 128 us -> none  [one_axis_at_a_time(): return functools.reduce(lax.psum, axes, value)]
    pallas_call x0 -> x6, Pallas kernels: none -> 110 us  [the longest x1 29.7 us: body(): pl.pallas_call(second_up_kernel, grid_spec=pltpu.PrefetchScalarGridSpec(n...]
    gather x4 -> x0, local copies, waits for them, and re-layouts: 79.9 us -> none  [hop_lead(): picked = cube[tile_columns]]
    all_to_all x10 -> x6, waiting for transfers between devices: 172 us -> 93.6 us  [the longest x1 32.4 us: body(): lax.all_to_all(jnp.stack(parts), UP, 0, 0, tiled=True).reshape(NT, T, T)]
    dot_general x5 -> x0, matrix products: 63.4 us -> none  [the longest x4 52.3 us: hop_lead(): jnp.einsum('ikab,ikbm->iam', signed, picked, preferred_element_type=jnp.f...]
    convert_element_type x15 -> x0, local copies, waits for them, and re-layouts: 54.8 us -> none  [the longest x10 31.5 us: hop_lead(): return result.reshape(layout).astype(jnp.bfloat16)]
    convert_element_type x8 -> x1, other arithmetic: 34.9 us -> 4.45 us  [body(): occ = occupation.astype(bf16)]
    another operation x8 -> x1, local copies, waits for them, and re-layouts: 27.8 us -> 0.74 us  [body(): jnp.stack(parts)]
  transfers between devices with their start and end apart: 10 -> 6, of which waited for: 8 -> 5; matrix products, arithmetic and copies ran while one was open for 20% -> 7% of each run, Pallas kernels for 0% -> 29%
where the time goes in v1:
time: 307 us; the launch traced here: 304 us
  Pallas kernels  110 us (36%)
  waiting for transfers between devices  93.6 us (30%)
  starting transfers between devices  44.6 us (15%)
  local copies, waits for them, and re-layouts  32.1 us (10%)
  other arithmetic  13.2 us (4%)
  between operations  10.6 us (3%)
    all_to_all x1, waiting for transfers between devices, body(): lax.all_to_all(jnp.stack(parts), UP, 0, 0, tiled=True).reshape(NT, T, T)  32.4 us
    all_to_all x1, waiting for transfers between devices, body(): final = lax.all_to_all(v, DN, 0, 0, tiled=True).reshape(rows, cols)  31.3 us
    pallas_call x1, Pallas kernels, body(): pl.pallas_call(second_up_kernel, grid_spec=pltpu.PrefetchScalarGridSpec(n...  29.7 us
    pallas_call x1, Pallas kernels, body(): pl.pallas_call(second_down_kernel, grid_spec=pltpu.PrefetchScalarGridSpec...  25.3 us
    unnamed x29, local copies, waits for them, and re-layouts  20.1 us
    pallas_call x1, Pallas kernels, body(): pl.pallas_call(first_up_kernel, grid_spec=pltpu.PrefetchScalarGridSpec(nu...  18 us
    pallas_call x1, Pallas kernels, body(): pl.pallas_call(first_down_kernel, grid_spec=pltpu.PrefetchScalarGridSpec(...  15.1 us
    all_to_all x1, waiting for transfers between devices, body(): q_dn = lax.all_to_all(q.reshape(NU * ND, W, T), ALL, 0, 0, tiled=True)  14.1 us
  transfers between devices with their start and end apart: 6, of which 5 were waited for; matrix products, arithmetic and copies ran while one was open for 7% of the time, Pallas kernels for 29%

profile of v1, /device:TPU:24, one launch (start us, length us, event | category | flops | bytes accessed | tf_op | source)
XLA Modules:
  0.0 304.3 jit_solution(6264151408435693646)
XLA Ops:
  0.6 3.9 %fusion = (bf16[832,104]{1,0:T(8,128)(2,1)S(1)}, bf16[832,104]{1,0:T(8,128)(2,1)S(1)}, bf16[832,104]{1,0:T(8,128)(2,1)S(1)}, bf16[832,104]{1,0:T(8,128)(2,1)S(1)...) fusion(bf16[832,1664]{1,0:T(8,128)(2,1)} %param.5), kind=kLoop, calls=%fused_computation.27 | loop fusion | bytes 5191680 | tf_op jit(solution)/shard_map/slice | solution.py:305
  4.5 1.7 bitcast_dynamic-update-slice_fusion.15
  12.0 0.7 bitcast_dynamic-update-slice_fusion.6
  17.1 5.9 %all-to-all-start = ((bf16[16,832,128]{2,1,0:T(8,128)(2,1)}), bf16[16,832,128]{2,1,0:T(8,128)(2,1)S(1)}, u32[]{:S(2)}, u32[]{:S(2)}) async-start(bf16[16,832,128]{2,1,0:T(8,128)(2,1)} %bitcast_dynamic-update-slice_fusion), calls=%async_computation | async-start | bytes 6815744 | tf_op jit(solution)/shard_map/all_to_all | solution.py:306
  23.1 0.8 reshape.31.idx_ref
  23.9 5.1 %copy.18 = s32[16,13312]{0,1:T(8,128)} copy(s32[16,13312]{1,0:T(8,128)} %param.9) | data formatting | bytes 1703936 | tf_op args[4]
  29.0 4.4 %convert_element_type.22 = bf16[16,13312]{0,1:T(8,128)(2,1)} convert(s32[16,13312]{0,1:T(8,128)} %copy.18) | non-fusion elementwise | flops 212992 | bytes 1277952 | tf_op jit(solution)/shard_map/convert_element_type | solution.py:298
  33.4 1.4 dynamic-slice_bitcast_fusion
  35.5 32.4 %all-to-all-done = bf16[16,832,128]{2,1,0:T(8,128)(2,1)S(1)} async-done(((bf16[16,832,128]{2,1,0:T(8,128)(2,1)}), bf16[16,832,128]{2,1,0:T(8,128)(2,1)S(1)}, u32[]{:S(2)}, u32[]{:S(2)}) %all-to-all-start) | async-done | bytes 3407904 | tf_op jit(solution)/shard_map/all_to_all | solution.py:306
  67.9 1.7 copy-done.1
  69.6 8.3 %all-to-all-start.1 = ((bf16[8,104,1664]{2,1,0:T(8,128)(2,1)}), bf16[8,104,1664]{2,1,0:T(8,128)(2,1)S(1)}, u32[]{:S(2)}, u32[]{:S(2)}) async-start(bf16[8,104,1664]{2,1,0:T(8,128)(2,1)} %bitcast.59), calls=%async_computation.1 | async-start | bytes 5537792 | tf_op jit(solution)/shard_map/all_to_all | solution.py:308
  77.9 4.3 %convert_bitcast_fusion.occ_rows_ref = bf16[13312,16]{1,0:T(8,128)(2,1)} fusion(s32[16,13312]{0,1:T(8,128)} %copy.18), kind=kLoop, calls=%fused_computation.29 | loop fusion | flops 212992 | bytes 1277952 | tf_op jit(solution)/shard_map/transpose | solution.py:299
  82.2 18.0 %first_up.1 = (bf16[104,128,128]{2,1,0:T(8,128)(2,1)}, f32[8,128]{1,0:T(8,128)}) custom-call(s32[520]{0:T(1024)} %reshape.31.idx_ref, bf16[104,128,128]{2,1,0:T(8,128)(2,1)} %bitcast.56, bf16[104,5,128,128]{3,2,1,0:T(8,128)(2,1)} %tiles_ref.7, bf16[13312,16]{1,0:T(8,128)(2,1)} %convert_bitcast_fusion.occ_rows_ref, bf16[16,128]{1,0:T(8,128)(2,1)} %pad.69.clone.occ_cols_ref), custom_call_target="tpu_custom_call" | custom-call | flops 2181038080 | bytes 25427968 | tf_op jit(solution)/shard_map/first_up/pallas_call | solution.py:318
  100.2 10.1 %all-to-all-done.1.a_ref = bf16[8,104,1664]{2,1,0:T(8,128)(2,1)S(1)} async-done(((bf16[8,104,1664]{2,1,0:T(8,128)(2,1)}), bf16[8,104,1664]{2,1,0:T(8,128)(2,1)S(1)}, u32[]{:S(2)}, u32[]{:S(2)}) %all-to-all-start.1) | async-done | bytes 2768928 | tf_op jit(solution)/shard_map/all_to_all | solution.py:308
  110.3 1.5 copy-done
  111.8 8.1 %all-to-all-start.2 = ((bf16[128,104,128]{2,1,0:T(8,128)(2,1)}), bf16[128,104,128]{2,1,0:T(8,128)(2,1)}, u32[]{:S(2)}, u32[]{:S(2)}) async-start(bf16[128,104,128]{2,1,0:T(8,128)(2,1)} %bitcast.61), calls=%async_computation.2 | async-start | bytes 6815744 | tf_op jit(solution)/shard_map/all_to_all | solution.py:333
  119.9 15.1 %first_down.1 = (bf16[8,104,1664]{2,1,0:T(8,128)(2,1)}, f32[8,128]{1,0:T(8,128)}) custom-call(s32[520]{0:T(1024)} %reshape.31.idx_ref, bf16[8,104,1664]{2,1,0:T(8,128)(2,1)} %copy-done, bf16[104,5,128,128]{3,2,1,0:T(8,128)(2,1)} %tiles_ref.7), custom_call_target="tpu_custom_call" | custom-call | flops 2181038080 | bytes 25427968 | tf_op jit(solution)/shard_map/first_down/pallas_call | solution.py:335
  135.0 29.7 %second_up.1 = bf16[104,128,128]{2,1,0:T(8,128)(2,1)} custom-call(s32[520]{0:T(1024)} %reshape.31.idx_ref, bf16[104,128,128]{2,1,0:T(8,128)(2,1)} %bitcast.57, bf16[104,128,128]{2,1,0:T(8,128)(2,1)} %get-tuple-element.18.p_in_ref, bf16[104,5,128,128]{3,2,1,0:T(8,128)(2,1)} %tiles_ref.7, bf16[13312,16]{1,0:T(8,128)(2,1)} %convert_bitcast_fusion.occ_rows_ref, ...), custom_call_target="tpu_custom_call" | custom-call | flops 2181038080 | bytes 25427968 | tf_op jit(solution)/shard_map/second_up/pallas_call | solution.py:350
  164.7 10.2 %all-to-all-start.3 = ((bf16[128,104,128]{2,1,0:T(8,128)(2,1)}), bf16[128,104,128]{2,1,0:T(8,128)(2,1)}, u32[]{:S(2)}, u32[]{:S(2)}) async-start(bf16[128,104,128]{2,1,0:T(8,128)(2,1)} %bitcast.60), calls=%async_computation.3 | async-start | bytes 6815744 | tf_op jit(solution)/shard_map/all_to_all | solution.py:374
  174.8 3.2 %copy.22 = bf16[16,8,1664]{2,0,1:T(8,128)(2,1)} copy(bf16[16,8,1664]{0,2,1:T(8,128)(2,1)S(1)} %bitcast.58) | data formatting | bytes 851968 | tf_op jit(solution)/shard_map/reshape | solution.py:303
  178.0 25.3 %second_down.1 = (f32[8,104,1664]{2,1,0:T(8,128)}, f32[8,104,1664]{2,1,0:T(8,128)}) custom-call(s32[520]{0:T(1024)} %reshape.31.idx_ref, bf16[8,104,1664]{2,1,0:T(8,128)(2,1)} %copy-done, bf16[8,104,1664]{2,1,0:T(8,128)(2,1)} %get-tuple-element.16.r_ref, bf16[128,104,128]{2,1,0:T(8,128)(2,1)} %all-to-all-done.2.p_ref, bf16[104,5,128,128]{3,2,1,0:T(8,128)(2,1)} %tiles_ref.7, ...), custom_call_target="tpu_custom_call" | custom-call | flops 2181038080 | bytes 25427968 | tf_op jit(solution)/shard_map/second_down/pallas_call | solution.py:376
  203.3 14.1 %all-to-all-done.3.q_ref = bf16[128,104,128]{2,1,0:T(8,128)(2,1)} async-done(((bf16[128,104,128]{2,1,0:T(8,128)(2,1)}), bf16[128,104,128]{2,1,0:T(8,128)(2,1)}, u32[]{:S(2)}, u32[]{:S(2)}) %all-to-all-start.3) | async-done | bytes 3407904 | tf_op jit(solution)/shard_map/all_to_all | solution.py:374
  217.4 12.9 %joined.1 = (f32[8,104,1664]{2,1,0:T(8,128)}, f32[128,128]{1,0:T(8,128)}) custom-call(bf16[8,104,1664]{2,1,0:T(8,128)(2,1)} %copy-done, f32[8,104,1664]{2,1,0:T(8,128)} %get-tuple-element.22.w_ref, f32[8,104,1664]{2,1,0:T(8,128)} %get-tuple-element.23.t_ref, bf16[128,104,128]{2,1,0:T(8,128)(2,1)} %all-to-all-done.3.q_ref), custom_call_target="tpu_custom_call" | custom-call | tf_op jit(solution)/shard_map/joined/pallas_call | solution.py:399
  230.3 6.0 %all-to-all-start.4 = ((f32[128,1,128]{2,1,0:T(1,128)}), f32[128,1,128]{2,1,0:T(1,128)S(1)}, u32[]{:S(2)}, u32[]{:S(2)}) async-start(f32[128,1,128]{2,1,0:T(1,128)} %bitcast.65), calls=%async_computation.4 | async-start | bytes 131072 | tf_op jit(solution)/shard_map/all_to_all | solution.py:410
  236.4 1.4 fusion.1
  238.5 5.8 %all-to-all-done.4 = f32[128,1,128]{2,1,0:T(1,128)S(1)} async-done(((f32[128,1,128]{2,1,0:T(1,128)}), f32[128,1,128]{2,1,0:T(1,128)S(1)}, u32[]{:S(2)}, u32[]{:S(2)}) %all-to-all-start.4) | async-done | bytes 65568 | tf_op jit(solution)/shard_map/all_to_all | solution.py:410
  244.2 0.8 slice_reduce_fusion
  254.8 9.2 %final.1 = bf16[8,104,1664]{2,1,0:T(8,128)(2,1)} custom-call(f32[3]{0:T(128)} %pad_maximum_fusion.coef_ref, bf16[8,104,1664]{2,1,0:T(8,128)(2,1)} %copy-done, f32[8,104,1664]{2,1,0:T(8,128)} %get-tuple-element.22.w_ref, f32[8,104,1664]{2,1,0:T(8,128)} %get-tuple-element.26.g_ref), custom_call_target="tpu_custom_call" | custom-call | tf_op jit(solution)/shard_map/final/pallas_call | solution.py:428
  264.1 6.1 %all-to-all-start.5 = ((bf16[8,104,1664]{2,1,0:T(8,128)(2,1)}), bf16[8,104,1664]{2,1,0:T(8,128)(2,1)S(1)}, u32[]{:S(2)}, u32[]{:S(2)}) async-start(bf16[8,104,1664]{2,1,0:T(8,128)(2,1)} %final.1), calls=%async_computation.5 | async-start | bytes 5537792 | tf_op jit(solution)/shard_map/all_to_all | solution.py:440
  270.2 1.3 pad_maximum_fusion.1
  271.5 31.3 %all-to-all-done.5 = bf16[8,104,1664]{2,1,0:T(8,128)(2,1)S(1)} async-done(((bf16[8,104,1664]{2,1,0:T(8,128)(2,1)}), bf16[8,104,1664]{2,1,0:T(8,128)(2,1)S(1)}, u32[]{:S(2)}, u32[]{:S(2)}) %all-to-all-start.5) | async-done | bytes 2768928 | tf_op jit(solution)/shard_map/all_to_all | solution.py:440
  302.8 1.5 copy.43
  (30 shorter events, 11.6 us)
Async XLA Ops:
  0.6 3.9 %copy-start.5 = (pred[128]{0:T(512)(128)(4,1)S(1)}, pred[128]{0:T(512)(128)(4,1)}, u32[]{:S(2)}) copy-start(pred[128]{0:T(512)(128)(4,1)} %constant.12.clone.1) | copy-start | bytes 388
  17.1 5.9 %copy-start.3 = (s32[104,5]{0,1:T(8,128)S(1)}, s32[104,5]{0,1:T(8,128)}, u32[]{:S(2)}) copy-start(s32[104,5]{0,1:T(8,128)} %param.7) | copy-start | bytes 6244
  17.1 5.9 %copy-start.4 = (s32[104,5]{0,1:T(8,128)S(1)}, s32[104,5]{0,1:T(8,128)}, u32[]{:S(2)}) copy-start(s32[104,5]{0,1:T(8,128)} %param.8) | copy-start | bytes 6244
  17.1 50.8 %all-to-all-start = ((bf16[16,832,128]{2,1,0:T(8,128)(2,1)}), bf16[16,832,128]{2,1,0:T(8,128)(2,1)S(1)}, u32[]{:S(2)}, u32[]{:S(2)}) async-start(bf16[16,832,128]{2,1,0:T(8,128)(2,1)} %bitcast_dynamic-update-slice_fusion), calls=%async_computation | async-start | bytes 6815744 | tf_op jit(solution)/shard_map/all_to_all | solution.py:306
  67.9 1.7 copy-start.1
  69.6 40.7 %all-to-all-start.1 = ((bf16[8,104,1664]{2,1,0:T(8,128)(2,1)}), bf16[8,104,1664]{2,1,0:T(8,128)(2,1)S(1)}, u32[]{:S(2)}, u32[]{:S(2)}) async-start(bf16[8,104,1664]{2,1,0:T(8,128)(2,1)} %bitcast.59), calls=%async_computation.1 | async-start | bytes 5537792 | tf_op jit(solution)/shard_map/all_to_all | solution.py:308
  110.3 1.5 copy-start
  111.8 52.9 %all-to-all-start.2 = ((bf16[128,104,128]{2,1,0:T(8,128)(2,1)}), bf16[128,104,128]{2,1,0:T(8,128)(2,1)}, u32[]{:S(2)}, u32[]{:S(2)}) async-start(bf16[128,104,128]{2,1,0:T(8,128)(2,1)} %bitcast.61), calls=%async_computation.2 | async-start | bytes 6815744 | tf_op jit(solution)/shard_map/all_to_all | solution.py:333
  164.7 10.2 %copy-start.2 = (bf16[16,13312]{0,1:T(8,128)(2,1)S(1)}, bf16[16,13312]{0,1:T(8,128)(2,1)}, u32[]{:S(2)}) copy-start(bf16[16,13312]{0,1:T(8,128)(2,1)} %convert_element_type.22) | copy-start | bytes 1277956
  164.7 52.8 %all-to-all-start.3 = ((bf16[128,104,128]{2,1,0:T(8,128)(2,1)}), bf16[128,104,128]{2,1,0:T(8,128)(2,1)}, u32[]{:S(2)}, u32[]{:S(2)}) async-start(bf16[128,104,128]{2,1,0:T(8,128)(2,1)} %bitcast.60), calls=%async_computation.3 | async-start | bytes 6815744 | tf_op jit(solution)/shard_map/all_to_all | solution.py:374
  230.3 13.9 %all-to-all-start.4 = ((f32[128,1,128]{2,1,0:T(1,128)}), f32[128,1,128]{2,1,0:T(1,128)S(1)}, u32[]{:S(2)}, u32[]{:S(2)}) async-start(f32[128,1,128]{2,1,0:T(1,128)} %bitcast.65), calls=%async_computation.4 | async-start | bytes 131072 | tf_op jit(solution)/shard_map/all_to_all | solution.py:410
  264.1 38.7 %all-to-all-start.5 = ((bf16[8,104,1664]{2,1,0:T(8,128)(2,1)}), bf16[8,104,1664]{2,1,0:T(8,128)(2,1)S(1)}, u32[]{:S(2)}, u32[]{:S(2)}) async-start(bf16[8,104,1664]{2,1,0:T(8,128)(2,1)} %final.1), calls=%async_computation.5 | async-start | bytes 5537792 | tf_op jit(solution)/shard_map/all_to_all | solution.py:440

commit v2 on v1

v2 whole, which is shorter than its diff:
```python
import jax
import jax.numpy as jnp
from jax import lax
from jax.experimental import pallas as pl
from jax.experimental.pallas import tpu as pltpu
from jax.sharding import Mesh
from jax.sharding import PartitionSpec as P


UP = ("up_0", "up_1", "up_2")
DN = ("dn_0", "dn_1")
ALL = UP + DN
coupling = 4.0

f32 = jnp.float32
bf16 = jnp.bfloat16

T = 128
NT = 104
KT = 5
G = 13
STEPS = NT // G
W = 104
NU = 16
ND = 8
MIB = 1024 * 1024


def params(mib):
    return pltpu.CompilerParams(dimension_semantics=("arbitrary",), vmem_limit_bytes=mib * MIB)


def whole(shape):
    zeros = (0,) * len(shape)
    return pl.BlockSpec(shape, lambda i, *_: zeros, pipeline_mode=pl.Buffered(1))


def tile_spec():
    return pl.BlockSpec((G, KT, T, T), lambda i, *_: (i, 0, 0, 0))


def lane_of(shape):
    return lax.broadcasted_iota(jnp.int32, shape, len(shape) - 1)


def pieces_of(x):
    hi = x.astype(bf16).astype(f32)
    mid = (x - hi).astype(bf16).astype(f32)
    return hi, mid, x - hi - mid


def total_of(x):
    return jnp.sum(jnp.sum(x, axis=0, keepdims=True), axis=1, keepdims=True)


def fold8(x):
    return jnp.sum(x.reshape(x.shape[0] // 8, 8, x.shape[1]), axis=0)


def hop_nat(i, g, idx_ref, tiles_ref, xs):
    row = i * G + g
    left = jnp.concatenate([tiles_ref[g, k] for k in range(KT)], axis=1)
    right = [xs[pl.ds(pl.multiple_of(idx_ref[row * KT + k] * T, T), T), :] for k in range(KT)]
    return jnp.dot(left, jnp.concatenate(right, axis=0), preferred_element_type=f32)


def hop_turned(i, g, idx_ref, tiles_ref, xs):
    row = i * G + g
    right = jnp.concatenate([tiles_ref[g, k] for k in range(KT)], axis=1)
    left = jnp.concatenate([xs[idx_ref[row * KT + k]] for k in range(KT)], axis=1)
    return lax.dot_general(left, right, (((1,), (1,)), ((), ())), preferred_element_type=f32)


LOW = T - W
STRIPS = -(-W // LOW)


def turned(x, shift):
    shift %= T
    return pltpu.roll(x, shift, 1) if shift else x


def with_strip(head, tail, k, lane):
    return jnp.where(lane < W, head, turned(tail, W - LOW * k))


def from_strips(strips, lane):
    value = turned(strips[-1], LOW * (STRIPS - 1) - W)
    for k in reversed(range(STRIPS - 1)):
        value = jnp.where(lane < LOW * (k + 1), turned(strips[k], LOW * k - W), value)
    return value


ROWS = 832
HEAD = 704
H = 64
WH = 88
S = W - WH


def pack_kernel(a_ref, out_ref):
    lane = lane_of((1, T))

    def cut(u, block):
        q, o = divmod(u * W, T)
        rows = slice(block * H, (block + 1) * H)
        x = turned(a_ref[rows, q * T : (q + 1) * T].astype(f32), -o)
        if o + W > T:
            y = turned(a_ref[rows, (q + 1) * T : (q + 2) * T].astype(f32), -o)
            x = jnp.where(lane < T - o, x, y)
        return x

    for u in range(NU):
        tails = [cut(u, HEAD // H + h) for h in range(2)]
        for block in range(HEAD // H):
            x = cut(u, block)
            if block < 2 * STRIPS:
                x = with_strip(x, tails[block % 2], block // 2, lane)
            out_ref[u, block * H : (block + 1) * H, :] = x.astype(bf16)


def packed(values, t, lane):
    x = values[pl.ds(pl.multiple_of(t * W, 8), WH), :]
    tail = values[pl.ds(pl.multiple_of(t * W + WH, 8), S), :]
    found = [with_strip(x[S * k : S * (k + 1)], tail, k, lane) for k in range(STRIPS)]
    return jnp.concatenate(found + [x[S * STRIPS :]], axis=0)


def unpacked(x, lane):
    tail = from_strips([x[S * k : S * (k + 1)] for k in range(STRIPS)], lane)
    return jnp.concatenate([x, tail], axis=0)


FREE = S * (STRIPS - 1)
FREE_LANE = W + W - LOW * (STRIPS - 1)


def first_up_kernel(idx_ref, a_ref, tiles_ref, occ_rows_ref, occ_cols_ref, p_ref, x_ref, sums_ref, xs, whole_w, some_p, acc):
    i = pl.program_id(0)
    lane = lane_of((1, T))

    @pl.when(i == 0)
    def _():
        acc[...] = jnp.zeros_like(acc)

        def put(s, c):
            def keep(row, x):
                x = jnp.where(lane < W, x, 0.0).astype(bf16)
                at = pl.multiple_of(s * ROWS + row, H)
                xs[pl.ds(at, H), :] = x
                xs[pl.ds(NT * T + at, H), :] = -x

            for block in range(HEAD // H):
                keep(block * H, a_ref[s, block * H : (block + 1) * H, :].astype(f32))
            for h in range(2):
                strips = [
                    a_ref[s, (2 * k + h) * H : (2 * k + h + 1) * H, :].astype(f32) for k in range(STRIPS)
                ]
                keep(HEAD + h * H, from_strips(strips, lane))
            return c

        lax.fori_loop(0, NU, put, 0)

    for g in range(G):
        rows = pl.ds(pl.multiple_of((i * G + g) * T, T), T)
        p = hop_nat(i, g, idx_ref, tiles_ref, xs).astype(bf16).astype(f32)
        some_p[g * T : (g + 1) * T, :] = p
        a = xs[rows, :].astype(f32)
        diag = coupling * jnp.dot(occ_rows_ref[rows, :], occ_cols_ref[...], preferred_element_type=f32)
        w = p + diag * a
        whole_w[rows, :] = w
        acc[0] += fold8(w * a)
        acc[1] += fold8(a * a)
    for t in range(NU):
        p_ref[i * NU + t] = packed(some_p, t, lane).astype(bf16)

    @pl.when(i == STEPS - 1)
    def _():
        energy = total_of(acc[0])
        norm = total_of(acc[1])
        center = (energy / jnp.maximum(norm, 1e-30)).astype(bf16)
        sub = lax.broadcasted_iota(jnp.int32, (8, T), 0)
        sums_ref[...] = jnp.where(sub == 0, energy, norm)
        fill = jnp.broadcast_to(center, (S, T))
        free = lane_of((S, T)) >= FREE_LANE

        def mark(s, c):
            p_ref[s, FREE : FREE + S, :] = jnp.where(free, fill, p_ref[s, FREE : FREE + S, :])
            return c

        lax.fori_loop(0, NU * ND, mark, 0)
        wide = center.astype(f32)

        def put(j, c):
            rows = pl.ds(pl.multiple_of(j * T, T), T)
            x_ref[rows, :] = (whole_w[rows, :] - wide * xs[rows, :].astype(f32)).astype(bf16)
            return c

        lax.fori_loop(0, NT, put, 0)


def second_up_kernel(idx_ref, x_ref, tiles_ref, sums_ref, dots_ref, q_ref, xs, some_q, extra):
    i = pl.program_id(0)
    lane = lane_of((1, T))

    @pl.when(i == 0)
    def _():
        energy = sums_ref[0:1, :] + dots_ref[0:1, :]
        norm = sums_ref[1:2, :]
        row = jnp.zeros((1, T), f32)
        for k, piece in enumerate(pieces_of(energy) + pieces_of(norm)):
            row = jnp.where(lane == FREE_LANE + k, piece, row)
        extra[...] = jnp.broadcast_to(row, extra.shape)

        def put(j, c):
            at = pl.multiple_of(j * T, T)
            x = x_ref[pl.ds(at, T), :]
            xs[pl.ds(at, T), :] = x
            xs[pl.ds(NT * T + at, T), :] = -x
            return c

        lax.fori_loop(0, NT, put, 0)

    for g in range(G):
        some_q[g * T : (g + 1) * T, :] = hop_nat(i, g, idx_ref, tiles_ref, xs)
    for t in range(NU):
        x = packed(some_q, t, lane)
        marked = jnp.where(lane >= FREE_LANE, extra[0:1, :], x[FREE : FREE + S])
        q_ref[t] = jnp.concatenate([x[:FREE], marked, x[FREE + S :]], axis=0).astype(bf16)


def first_down_kernel(idx_ref, a_ref, tiles_ref, r_ref, dots_ref, xs, acc):
    i = pl.program_id(0)

    @pl.when(i == 0)
    def _():
        acc[...] = jnp.zeros_like(acc)

        def put(d, c):
            for o in range(G):
                x = a_ref[d, :, o * T : (o + 1) * T]
                xs[d * G + o] = x
                xs[NT + d * G + o] = -x
            return c

        lax.fori_loop(0, ND, put, 0)

    for g in range(G):
        r = hop_turned(i, g, idx_ref, tiles_ref, xs).astype(bf16)
        r_ref[0, :, g * T : (g + 1) * T] = r
        acc[...] += fold8(r.astype(f32) * xs[i * G + g].astype(f32))

    @pl.when(i == STEPS - 1)
    def _():
        dots_ref[...] = jnp.broadcast_to(total_of(acc[...]), dots_ref.shape)


def pieces_in(o):
    found = []
    for u in range(NU):
        lo, hi = max(u * W, o * T), min((u + 1) * W, (o + 1) * T)
        if lo < hi:
            found.append((u, hi - o * T))
    return found


def assembled(rolled, o, lane):
    found = pieces_in(o)
    value = rolled[found[-1][0]]
    for u, end in reversed(found[:-1]):
        value = jnp.where(lane < end, rolled[u], value)
    return value


def second_down_kernel(idx_ref, a_ref, r_ref, p_ref, tiles_ref, occ_rows_ref, occ_cols_ref, u_ref, t_ref, center_ref, xs, w_ref, acc):
    i = pl.program_id(0)

    @pl.when(i == 0)
    def _():
        acc[...] = jnp.zeros_like(acc)
        lane = lane_of((1, T))

        def first(d, c):
            rolled, centers = {}, {}
            for o in range(G):
                for u, _end in pieces_in(o):
                    if u in rolled:
                        continue
                    x = p_ref[u * ND + d].astype(f32)
                    centers[u] = jnp.sum(jnp.where(lane == FREE_LANE, x[FREE : FREE + 1, :], 0.0), axis=1, keepdims=True)
                    rolled[u] = turned(unpacked(x, lane), u * W)
                p = assembled(rolled, o, lane)
                center = assembled(centers, o, lane)
                lanes = slice(o * T, (o + 1) * T)
                a = a_ref[d, :, lanes].astype(f32)
                r = r_ref[d, :, lanes].astype(f32)
                diag = coupling * jnp.dot(occ_rows_ref[...], occ_cols_ref[d, :, lanes], preferred_element_type=f32)
                w = p + r + diag * a
                w_ref[d, :, lanes] = w
                t_ref[d, :, lanes] = center * p + diag * w
                xs[d * G + o] = p.astype(bf16)
                acc[0] += fold8(w * a)
                acc[1] += fold8(a * a)
            return c

        lax.fori_loop(0, ND, first, 0)
        center = total_of(acc[0]) / jnp.maximum(total_of(acc[1]), 1e-30)
        center_ref[...] = jnp.broadcast_to(center, center_ref.shape)

        def second(d, c):
            for o in range(G):
                lanes = slice(o * T, (o + 1) * T)
                a = a_ref[d, :, lanes].astype(f32)
                r = r_ref[d, :, lanes].astype(f32)
                w = w_ref[d, :, lanes]
                u = w - center * a
                u_ref[d, :, lanes] = u.astype(bf16)
                x = (u + xs[d * G + o].astype(f32)).astype(bf16)
                xs[d * G + o] = x
                xs[NT + d * G + o] = -x
                t_ref[d, :, lanes] += center * (r - w - u)
            return c

        lax.fori_loop(0, ND, second, 0)

    for g in range(G):
        t_ref[i, :, g * T : (g + 1) * T] += hop_turned(i, g, idx_ref, tiles_ref, xs)


def joined_kernel(a_ref, u_ref, t_ref, q_ref, center_ref, g_ref, sums_ref, acc, scal):
    i = pl.program_id(0)
    lane = lane_of((1, T))

    @pl.when(i == 0)
    def _():
        acc[...] = jnp.zeros_like(acc)

        def add(s, c):
            for k in range(8):
                c = c + q_ref[s * 8 + k, FREE : FREE + S, :].astype(f32)
            return c

        row = lax.fori_loop(0, NU * ND // 8, add, jnp.zeros((S, T), f32))[0:1, :]
        first = (lane >= FREE_LANE) & (lane < FREE_LANE + 3)
        second = (lane >= FREE_LANE + 3) & (lane < FREE_LANE + 6)
        energy = jnp.sum(jnp.where(first, row, 0.0), axis=1, keepdims=True)
        norm = jnp.sum(jnp.where(second, row, 0.0), axis=1, keepdims=True)
        alpha = energy / jnp.maximum(norm, 1.0)
        scal[...] = jnp.where(lane_of(scal.shape) == 0, alpha, norm)

    off = center_ref[0:1, 0:1] - scal[0:1, 0:1]
    rolled = {}
    for o in range(G):
        for u, _end in pieces_in(o):
            if u not in rolled:
                rolled[u] = turned(unpacked(q_ref[u * ND + i].astype(f32), lane), u * W)
        lanes = slice(o * T, (o + 1) * T)
        q = assembled(rolled, o, lane)
        a = a_ref[0, :, lanes].astype(f32)
        near = u_ref[0, :, lanes].astype(f32)
        g = q + t_ref[0, :, lanes]
        g_ref[i, :, lanes] = g
        u = near + off * a
        h = g + off * (near + u)
        acc[0] += fold8(u * u)
        acc[1] += fold8(u * a)
        acc[2] += fold8(h * h)
        acc[3] += fold8(h * u)
        acc[4] += fold8(h * a)

    @pl.when(i == ND - 1)
    def _():
        row = jnp.where(lane == 5, scal[0:1, 0:1], jnp.where(lane == 6, scal[0:1, 1:2], 0.0))
        for k in range(5):
            row = jnp.where(lane == k, total_of(acc[k]), row)
        sums_ref[...] = jnp.broadcast_to(row, sums_ref.shape)


def final_kernel(a_ref, u_ref, g_ref, center_ref, shared_ref, v_ref, out_ref, coef):
    i = pl.program_id(0)
    lane = lane_of((1, T))

    @pl.when(i == 0)
    def _():
        sums = jnp.sum(shared_ref[...], axis=0, keepdims=True)
        own = shared_ref[0:1, :]

        def pick(row, k):
            return jnp.sum(jnp.where(lane == k, row, 0.0), axis=1, keepdims=True)

        uu, ua, hh, hu, ha = [pick(sums, k) for k in range(5)]
        alpha1, norm = pick(own, 5), pick(own, 6)
        scale2 = 1.0 / jnp.maximum(norm, 1.0)
        square1 = jnp.maximum(scale2 * uu, 1.0)
        ratio2 = scale2 / square1
        alpha2 = ratio2 * (hu + alpha1 * uu - square1 * ua)
        move = alpha2 - alpha1
        nn = hh + square1 * square1 * norm + move * move * uu
        nn = nn - 2.0 * square1 * ha - 2.0 * move * hu + 2.0 * square1 * move * ua
        square2 = jnp.maximum(ratio2 * nn, 1.0)
        beta1, beta2 = jnp.sqrt(square1), jnp.sqrt(square2)
        cg = jnp.sqrt(ratio2) / beta2
        row = jnp.zeros((1, T), f32)
        off = center_ref[0:1, 0:1] - alpha1
        for k, value in enumerate(
            [alpha1, alpha2, beta1, beta2, cg * (off * (off - move) - square1), cg * (2.0 * off - move), cg]
        ):
            row = jnp.where(lane == k, value, row)
        coef[...] = jnp.broadcast_to(row, coef.shape)
        out_ref[...] = jnp.broadcast_to(row, out_ref.shape)

    ca, cu, cg = coef[0:1, 4:5], coef[0:1, 5:6], coef[0:1, 6:7]
    v_ref[0] = (cg * g_ref[i] + cu * u_ref[0].astype(f32) + ca * a_ref[0].astype(f32)).astype(bf16)


def swapped_down(start_vector):
    down = lax.axis_index(DN)
    cols = start_vector.shape[1]
    joined = jnp.zeros((ND, W, cols), start_vector.dtype)
    for s in range(ND):
        piece = lax.dynamic_slice_in_dim(start_vector, (down + s) % ND * W, W, 0)
        if s:
            piece = lax.ppermute(piece, DN, [(k, (k + s) % ND) for k in range(ND)])
        joined = lax.dynamic_update_slice(joined, piece[None], ((down - s) % ND, 0, 0))
    return joined


def body(start_vector, hop_tiles, tile_columns, tile_signs, occupation):
    rows, cols = start_vector.shape
    index = (tile_columns + NT * tile_signs).astype(jnp.int32).reshape(-1)
    up = lax.axis_index(UP)
    down = lax.axis_index(DN)
    occ = occupation.astype(bf16)
    occ_rows = occ.T
    a_cols = lax.dynamic_slice_in_dim(occ, down * cols + up * W, W, 1)
    a_cols = jnp.pad(a_cols, ((0, 0), (0, T - W)))
    b_rows = lax.dynamic_slice_in_dim(occ_rows, up * rows + down * W, W, 0)
    b_cols = jnp.moveaxis(occ.reshape(occ.shape[0], ND, cols), 1, 0)

    parts = pl.pallas_call(
        pack_kernel,
        out_shape=pltpu.HBM((NU, HEAD, T), bf16),
        compiler_params=pltpu.CompilerParams(vmem_limit_bytes=24 * MIB),
        name="pack",
    )(pltpu.with_memory_space_constraint(start_vector, pltpu.HBM))
    a_up = lax.all_to_all(parts, UP, 0, 0, tiled=True)
    a_dn = swapped_down(start_vector)

    hop_flops = 2 * NT * KT * T * T * T
    tile_bytes = NT * KT * T * T * 2
    cost = pl.CostEstimate(flops=hop_flops, bytes_accessed=tile_bytes + 8 * 2**20, transcendentals=0)
    tall = (NT * T, T)
    packs = (NU * ND, WH, T)
    wide = (ND, W, cols)
    xs_tall = pltpu.VMEM((2 * NT * T, T), bf16)
    some = pltpu.VMEM((G * T, T), f32)
    xs_turned = pltpu.VMEM((2 * NT, W, T), bf16)

    first_up = pl.pallas_call(
        first_up_kernel,
        grid_spec=pltpu.PrefetchScalarGridSpec(
            num_scalar_prefetch=1,
            grid=(STEPS,),
            in_specs=[whole((NU, HEAD, T)), tile_spec(), whole(occ_rows.shape), whole(a_cols.shape)],
            out_specs=[whole(packs), whole(tall), whole((8, T))],
            scratch_shapes=[xs_tall, pltpu.VMEM(tall, f32), some, pltpu.VMEM((2, 8, T), f32)],
        ),
        out_shape=[
            pltpu.HBM(packs, bf16),
            pltpu.HBM(tall, bf16),
            jax.ShapeDtypeStruct((8, T), f32),
        ],
        compiler_params=params(44),
        cost_estimate=cost,
        name="first_up",
    )
    p, x, sums = first_up(index, a_up, hop_tiles, occ_rows, a_cols)

    p_dn = lax.all_to_all(p, ALL, 0, 0, tiled=True)

    r, dots = pl.pallas_call(
        first_down_kernel,
        grid_spec=pltpu.PrefetchScalarGridSpec(
            num_scalar_prefetch=1,
            grid=(STEPS,),
            in_specs=[whole(wide), tile_spec()],
            out_specs=[pl.BlockSpec((1, W, cols), lambda i, *_: (i, 0, 0)), whole((8, T))],
            scratch_shapes=[xs_turned, pltpu.VMEM((8, T), f32)],
        ),
        out_shape=[pltpu.HBM(wide, bf16), jax.ShapeDtypeStruct((8, T), f32)],
        compiler_params=params(32),
        cost_estimate=cost,
        name="first_down",
    )(index, a_dn, hop_tiles)

    q = pl.pallas_call(
        second_up_kernel,
        grid_spec=pltpu.PrefetchScalarGridSpec(
            num_scalar_prefetch=1,
            grid=(STEPS,),
            in_specs=[whole(tall), tile_spec(), whole((8, T)), whole((8, T))],
            out_specs=pl.BlockSpec((NU, WH, T), lambda i, *_: (i, 0, 0)),
            scratch_shapes=[xs_tall, some, pltpu.VMEM((8, T), f32)],
        ),
        out_shape=pltpu.HBM(packs, bf16),
        compiler_params=params(32),
        cost_estimate=cost,
        name="second_up",
    )(index, x, hop_tiles, sums, dots)

    p_dn, q = lax.optimization_barrier((p_dn, q))
    q_dn = lax.all_to_all(q, ALL, 0, 0, tiled=True)

    near = pl.BlockSpec(memory_space=pltpu.VMEM)
    kept = pltpu.VMEM(wide, f32)
    u, t, center = pl.pallas_call(
        second_down_kernel,
        grid_spec=pltpu.PrefetchScalarGridSpec(
            num_scalar_prefetch=1,
            grid=(STEPS,),
            in_specs=[
                whole(wide),
                whole(wide),
                whole(packs),
                tile_spec(),
                whole(b_rows.shape),
                whole(b_cols.shape),
            ],
            out_specs=[whole(wide), whole(wide), whole((8, T))],
            scratch_shapes=[xs_turned, kept, pltpu.VMEM((2, 8, T), f32)],
        ),
        out_shape=[pltpu.HBM(wide, bf16), pltpu.HBM(wide, f32), jax.ShapeDtypeStruct((8, T), f32)],
        compiler_params=params(48),
        cost_estimate=cost,
        name="second_down",
    )(index, a_dn, r, p_dn, hop_tiles, b_rows, b_cols)

    block = pl.BlockSpec((1, W, cols), lambda i, *_: (i, 0, 0))
    g, partial = pl.pallas_call(
        joined_kernel,
        grid=(ND,),
        in_specs=[block, block, block, whole(packs), whole((8, T))],
        out_specs=[near, whole((NU * ND, T))],
        out_shape=[kept, jax.ShapeDtypeStruct((NU * ND, T), f32)],
        scratch_shapes=[pltpu.VMEM((5, 8, T), f32), pltpu.VMEM((8, T), f32)],
        compiler_params=params(20),
        name="joined",
    )(a_dn, u, t, q_dn, center)

    shared = lax.all_to_all(partial, ALL, 0, 0, tiled=True)
    v, scalars = pl.pallas_call(
        final_kernel,
        grid=(ND,),
        in_specs=[block, block, near, whole((8, T)), whole((NU * ND, T))],
        out_specs=[block, whole((8, T))],
        out_shape=[pltpu.HBM(wide, bf16), jax.ShapeDtypeStruct((8, T), f32)],
        scratch_shapes=[pltpu.VMEM((8, T), f32)],
        compiler_params=params(16),
        name="final",
    )(a_dn, u, g, center, shared)
    final = lax.all_to_all(v, DN, 0, 0, tiled=True).reshape(rows, cols)
    return final, scalars[0, 0:2], scalars[0, 2:4]


def solution(mesh):
    torus = Mesh(mesh.devices.reshape(2, 4, 2, 2, 4), ALL)
    return jax.shard_map(
        body,
        mesh=torus,
        in_specs=(P(UP, DN), P(), P(), P(), P()),
        out_specs=(P(UP, DN), P(), P()),
        check_vma=False,
    )
```

time: 307 us -> 300 us (0.977)
  Pallas kernels: 110 us -> 85.7 us
  starting transfers between devices: 44.6 us -> 61.3 us
  blocking collectives: 0 us -> 13.5 us
  between operations: 10.6 us -> 0.96 us
  local copies, waits for them, and re-layouts: 32.1 us -> 39.3 us
  waiting for transfers between devices: 93.6 us -> 88.6 us
  other arithmetic: 13.2 us -> 8.84 us
    all_to_all x5 -> x3, waiting for transfers between devices: 62.4 us -> 25.1 us  [the longest x1 19.6 us: body(): a_up = lax.all_to_all(parts, UP, 0, 0, tiled=True)]
    ppermute x0 -> x7, waiting for transfers between devices: none -> 31.5 us  [swapped_down(): piece = lax.ppermute(piece, DN, [(k, (k + s) % ND) for k in range(ND)])]
    pallas_call x1, Pallas kernels: 29.7 us -> 9.4 us  [body(): pl.pallas_call(second_up_kernel, grid_spec=pltpu.PrefetchScalarGridSpec(n...]
    ppermute x0 -> x7, starting transfers between devices: none -> 17.9 us  [swapped_down(): piece = lax.ppermute(piece, DN, [(k, (k + s) % ND) for k in range(ND)])]
    all_to_all x0 -> x1, blocking collectives: none -> 13.5 us  [body(): shared = lax.all_to_all(partial, ALL, 0, 0, tiled=True)]
    dynamic_update_slice x0 -> x8, local copies, waits for them, and re-layouts: none -> 6.17 us  [swapped_down(): lax.dynamic_update_slice(joined, piece[None], ((down - s) % ND, 0, 0))]
    unnamed x29, local copies, waits for them, and re-layouts: 20.1 us -> 25.7 us
    pallas_call x1, Pallas kernels: 15.1 us -> 9.77 us  [body(): pl.pallas_call(first_down_kernel, grid_spec=pltpu.PrefetchScalarGridSpec(...]
  transfers between devices with their start and end apart: 6 -> 11, of which waited for: 5 -> 4; matrix products, arithmetic and copies ran while one was open for 7% -> 8% of each run, Pallas kernels for 29% -> 24%
where the time goes in v2:
time: 300 us; the launch traced here: 298 us
  waiting for transfers between devices  88.6 us (30%)
  Pallas kernels  85.7 us (29%)
  starting transfers between devices  61.3 us (20%)
  local copies, waits for them, and re-layouts  39.3 us (13%)
  blocking collectives  13.5 us (4%)
  other arithmetic  8.84 us (3%)
    all_to_all x1, waiting for transfers between devices, body(): final = lax.all_to_all(v, DN, 0, 0, tiled=True).reshape(rows, cols)  32 us
    ppermute x7, waiting for transfers between devices, swapped_down(): piece = lax.ppermute(piece, DN, [(k, (k + s) % ND) for k in range(ND)])  31.5 us
    pallas_call x1, Pallas kernels, body(): pl.pallas_call(second_down_kernel, grid_spec=pltpu.PrefetchScalarGridSpec...  26.4 us
    unnamed x29, local copies, waits for them, and re-layouts  25.7 us
    all_to_all x1, starting transfers between devices, body(): p_dn = lax.all_to_all(p, ALL, 0, 0, tiled=True)  21 us
    pallas_call x1, Pallas kernels, body(): p, x, sums = first_up(index, a_up, hop_tiles, occ_rows, a_cols)  20.1 us
    all_to_all x1, waiting for transfers between devices, body(): a_up = lax.all_to_all(parts, UP, 0, 0, tiled=True)  19.6 us
    ppermute x7, starting transfers between devices, swapped_down(): piece = lax.ppermute(piece, DN, [(k, (k + s) % ND) for k in range(ND)])  17.9 us
  transfers between devices with their start and end apart: 11, of which 4 were waited for; matrix products, arithmetic and copies ran while one was open for 8% of the time, Pallas kernels for 24%

profile of v2, /device:TPU:24, one launch (start us, length us, event | category | flops | bytes accessed | tf_op | source)
XLA Modules:
  0.0 298.2 jit_solution(4258842558530245643)
XLA Ops:
  0.7 3.1 %constant_dynamic-slice_fusion.1 = (bf16[104,1664]{1,0:T(8,128)(2,1)}, bf16[104,1664]{1,0:T(8,128)(2,1)}, bf16[104,1664]{1,0:T(8,128)(2,1)}, bf16[104,1664]{1,0:...) fusion(bf16[832,1664]{1,0:T(8,128)(2,1)} %a_ref.1, ...), kind=kLoop, calls=%fused_computation.10 | loop fusion | bytes 4845596 | tf_op jit(solution)/shard_map/dynamic_slice | solution.py:421
  3.8 1.9 collective-permute-start
  5.7 3.6 %collective-permute-start.1 = (bf16[104,1664]{1,0:T(8,128)(2,1)}, bf16[104,1664]{1,0:T(8,128)(2,1)}, u32[]{:S(2)}, u32[]{:S(2)}) collective-permute-start(bf16[104,1664]{1,0:T(8,128)(2,1)} %get-tuple-element.38), channel_id=1, source_target_pairs={{0,2},{1,3},{2,4},{3,5},{4,6},{5,7},{6,0},{7,1},{8,10},{9,11},{10,... | collective-permute-start | bytes 1038344 | tf_op jit(solution)/shard_map/ppermute | solution.py:423
  11.0 2.3 collective-permute-start.3
  15.0 6.3 %pack.1 = bf16[16,704,128]{2,1,0:T(8,128)(2,1)} custom-call(bf16[832,1664]{1,0:T(8,128)(2,1)} %a_ref.1), custom_call_target="tpu_custom_call" | custom-call | tf_op jit(solution)/shard_map/pack/pallas_call | solution.py:440
  21.3 5.9 %all-to-all-start = ((bf16[16,704,128]{2,1,0:T(8,128)(2,1)}), bf16[16,704,128]{2,1,0:T(8,128)(2,1)}, u32[]{:S(2)}, u32[]{:S(2)}) async-start(bf16[16,704,128]{2,1,0:T(8,128)(2,1)} %pack.1), calls=%async_computation | async-start | bytes 5767168 | tf_op jit(solution)/shard_map/all_to_all | solution.py:446
  27.5 4.3 %copy.16 = s32[16,13312]{0,1:T(8,128)} copy(s32[16,13312]{1,0:T(8,128)S(1)} %copy-done.9) | data formatting | bytes 1703936 | tf_op args[4]
  31.8 3.2 %convert_element_type.5 = bf16[16,13312]{0,1:T(8,128)(2,1)S(1)} convert(s32[16,13312]{0,1:T(8,128)} %copy.16) | non-fusion elementwise | flops 212992 | bytes 1277952 | tf_op jit(solution)/shard_map/convert_element_type | solution.py:433
  35.0 5.6 %convert_bitcast_fusion.occ_rows_ref = bf16[13312,16]{1,0:T(8,128)(2,1)} fusion(s32[16,13312]{0,1:T(8,128)} %copy.16), kind=kLoop, calls=%fused_computation.20 | loop fusion | flops 212992 | bytes 1277952 | tf_op jit(solution)/shard_map/transpose | solution.py:434
  42.0 2.4 collective-permute-start.5
  45.4 19.6 %all-to-all-done.a_ref = bf16[16,704,128]{2,1,0:T(8,128)(2,1)} async-done(((bf16[16,704,128]{2,1,0:T(8,128)(2,1)}), bf16[16,704,128]{2,1,0:T(8,128)(2,1)}, u32[]{:S(2)}, u32[]{:S(2)}) %all-to-all-start) | async-done | bytes 2883616 | tf_op jit(solution)/shard_map/all_to_all | solution.py:446
  65.0 2.0 copy-done.2
  67.0 20.1 %first_up.1 = (bf16[128,88,128]{2,1,0:T(8,128)(2,1)}, bf16[13312,128]{1,0:T(8,128)(2,1)}, f32[8,128]{1,0:T(8,128)S(1)}) custom-call(s32[520]{0:T(1024)S(1)} %reshape.17.idx_ref, bf16[16,704,128]{2,1,0:T(8,128)(2,1)} %all-to-all-done.a_ref, bf16[104,5,128,128]{3,2,1,0:T(8,128)(2,1)} %tiles_ref.7, bf16[13312,16]{1,0:T(8,128)(2,1)S(1)} %copy-done.2, ...), custom_call_target="tpu_custom_call" | custom-call | flops 2181038080 | bytes 25427968 | tf_op jit(solution)/shard_map/first_up/pallas_call | solution.py:477
  87.0 21.0 %all-to-all-start.1 = ((bf16[128,88,128]{2,1,0:T(8,128)(2,1)}), bf16[128,88,128]{2,1,0:T(8,128)(2,1)}, u32[]{:S(2)}, u32[]{:S(2)}) async-start(bf16[128,88,128]{2,1,0:T(8,128)(2,1)} %get-tuple-element.18), calls=%async_computation.1 | async-start | bytes 5767168 | tf_op jit(solution)/shard_map/all_to_all | solution.py:479
  108.1 4.3 %collective-permute-start.6 = (bf16[104,1664]{1,0:T(8,128)(2,1)S(1)}, bf16[104,1664]{1,0:T(8,128)(2,1)S(1)}, u32[]{:S(2)}, u32[]{:S(2)}) collective-permute-start(bf16[104,1664]{1,0:T(8,128)(2,1)S(1)} %copy-done.10), channel_id=1, source_target_pairs={{0,7},{1,0},{2,1},{3,2},{4,3},{5,4},{6,5},{7,6},{8,15},{9,8},{10,9... | collective-permute-start | bytes 1038344 | tf_op jit(solution)/shard_map/ppermute | solution.py:423
  116.6 31.5 %collective-permute-done.6 = bf16[104,1664]{1,0:T(8,128)(2,1)S(1)} collective-permute-done((bf16[104,1664]{1,0:T(8,128)(2,1)S(1)}, bf16[104,1664]{1,0:T(8,128)(2,1)S(1)}, u32[]{:S(2)}, u32[]{:S(2)}) %collective-permute-start.6) | collective-permute-done | bytes 346144 | tf_op jit(solution)/shard_map/ppermute | solution.py:423
  148.1 5.8 %copy-done = bf16[104,5,128,128]{3,2,1,0:T(8,128)(2,1)S(1)} copy-done((bf16[104,5,128,128]{3,2,1,0:T(8,128)(2,1)S(1)}, bf16[104,5,128,128]{3,2,1,0:T(8,128)(2,1)}, u32[]{:S(2)}) %copy-start) | copy-done | bytes 17039384
  153.9 9.8 %first_down.1 = (bf16[8,104,1664]{2,1,0:T(8,128)(2,1)}, f32[8,128]{1,0:T(8,128)S(1)}) custom-call(s32[520]{0:T(1024)S(1)} %reshape.17.idx_ref, bf16[8,104,1664]{2,1,0:T(8,128)(2,1)S(1)} %bitcast_dynamic-update-slice_fusion.a_ref, bf16[104,5,128,128]{3,2,1,0:T(8,128)(2,1)S(1)} %copy-done), custom_call_target="tpu_custom_call" | custom-call | flops 2181038080 | bytes 25427968 | tf_op jit(solution)/shard_map/first_down/pallas_call | solution.py:481
  163.7 5.8 %copy-done.1 = bf16[104,5,128,128]{3,2,1,0:T(8,128)(2,1)S(1)} copy-done((bf16[104,5,128,128]{3,2,1,0:T(8,128)(2,1)S(1)}, bf16[104,5,128,128]{3,2,1,0:T(8,128)(2,1)}, u32[]{:S(2)}) %copy-start.1) | copy-done | bytes 17039384
  169.5 9.4 %second_up.1 = bf16[128,88,128]{2,1,0:T(8,128)(2,1)} custom-call(s32[520]{0:T(1024)S(1)} %reshape.17.idx_ref, bf16[13312,128]{1,0:T(8,128)(2,1)S(1)} %copy-done.6, bf16[104,5,128,128]{3,2,1,0:T(8,128)(2,1)S(1)} %copy-done.1, f32[8,128]{1,0:T(8,128)S(1)} %get-tuple-element.20.sums_ref, f32[8,128]{1,0:T(8,128)S(1)} %get-tuple-element.21.dots_ref), custom_call_target="tpu_custom_call" | custom-call | flops 2181038080 | bytes 25427968 | tf_op jit(solution)/shard_map/second_up/pallas_call | solution.py:496
  178.9 10.3 %all-to-all-start.2 = ((bf16[128,88,128]{2,1,0:T(8,128)(2,1)}), bf16[128,88,128]{2,1,0:T(8,128)(2,1)}, u32[]{:S(2)}, u32[]{:S(2)}) async-start(bf16[128,88,128]{2,1,0:T(8,128)(2,1)} %second_up.1), calls=%async_computation.2 | async-start | bytes 5767168 | tf_op jit(solution)/shard_map/all_to_all | solution.py:512
  189.3 3.3 %copy.19 = bf16[16,8,1664]{2,0,1:T(8,128)(2,1)S(1)} copy(bf16[16,8,1664]{0,2,1:T(8,128)(2,1)} %bitcast.34) | data formatting | bytes 851968 | tf_op jit(solution)/shard_map/reshape | solution.py:438
  192.6 1.8 copy-done.7
  194.4 26.4 %second_down.1 = (bf16[8,104,1664]{2,1,0:T(8,128)(2,1)}, f32[8,104,1664]{2,1,0:T(8,128)}, f32[8,128]{1,0:T(8,128)S(1)}) custom-call(s32[520]{0:T(1024)S(1)} %reshape.17.idx_ref, bf16[8,104,1664]{2,1,0:T(8,128)(2,1)S(1)} %bitcast_dynamic-update-slice_fusion.a_ref, bf16[8,104,1664]{2,1,0:T(8,128)(2,1)S(1)} %copy-done.7, ...), custom_call_target="tpu_custom_call" | custom-call | flops 2181038080 | bytes 25427968 | tf_op jit(solution)/shard_map/second_down/pallas_call | solution.py:516
  220.8 5.5 %all-to-all-done.2.q_ref = bf16[128,88,128]{2,1,0:T(8,128)(2,1)} async-done(((bf16[128,88,128]{2,1,0:T(8,128)(2,1)}), bf16[128,88,128]{2,1,0:T(8,128)(2,1)}, u32[]{:S(2)}, u32[]{:S(2)}) %all-to-all-start.2) | async-done | bytes 2883616 | tf_op jit(solution)/shard_map/all_to_all | solution.py:512
  226.3 1.8 copy-done.3
  228.1 2.6 copy-done.5
  230.7 8.4 %joined.1 = (f32[8,104,1664]{2,1,0:T(8,128)S(1)}, f32[128,128]{1,0:T(8,128)S(1)}) custom-call(bf16[8,104,1664]{2,1,0:T(8,128)(2,1)S(1)} %bitcast_dynamic-update-slice_fusion.a_ref, bf16[8,104,1664]{2,1,0:T(8,128)(2,1)S(1)} %copy-done.3, f32[8,104,1664]{2,1,0:T(8,128)S(1)} %copy-done.5, bf16[128,88,128]{2,1,0:T(8,128)(2,1)} %all-to-all-done.2.q_ref, ...), custom_call_target="tpu_custom_call" | custom-call | tf_op jit(solution)/shard_map/joined/pallas_call | solution.py:539
  239.1 13.5 %all_to_all.31 = f32[128,1,128]{2,1,0:T(1,128)S(1)} all-to-all(f32[128,1,128]{2,1,0:T(1,128)S(1)} %bitcast.33), channel_id=1, replica_groups=mesh['up_0'=2,'up_1'=4,'up_2'=2,'dn_0'=2,'dn_1'=4] {'up_0','up_1','up_2'..., dimensions={0} | all-to-all | bytes 131072 | tf_op jit(solution)/shard_map/all_to_all | solution.py:550
  252.6 5.3 %final.1 = (bf16[8,104,1664]{2,1,0:T(8,128)(2,1)}, f32[8,128]{1,0:T(8,128)S(1)}) custom-call(bf16[8,104,1664]{2,1,0:T(8,128)(2,1)S(1)} %bitcast_dynamic-update-slice_fusion.a_ref, bf16[8,104,1664]{2,1,0:T(8,128)(2,1)S(1)} %copy-done.4, f32[8,104,1664]{2,1,0:T(8,128)S(1)} %get-tuple-element.27.g_ref, f32[8,128]{1,0:T(8,128)S(1)} %get-tuple-element.26.center_ref, ...), custom_call_target="tpu_custom_call" | custom-call | tf_op jit(solution)/shard_map/final/pallas_call | solution.py:551
  257.9 6.1 %all-to-all-start.4 = ((bf16[8,104,1664]{2,1,0:T(8,128)(2,1)}), bf16[8,104,1664]{2,1,0:T(8,128)(2,1)S(1)}, u32[]{:S(2)}, u32[]{:S(2)}) async-start(bf16[8,104,1664]{2,1,0:T(8,128)(2,1)} %get-tuple-element.29), calls=%async_computation.4 | async-start | bytes 5537792 | tf_op jit(solution)/shard_map/all_to_all | solution.py:561
  264.6 32.0 %all-to-all-done.4 = bf16[8,104,1664]{2,1,0:T(8,128)(2,1)S(1)} async-done(((bf16[8,104,1664]{2,1,0:T(8,128)(2,1)}), bf16[8,104,1664]{2,1,0:T(8,128)(2,1)S(1)}, u32[]{:S(2)}, u32[]{:S(2)}) %all-to-all-start.4) | async-done | bytes 2768928 | tf_op jit(solution)/shard_map/all_to_all | solution.py:561
  (46 shorter events, 12.3 us)
Async XLA Ops:
  3.8 38.2 %collective-permute-start = (bf16[104,1664]{1,0:T(8,128)(2,1)}, bf16[104,1664]{1,0:T(8,128)(2,1)}, u32[]{:S(2)}, u32[]{:S(2)}) collective-permute-start(bf16[104,1664]{1,0:T(8,128)(2,1)} %get-tuple-element.39), channel_id=1, source_target_pairs={{0,1},{1,2},{2,3},{3,4},{4,5},{5,6},{6,7},{7,0},{8,9},{9,10},{10,1... | collective-permute-start | bytes 1038344 | tf_op jit(solution)/shard_map/ppermute | solution.py:423
  5.7 102.4 %collective-permute-start.1 = (bf16[104,1664]{1,0:T(8,128)(2,1)}, bf16[104,1664]{1,0:T(8,128)(2,1)}, u32[]{:S(2)}, u32[]{:S(2)}) collective-permute-start(bf16[104,1664]{1,0:T(8,128)(2,1)} %get-tuple-element.38), channel_id=1, source_target_pairs={{0,2},{1,3},{2,4},{3,5},{4,6},{5,7},{6,0},{7,1},{8,10},{9,11},{10,... | collective-permute-start | bytes 1038344 | tf_op jit(solution)/shard_map/ppermute | solution.py:423
  9.3 104.1 %collective-permute-start.2 = (bf16[104,1664]{1,0:T(8,128)(2,1)}, bf16[104,1664]{1,0:T(8,128)(2,1)}, u32[]{:S(2)}, u32[]{:S(2)}) collective-permute-start(bf16[104,1664]{1,0:T(8,128)(2,1)} %get-tuple-element.37), channel_id=1, source_target_pairs={{0,3},{1,4},{2,5},{3,6},{4,7},{5,0},{6,1},{7,2},{8,11},{9,12},{10,... | collective-permute-start | bytes 1038344 | tf_op jit(solution)/shard_map/ppermute | solution.py:423
  11.0 103.5 %collective-permute-start.3 = (bf16[104,1664]{1,0:T(8,128)(2,1)}, bf16[104,1664]{1,0:T(8,128)(2,1)}, u32[]{:S(2)}, u32[]{:S(2)}) collective-permute-start(bf16[104,1664]{1,0:T(8,128)(2,1)} %get-tuple-element.36), channel_id=1, source_target_pairs={{0,4},{1,5},{2,6},{3,7},{4,0},{5,1},{6,2},{7,3},{8,12},{9,13},{10,... | collective-permute-start | bytes 1038344 | tf_op jit(solution)/shard_map/ppermute | solution.py:423
  13.3 102.2 %collective-permute-start.4 = (bf16[104,1664]{1,0:T(8,128)(2,1)}, bf16[104,1664]{1,0:T(8,128)(2,1)}, u32[]{:S(2)}, u32[]{:S(2)}) collective-permute-start(bf16[104,1664]{1,0:T(8,128)(2,1)} %get-tuple-element.35), channel_id=1, source_target_pairs={{0,5},{1,6},{2,7},{3,0},{4,1},{5,2},{6,3},{7,4},{8,13},{9,14},{10,... | collective-permute-start | bytes 1038344 | tf_op jit(solution)/shard_map/ppermute | solution.py:423
  21.3 5.9 %copy-start.11 = (s32[104,5]{0,1:T(8,128)S(1)}, s32[104,5]{0,1:T(8,128)}, u32[]{:S(2)}) copy-start(s32[104,5]{0,1:T(8,128)} %param.7) | copy-start | bytes 6244
  21.3 5.9 %copy-start.12 = (s32[104,5]{0,1:T(8,128)S(1)}, s32[104,5]{0,1:T(8,128)}, u32[]{:S(2)}) copy-start(s32[104,5]{0,1:T(8,128)} %param.8) | copy-start | bytes 6244
  21.3 6.2 %copy-start.9 = (s32[16,13312]{1,0:T(8,128)S(1)}, s32[16,13312]{1,0:T(8,128)}, u32[]{:S(2)}) copy-start(s32[16,13312]{1,0:T(8,128)} %param.9) | copy-start | bytes 2555908
  21.3 43.7 %all-to-all-start = ((bf16[16,704,128]{2,1,0:T(8,128)(2,1)}), bf16[16,704,128]{2,1,0:T(8,128)(2,1)}, u32[]{:S(2)}, u32[]{:S(2)}) async-start(bf16[16,704,128]{2,1,0:T(8,128)(2,1)} %pack.1), calls=%async_computation | async-start | bytes 5767168 | tf_op jit(solution)/shard_map/all_to_all | solution.py:446
  35.0 5.7 %copy-start.8 = (bf16[16,13312]{0,1:T(8,128)(2,1)}, bf16[16,13312]{0,1:T(8,128)(2,1)S(1)}, u32[]{:S(2)}) copy-start(bf16[16,13312]{0,1:T(8,128)(2,1)S(1)} %convert_element_type.5) | copy-start | bytes 1277956
  42.0 74.5 %collective-permute-start.5 = (bf16[104,1664]{1,0:T(8,128)(2,1)}, bf16[104,1664]{1,0:T(8,128)(2,1)S(1)}, u32[]{:S(2)}, u32[]{:S(2)}) collective-permute-start(bf16[104,1664]{1,0:T(8,128)(2,1)} %get-tuple-element.34), channel_id=1, source_target_pairs={{0,6},{1,7},{2,0},{3,1},{4,2},{5,3},{6,4},{7,5},{8,14},{9,15},{10,... | collective-permute-start | bytes 1038344 | tf_op jit(solution)/shard_map/ppermute | solution.py:423
  65.0 2.0 copy-start.2
  87.0 21.0 %copy-start.10 = (bf16[104,1664]{1,0:T(8,128)(2,1)S(1)}, bf16[104,1664]{1,0:T(8,128)(2,1)}, u32[]{:S(2)}) copy-start(bf16[104,1664]{1,0:T(8,128)(2,1)} %get-tuple-element.33) | copy-start | bytes 1038340
  87.0 91.9 %all-to-all-start.1 = ((bf16[128,88,128]{2,1,0:T(8,128)(2,1)}), bf16[128,88,128]{2,1,0:T(8,128)(2,1)}, u32[]{:S(2)}, u32[]{:S(2)}) async-start(bf16[128,88,128]{2,1,0:T(8,128)(2,1)} %get-tuple-element.18), calls=%async_computation.1 | async-start | bytes 5767168 | tf_op jit(solution)/shard_map/all_to_all | solution.py:479
  108.1 39.9 %collective-permute-start.6 = (bf16[104,1664]{1,0:T(8,128)(2,1)S(1)}, bf16[104,1664]{1,0:T(8,128)(2,1)S(1)}, u32[]{:S(2)}, u32[]{:S(2)}) collective-permute-start(bf16[104,1664]{1,0:T(8,128)(2,1)S(1)} %copy-done.10), channel_id=1, source_target_pairs={{0,7},{1,0},{2,1},{3,2},{4,3},{5,4},{6,5},{7,6},{8,15},{9,8},{10,9... | collective-permute-start | bytes 1038344 | tf_op jit(solution)/shard_map/ppermute | solution.py:423
  148.1 5.8 %copy-start = (bf16[104,5,128,128]{3,2,1,0:T(8,128)(2,1)S(1)}, bf16[104,5,128,128]{3,2,1,0:T(8,128)(2,1)}, u32[]{:S(2)}) copy-start(bf16[104,5,128,128]{3,2,1,0:T(8,128)(2,1)} %tiles_ref.7) | copy-start | bytes 51118084
  153.9 9.8 %copy-start.6 = (bf16[13312,128]{1,0:T(8,128)(2,1)S(1)}, bf16[13312,128]{1,0:T(8,128)(2,1)}, u32[]{:S(2)}) copy-start(bf16[13312,128]{1,0:T(8,128)(2,1)} %get-tuple-element.19.x_ref) | copy-start | bytes 10223620
  163.7 5.8 %copy-start.1 = (bf16[104,5,128,128]{3,2,1,0:T(8,128)(2,1)S(1)}, bf16[104,5,128,128]{3,2,1,0:T(8,128)(2,1)}, u32[]{:S(2)}) copy-start(bf16[104,5,128,128]{3,2,1,0:T(8,128)(2,1)} %tiles_ref.7) | copy-start | bytes 51118084
  178.9 47.4 %all-to-all-start.2 = ((bf16[128,88,128]{2,1,0:T(8,128)(2,1)}), bf16[128,88,128]{2,1,0:T(8,128)(2,1)}, u32[]{:S(2)}, u32[]{:S(2)}) async-start(bf16[128,88,128]{2,1,0:T(8,128)(2,1)} %second_up.1), calls=%async_computation.2 | async-start | bytes 5767168 | tf_op jit(solution)/shard_map/all_to_all | solution.py:512
  192.6 1.8 copy-start.7
  226.3 1.8 copy-start.3
  228.1 2.6 copy-start.5
  230.7 21.9 %copy-start.4 = (bf16[8,104,1664]{2,1,0:T(8,128)(2,1)S(1)}, bf16[8,104,1664]{2,1,0:T(8,128)(2,1)}, u32[]{:S(2)}) copy-start(bf16[8,104,1664]{2,1,0:T(8,128)(2,1)} %get-tuple-element.23.u_ref) | copy-start | bytes 8306692
  257.9 38.7 %all-to-all-start.4 = ((bf16[8,104,1664]{2,1,0:T(8,128)(2,1)}), bf16[8,104,1664]{2,1,0:T(8,128)(2,1)S(1)}, u32[]{:S(2)}, u32[]{:S(2)}) async-start(bf16[8,104,1664]{2,1,0:T(8,128)(2,1)} %get-tuple-element.29), calls=%async_computation.4 | async-start | bytes 5537792 | tf_op jit(solution)/shard_map/all_to_all | solution.py:561

commit v3 on v2

v3 whole, which is shorter than its diff:
```python
import jax
import jax.numpy as jnp
from jax import lax
from jax.experimental import pallas as pl
from jax.experimental.pallas import tpu as pltpu
from jax.sharding import Mesh
from jax.sharding import PartitionSpec as P


UP = ("up_0", "up_1", "up_2")
DN = ("dn_0", "dn_1")
ALL = UP + DN
coupling = 4.0

f32 = jnp.float32
bf16 = jnp.bfloat16

T = 128
NT = 104
KT = 5
G = 13
STEPS = NT // G
W = 104
NU = 16
ND = 8
MIB = 1024 * 1024


def params(mib):
    return pltpu.CompilerParams(dimension_semantics=("arbitrary",), vmem_limit_bytes=mib * MIB)


def whole(shape):
    zeros = (0,) * len(shape)
    return pl.BlockSpec(shape, lambda i, *_: zeros, pipeline_mode=pl.Buffered(1))


def far(x):
    return pltpu.with_memory_space_constraint(x, pltpu.HBM)


def tile_spec():
    return pl.BlockSpec((G, KT, T, T), lambda i, *_: (i, 0, 0, 0))


def lane_of(shape):
    return lax.broadcasted_iota(jnp.int32, shape, len(shape) - 1)


def total_of(x):
    return jnp.sum(jnp.sum(x, axis=0, keepdims=True), axis=1, keepdims=True)


def fold8(x):
    return jnp.sum(x.reshape(x.shape[0] // 8, 8, x.shape[1]), axis=0)


def hop_nat(i, g, idx_ref, tiles_ref, xs):
    row = i * G + g
    left = jnp.concatenate([tiles_ref[g, k] for k in range(KT)], axis=1)
    right = [xs[pl.ds(pl.multiple_of(idx_ref[row * KT + k] * T, T), T), :] for k in range(KT)]
    return jnp.dot(left, jnp.concatenate(right, axis=0), preferred_element_type=f32)


def hop_turned(row, idx_ref, tiles, xs):
    right = jnp.concatenate([tiles[row, k] for k in range(KT)], axis=1)
    left = jnp.concatenate([xs[idx_ref[row * KT + k]] for k in range(KT)], axis=1)
    return lax.dot_general(left, right, (((1,), (1,)), ((), ())), preferred_element_type=f32)


LOW = T - W
STRIPS = -(-W // LOW)


def turned(x, shift):
    shift %= T
    return pltpu.roll(x, shift, 1) if shift else x


def with_strip(head, tail, k, lane):
    return jnp.where(lane < W, head, turned(tail, W - LOW * k))


def from_strips(strips, lane):
    value = turned(strips[-1], LOW * (STRIPS - 1) - W)
    for k in reversed(range(STRIPS - 1)):
        value = jnp.where(lane < LOW * (k + 1), turned(strips[k], LOW * k - W), value)
    return value


ROWS = 832
HEAD = 704
H = 64
WH = 88
S = W - WH


def pack_kernel(a_ref, out_ref):
    lane = lane_of((1, T))

    def cut(u, block):
        q, o = divmod(u * W, T)
        rows = slice(block * H, (block + 1) * H)
        x = turned(a_ref[rows, q * T : (q + 1) * T].astype(f32), -o)
        if o + W > T:
            y = turned(a_ref[rows, (q + 1) * T : (q + 2) * T].astype(f32), -o)
            x = jnp.where(lane < T - o, x, y)
        return x

    for u in range(NU):
        tails = [cut(u, HEAD // H + h) for h in range(2)]
        for block in range(HEAD // H):
            x = cut(u, block)
            if block < 2 * STRIPS:
                x = with_strip(x, tails[block % 2], block // 2, lane)
            out_ref[u, block * H : (block + 1) * H, :] = x.astype(bf16)


def packed(values, t, lane):
    x = values[pl.ds(pl.multiple_of(t * W, 8), WH), :]
    tail = values[pl.ds(pl.multiple_of(t * W + WH, 8), S), :]
    found = [with_strip(x[S * k : S * (k + 1)], tail, k, lane) for k in range(STRIPS)]
    return jnp.concatenate(found + [x[S * STRIPS :]], axis=0)


def unpacked(x, lane):
    tail = from_strips([x[S * k : S * (k + 1)] for k in range(STRIPS)], lane)
    return jnp.concatenate([x, tail], axis=0)


FREE = S * (STRIPS - 1)
FREE_LANE = W + W - LOW * (STRIPS - 1)


def spread(a_ref, lane, keep):
    def put(s, c):
        for block in range(HEAD // H):
            keep(pl.multiple_of(s * ROWS + block * H, H), a_ref[s, block * H : (block + 1) * H, :].astype(f32))
        for h in range(2):
            strips = [a_ref[s, (2 * k + h) * H : (2 * k + h + 1) * H, :].astype(f32) for k in range(STRIPS)]
            keep(pl.multiple_of(s * ROWS + HEAD + h * H, H), from_strips(strips, lane))
        return c

    lax.fori_loop(0, NU, put, 0)


def keep_both(xs, at, n, x):
    x = x.astype(bf16)
    xs[pl.ds(at, n), :] = x
    xs[pl.ds(NT * T + at, n), :] = -x


def first_up_kernel(idx_ref, a_ref, tiles_ref, mean_ref, p_ref, flat_ref, sums_ref, xs, some_p, acc):
    i = pl.program_id(0)
    lane = lane_of((1, T))

    @pl.when(i == 0)
    def _():
        acc[...] = jnp.zeros_like(acc)
        spread(a_ref, lane, lambda at, x: keep_both(xs, at, H, jnp.where(lane < W, x, 0.0)))

    for g in range(G):
        rows = pl.ds(pl.multiple_of((i * G + g) * T, T), T)
        p = hop_nat(i, g, idx_ref, tiles_ref, xs).astype(bf16)
        flat_ref[g * T : (g + 1) * T, :] = p
        p = p.astype(f32)
        some_p[g * T : (g + 1) * T, :] = p
        a = xs[rows, :].astype(f32)
        acc[0] += fold8(p * a)
        acc[1] += fold8(a * a)
    for t in range(NU):
        p_ref[i * NU + t] = packed(some_p, t, lane).astype(bf16)

    @pl.when(i == STEPS - 1)
    def _():
        energy = total_of(acc[0])
        center = (2.0 * energy / jnp.maximum(total_of(acc[1]), 1e-30) + mean_ref[0:1, 0:1]).astype(bf16)
        sub = lax.broadcasted_iota(jnp.int32, (8, T), 0)
        sums_ref[...] = jnp.where(sub == 0, energy, center.astype(f32))
        fill = jnp.broadcast_to(center, (S, T))
        free = lane_of((S, T)) >= FREE_LANE

        def mark(s, c):
            for k in range(8):
                at = s * 8 + k
                p_ref[at, FREE : FREE + S, :] = jnp.where(free, fill, p_ref[at, FREE : FREE + S, :])
            return c

        lax.fori_loop(0, NU * ND // 8, mark, 0)


def second_up_kernel(idx_ref, a_ref, flat_ref, tiles_ref, occ_rows_ref, occ_cols_ref, sums_ref, q_ref, out_ref, xs, some_q, acc):
    i = pl.program_id(0)
    lane = lane_of((1, T))

    @pl.when(i == 0)
    def _():
        acc[...] = jnp.zeros_like(acc)
        center = sums_ref[1:2, :]

        def keep(at, a):
            a = jnp.where(lane < W, a, 0.0)
            rows = pl.ds(at, H)
            diag = coupling * jnp.dot(occ_rows_ref[rows, :], occ_cols_ref[...], preferred_element_type=f32)
            acc[...] += fold8(diag * a * a)
            keep_both(xs, at, H, flat_ref[rows, :].astype(f32) + (diag - center) * a)

        spread(a_ref, lane, keep)
        out_ref[...] = jnp.broadcast_to(sums_ref[0:1, :] + total_of(acc[...]), out_ref.shape)

    for g in range(G):
        some_q[g * T : (g + 1) * T, :] = hop_nat(i, g, idx_ref, tiles_ref, xs)
    for t in range(NU):
        q_ref[t] = packed(some_q, t, lane).astype(bf16)


def pieces_in(o):
    found = []
    for u in range(NU):
        lo, hi = max(u * W, o * T), min((u + 1) * W, (o + 1) * T)
        if lo < hi:
            found.append((u, hi - o * T))
    return found


def assembled(rolled, o, lane):
    found = pieces_in(o)
    value = rolled[found[-1][0]]
    for u, end in reversed(found[:-1]):
        value = jnp.where(lane < end, rolled[u], value)
    return value


def down_kernel(idx_ref, *refs):
    pieces, refs = refs[:ND], refs[ND:]
    p_ref, tiles_ref, occ_rows_ref, occ_cols_ref = refs[:4]
    a_ref, u_ref, t_ref, sums_ref, tiles, xs, some_r, some_u, some_t, acc, sems = refs[4:]
    i = pl.program_id(0)
    lane = lane_of((1, T))

    def fetch(k):
        rows = pl.ds(k * G, G)
        return pltpu.make_async_copy(tiles_ref.at[rows], tiles.at[rows], sems.at[k])

    @pl.when(i == 0)
    def _():
        for k in range(STEPS):
            fetch(k).start()
        acc[...] = jnp.zeros_like(acc)
        down = idx_ref[NT * KT]
        for s in range(ND):
            source = lax.rem(down + ND - s, ND)
            for o in range(G):
                x = pieces[s][:, o * T : (o + 1) * T]
                xs[source * G + o] = x
                xs[NT + source * G + o] = -x

    @pl.when(i < STEPS)
    def _():
        fetch(i).wait()
        for g in range(G):
            row = i * G + g
            r = hop_turned(row, idx_ref, tiles, xs)
            some_r[row] = r
            acc[2] += fold8(r * xs[row].astype(f32))

    @pl.when(i == STEPS)
    def _():
        def first(d, c):
            rolled, centers = {}, {}
            for o in range(G):
                for u, _end in pieces_in(o):
                    if u in rolled:
                        continue
                    x = p_ref[u * ND + d].astype(f32)
                    centers[u] = jnp.sum(
                        jnp.where(lane == FREE_LANE, x[FREE : FREE + 1, :], 0.0), axis=1, keepdims=True
                    )
                    rolled[u] = turned(unpacked(x, lane), u * W)
                p = assembled(rolled, o, lane)
                center = assembled(centers, o, lane)
                at = d * G + o
                a = xs[at].astype(f32)
                diag = coupling * jnp.dot(
                    occ_rows_ref[...], occ_cols_ref[d, :, o * T : (o + 1) * T], preferred_element_type=f32
                )
                w = p + some_r[at] + diag * a
                some_u[at] = w
                some_t[at] = center * p + diag * w
                xs[NT + at] = p.astype(bf16)
                acc[0] += fold8(w * a)
                acc[1] += fold8(a * a)
            return c

        lax.fori_loop(0, ND, first, 0)
        center = total_of(acc[0]) / jnp.maximum(total_of(acc[1]), 1e-30)
        sub = lax.broadcasted_iota(jnp.int32, (8, T), 0)
        sums_ref[...] = jnp.where(sub == 0, center, total_of(acc[2]))

        def second(d, c):
            for o in range(G):
                at = d * G + o
                a = xs[at]
                a_ref[d, :, o * T : (o + 1) * T] = a
                w = some_u[at]
                u = w - center * a.astype(f32)
                some_u[at] = u
                some_t[at] += center * (some_r[at] - w - u)
                x = (u + xs[NT + at].astype(f32)).astype(bf16)
                xs[at] = x
                xs[NT + at] = -x
            return c

        lax.fori_loop(0, ND, second, 0)

    @pl.when(i >= STEPS)
    def _():
        for g in range(G):
            row = (i - STEPS) * G + g
            lanes = slice(g * T, (g + 1) * T)
            u_ref[0, :, lanes] = some_u[row]
            t_ref[0, :, lanes] = some_t[row] + hop_turned(row, idx_ref, tiles, xs)


def joined_kernel(a_ref, u_ref, t_ref, q_ref, up_ref, down_ref, g_ref, u_out_ref, sums_ref, acc):
    i = pl.program_id(0)
    lane = lane_of((1, T))

    @pl.when(i == 0)
    def _():
        acc[...] = jnp.zeros_like(acc)

    rolled = {}
    for o in range(G):
        for u, _end in pieces_in(o):
            if u not in rolled:
                rolled[u] = turned(unpacked(q_ref[u * ND + i].astype(f32), lane), u * W)
        lanes = slice(o * T, (o + 1) * T)
        a = a_ref[0, :, lanes].astype(f32)
        u = u_ref[0, :, lanes]
        g = assembled(rolled, o, lane) + t_ref[0, :, lanes]
        g_ref[i, :, lanes] = g
        u_out_ref[i, :, lanes] = u
        for k, product in enumerate([u * u, u * a, a * a, g * g, g * u, g * a]):
            acc[k] += fold8(product)

    @pl.when(i == ND - 1)
    def _():
        row = jnp.where(lane == 6, up_ref[0:1, :] + down_ref[1:2, :], down_ref[0:1, :])
        for k in range(6):
            row = jnp.where(lane == k, total_of(acc[k]), row)
        sums_ref[...] = jnp.broadcast_to(row, sums_ref.shape)


def final_kernel(a_ref, u_ref, g_ref, center_ref, shared_ref, v_ref, out_ref, coef):
    i = pl.program_id(0)
    lane = lane_of((1, T))

    @pl.when(i == 0)
    def _():
        uu, ua, aa, gg, gu, ga, energy, center = [shared_ref[:, k : k + 1] for k in range(8)]

        def total(x):
            return jnp.sum(x, axis=0, keepdims=True)

        norm = total(aa)
        scale2 = 1.0 / jnp.maximum(norm, 1.0)
        alpha1 = total(energy) * scale2
        off = center - alpha1
        hh = total(gg + 4.0 * off * (gu + off * (uu + off * ua)) + off * off * (2.0 * ga + off * off * aa))
        hu = total(gu + off * (2.0 * uu + ga + off * (3.0 * ua + off * aa)))
        ha = total(ga + off * (2.0 * ua + off * aa))
        uu = total(uu + off * (2.0 * ua + off * aa))
        ua = total(ua + off * aa)
        square1 = jnp.maximum(scale2 * uu, 1.0)
        ratio2 = scale2 / square1
        alpha2 = ratio2 * (hu + alpha1 * uu - square1 * ua)
        move = alpha2 - alpha1
        nn = hh + square1 * square1 * norm + move * move * uu
        nn = nn - 2.0 * square1 * ha - 2.0 * move * hu + 2.0 * square1 * move * ua
        square2 = jnp.maximum(ratio2 * nn, 1.0)
        beta1, beta2 = jnp.sqrt(square1), jnp.sqrt(square2)
        cg = jnp.sqrt(ratio2) / beta2
        off = center_ref[0:1, 0:1] - alpha1
        row = jnp.zeros((1, T), f32)
        for k, value in enumerate(
            [alpha1, alpha2, beta1, beta2, cg * (off * (off - move) - square1), cg * (2.0 * off - move), cg]
        ):
            row = jnp.where(lane == k, value, row)
        coef[...] = jnp.broadcast_to(row, coef.shape)
        out_ref[...] = jnp.broadcast_to(row, out_ref.shape)

    ca, cu, cg = coef[0:1, 4:5], coef[0:1, 5:6], coef[0:1, 6:7]
    v_ref[0] = (cg * g_ref[i] + cu * u_ref[i] + ca * a_ref[0].astype(f32)).astype(bf16)


def swapped_down(start_vector):
    down = lax.axis_index(DN)
    pieces = []
    for s in range(ND):
        piece = lax.dynamic_slice_in_dim(start_vector, (down + s) % ND * W, W, 0)
        if s:
            piece = lax.ppermute(piece, DN, [(k, (k + s) % ND) for k in range(ND)])
        pieces.append(piece)
    return pieces


def body(start_vector, hop_tiles, tile_columns, tile_signs, occupation):
    rows, cols = start_vector.shape
    index = (tile_columns + NT * tile_signs).astype(jnp.int32).reshape(-1)
    up = lax.axis_index(UP)
    down = lax.axis_index(DN)
    occ = occupation.astype(bf16)
    occ_rows = occ.T
    a_cols = lax.dynamic_slice_in_dim(occ, down * cols + up * W, W, 1)
    a_cols = jnp.pad(a_cols, ((0, 0), (0, T - W)))
    filled = jnp.sum(occ, axis=1, dtype=f32) * jnp.sum(a_cols, axis=1, dtype=f32)
    mean = jnp.full((8, T), coupling * jnp.sum(filled) / (occ.shape[1] * W), f32)
    b_rows = lax.dynamic_slice_in_dim(occ_rows, up * rows + down * W, W, 0)
    b_cols = jnp.moveaxis(occ.reshape(occ.shape[0], ND, cols), 1, 0)

    parts = pl.pallas_call(
        pack_kernel,
        out_shape=pltpu.HBM((NU, HEAD, T), bf16),
        compiler_params=pltpu.CompilerParams(vmem_limit_bytes=24 * MIB),
        name="pack",
    )(far(start_vector))
    a_up = lax.all_to_all(parts, UP, 0, 0, tiled=True)
    pieces = swapped_down(start_vector)

    hop_flops = 2 * NT * KT * T * T * T
    tile_bytes = NT * KT * T * T * 2
    cost = pl.CostEstimate(flops=hop_flops, bytes_accessed=tile_bytes + 8 * 2**20, transcendentals=0)
    tall = (NT * T, T)
    packs = (NU * ND, WH, T)
    wide = (ND, W, cols)
    xs_tall = pltpu.VMEM((2 * NT * T, T), bf16)
    some = pltpu.VMEM((G * T, T), f32)

    first_up = pl.pallas_call(
        first_up_kernel,
        grid_spec=pltpu.PrefetchScalarGridSpec(
            num_scalar_prefetch=1,
            grid=(STEPS,),
            in_specs=[whole((NU, HEAD, T)), tile_spec(), whole((8, T))],
            out_specs=[whole(packs), pl.BlockSpec((G * T, T), lambda i, *_: (i, 0)), whole((8, T))],
            scratch_shapes=[xs_tall, some, pltpu.VMEM((2, 8, T), f32)],
        ),
        out_shape=[
            pltpu.HBM(packs, bf16),
            pltpu.HBM(tall, bf16),
            jax.ShapeDtypeStruct((8, T), f32),
        ],
        compiler_params=params(28),
        cost_estimate=cost,
        name="first_up",
    )
    p, flat, sums = first_up(index, a_up, far(hop_tiles), mean)

    p_dn = lax.all_to_all(p, ALL, 0, 0, tiled=True)

    second_up = pl.pallas_call(
        second_up_kernel,
        grid_spec=pltpu.PrefetchScalarGridSpec(
            num_scalar_prefetch=1,
            grid=(STEPS,),
            in_specs=[
                whole((NU, HEAD, T)),
                whole(tall),
                tile_spec(),
                whole(occ_rows.shape),
                whole(a_cols.shape),
                whole((8, T)),
            ],
            out_specs=[pl.BlockSpec((NU, WH, T), lambda i, *_: (i, 0, 0)), whole((8, T))],
            scratch_shapes=[xs_tall, some, pltpu.VMEM((8, T), f32)],
        ),
        out_shape=[pltpu.HBM(packs, bf16), jax.ShapeDtypeStruct((8, T), f32)],
        compiler_params=params(32),
        cost_estimate=cost,
        name="second_up",
    )
    q, up_dots = second_up(index, far(a_up), flat, far(hop_tiles), far(occ_rows), a_cols, sums)

    p_dn, q, b_cols = lax.optimization_barrier((p_dn, q, b_cols))
    q_dn = lax.all_to_all(q, ALL, 0, 0, tiled=True)

    near = pl.BlockSpec(memory_space=pltpu.VMEM)
    kept = pltpu.VMEM(wide, f32)
    cut = pltpu.VMEM((NT, W, T), f32)
    late = pl.BlockSpec((1, W, cols), lambda i, *_: (jnp.maximum(i - STEPS, 0), 0, 0))
    a_dn, u, t, down_dots = pl.pallas_call(
        down_kernel,
        grid_spec=pltpu.PrefetchScalarGridSpec(
            num_scalar_prefetch=1,
            grid=(2 * STEPS,),
            in_specs=[whole((W, cols))] * ND
            + [
                whole(packs),
                pl.BlockSpec(memory_space=pl.ANY),
                whole(b_rows.shape),
                whole(b_cols.shape),
            ],
            out_specs=[whole(wide), late, late, whole((8, T))],
            scratch_shapes=[
                pltpu.VMEM((NT, KT, T, T), bf16),
                pltpu.VMEM((2 * NT, W, T), bf16),
                cut,
                cut,
                cut,
                pltpu.VMEM((3, 8, T), f32),
                pltpu.SemaphoreType.DMA((STEPS,)),
            ],
        ),
        out_shape=[
            pltpu.HBM(wide, bf16),
            pltpu.HBM(wide, f32),
            pltpu.HBM(wide, f32),
            jax.ShapeDtypeStruct((8, T), f32),
        ],
        compiler_params=params(56),
        cost_estimate=cost,
        name="down",
    )(jnp.concatenate([index, down[None]]), *[far(x) for x in pieces], p_dn, far(hop_tiles), b_rows, b_cols)

    block = pl.BlockSpec((1, W, cols), lambda i, *_: (i, 0, 0))
    g, u, partial = pl.pallas_call(
        joined_kernel,
        grid=(ND,),
        in_specs=[block, block, block, whole(packs), whole((8, T)), whole((8, T))],
        out_specs=[near, near, whole((NU * ND, T))],
        out_shape=[kept, kept, jax.ShapeDtypeStruct((NU * ND, T), f32)],
        scratch_shapes=[pltpu.VMEM((6, 8, T), f32)],
        compiler_params=params(20),
        name="joined",
    )(far(a_dn), far(u), far(t), q_dn, up_dots, down_dots)

    shared = lax.all_to_all(partial, ALL, 0, 0, tiled=True)
    v, scalars = pl.pallas_call(
        final_kernel,
        grid=(ND,),
        in_specs=[block, near, near, whole((8, T)), whole((NU * ND, T))],
        out_specs=[block, whole((8, T))],
        out_shape=[pltpu.HBM(wide, bf16), jax.ShapeDtypeStruct((8, T), f32)],
        scratch_shapes=[pltpu.VMEM((8, T), f32)],
        compiler_params=params(16),
        name="final",
    )(a_dn, u, g, down_dots, shared)
    final = lax.all_to_all(v, DN, 0, 0, tiled=True).reshape(rows, cols)
    return final, scalars[0, 0:2], scalars[0, 2:4]


def solution(mesh):
    torus = Mesh(mesh.devices.reshape(2, 4, 2, 2, 4), ALL)
    return jax.shard_map(
        body,
        mesh=torus,
        in_specs=(P(UP, DN), P(), P(), P(), P()),
        out_specs=(P(UP, DN), P(), P()),
        check_vma=False,
    )
```

time: 300 us -> 312 us (1.040)
  waiting for transfers between devices: 88.6 us -> 118 us
  local copies, waits for them, and re-layouts: 39.3 us -> 17 us
  starting transfers between devices: 61.3 us -> 54.6 us
  blocking collectives: 13.5 us -> 19.4 us
  Pallas kernels: 85.7 us -> 91.6 us
    ppermute x7, waiting for transfers between devices: 31.5 us -> 49.3 us  [swapped_down(): piece = lax.ppermute(piece, DN, [(k, (k + s) % ND) for k in range(ND)])]
    unnamed x29, local copies, waits for them, and re-layouts: 25.7 us -> 8.16 us
    all_to_all x1, waiting for transfers between devices: 0.01 us -> 13.6 us  [body(): p_dn = lax.all_to_all(p, ALL, 0, 0, tiled=True)]
    all_to_all x1, starting transfers between devices: 21 us -> 10.2 us  [body(): p_dn = lax.all_to_all(p, ALL, 0, 0, tiled=True)]
    ppermute x7, starting transfers between devices: 17.9 us -> 26.6 us  [swapped_down(): piece = lax.ppermute(piece, DN, [(k, (k + s) % ND) for k in range(ND)])]
    reduce_sum x0 -> x3, other arithmetic: none -> 6.94 us  [the longest x1 6.3 us: body(): jnp.sum(occ, axis=1, dtype=f32) * jnp.sum(a_cols, axis=1, dtype=f32)]
    dynamic_update_slice x8 -> x0, local copies, waits for them, and re-layouts: 6.17 us -> none  [swapped_down(): lax.dynamic_update_slice(joined, piece[None], ((down - s) % ND, 0, 0))]
    all_to_all x1, blocking collectives: 13.5 us -> 19.4 us  [body(): shared = lax.all_to_all(partial, ALL, 0, 0, tiled=True)]
  transfers between devices with their start and end apart: 11 -> 11, of which waited for: 4 -> 6; matrix products, arithmetic and copies ran while one was open for 8% -> 7% of each run, Pallas kernels for 24% -> 17%
where the time goes in v3:
time: 312 us; the launch traced here: 310 us
  waiting for transfers between devices  118 us (38%)
  Pallas kernels  91.6 us (29%)
  starting transfers between devices  54.6 us (18%)
  blocking collectives  19.4 us (6%)
  local copies, waits for them, and re-layouts  17 us (5%)
  other arithmetic  7.61 us (2%)
    ppermute x7, waiting for transfers between devices, swapped_down(): piece = lax.ppermute(piece, DN, [(k, (k + s) % ND) for k in range(ND)])  49.3 us
    pallas_call x1, Pallas kernels, body(): pl.pallas_call(down_kernel, grid_spec=pltpu.PrefetchScalarGridSpec(num_sc...  33 us
    all_to_all x1, waiting for transfers between devices, body(): final = lax.all_to_all(v, DN, 0, 0, tiled=True).reshape(rows, cols)  32 us
    ppermute x7, starting transfers between devices, swapped_down(): piece = lax.ppermute(piece, DN, [(k, (k + s) % ND) for k in range(ND)])  26.6 us
    all_to_all x1, waiting for transfers between devices, body(): a_up = lax.all_to_all(parts, UP, 0, 0, tiled=True)  23.4 us
    pallas_call x1, Pallas kernels, body(): second_up(index, far(a_up), flat, far(hop_tiles), far(occ_rows), a_cols,...  19.4 us
    all_to_all x1, blocking collectives, body(): shared = lax.all_to_all(partial, ALL, 0, 0, tiled=True)  19.4 us
    pallas_call x1, Pallas kernels, body(): p, flat, sums = first_up(index, a_up, far(hop_tiles), mean)  17 us
  transfers between devices with their start and end apart: 11, of which 6 were waited for; matrix products, arithmetic and copies ran while one was open for 7% of the time, Pallas kernels for 17%

profile of v3, /device:TPU:24, one launch (start us, length us, event | category | flops | bytes accessed | tf_op | source)
XLA Modules:
  0.0 310.0 jit_solution(2856836865161726598)
XLA Ops:
  0.6 6.4 %pack.1 = bf16[16,704,128]{2,1,0:T(8,128)(2,1)} custom-call(bf16[832,1664]{1,0:T(8,128)(2,1)} %a_ref.1), custom_call_target="tpu_custom_call" | custom-call | tf_op jit(solution)/shard_map/pack/pallas_call | solution.py:422
  7.1 5.9 %all-to-all-start = ((bf16[16,704,128]{2,1,0:T(8,128)(2,1)}), bf16[16,704,128]{2,1,0:T(8,128)(2,1)S(1)}, u32[]{:S(2)}, u32[]{:S(2)}) async-start(bf16[16,704,128]{2,1,0:T(8,128)(2,1)} %pack.1), calls=%async_computation | async-start | bytes 5767168 | tf_op jit(solution)/shard_map/all_to_all | solution.py:428
  13.3 5.1 %copy.16 = s32[16,13312]{0,1:T(8,128)} copy(s32[16,13312]{1,0:T(8,128)} %param.9) | data formatting | bytes 1703936 | tf_op args[4]
  18.4 6.3 %convert_reduce_fusion = (f32[16]{0:T(128)S(1)}, bf16[16,13312]{0,1:T(8,128)(2,1)}) fusion(s32[16,13312]{0,1:T(8,128)} %copy.16), kind=kLoop, calls=%fused_computation | loop fusion | flops 638960 | bytes 1278016 | tf_op jit(solution)/shard_map/reduce_sum | solution.py:417
  24.7 1.4 dynamic-slice_bitcast_fusion
  26.1 0.6 multiply_reduce_fusion
  27.4 23.4 %all-to-all-done.a_ref = bf16[16,704,128]{2,1,0:T(8,128)(2,1)S(1)} async-done(((bf16[16,704,128]{2,1,0:T(8,128)(2,1)}), bf16[16,704,128]{2,1,0:T(8,128)(2,1)S(1)}, u32[]{:S(2)}, u32[]{:S(2)}) %all-to-all-start) | async-done | bytes 2883616 | tf_op jit(solution)/shard_map/all_to_all | solution.py:428
  50.8 17.0 %first_up.1 = (bf16[128,88,128]{2,1,0:T(8,128)(2,1)}, bf16[13312,128]{1,0:T(8,128)(2,1)}, f32[8,128]{1,0:T(8,128)S(1)}) custom-call(s32[520]{0:T(1024)S(1)} %reshape.17.idx_ref, bf16[16,704,128]{2,1,0:T(8,128)(2,1)S(1)} %all-to-all-done.a_ref, bf16[104,5,128,128]{3,2,1,0:T(8,128)(2,1)} %refs_9_.1, f32[8,128]{1,0:T(8,128)S(1)} %broadcast_in_dim.7.mean_ref), custom_call_target="tpu_custom_call" | custom-call | flops 2181038080 | bytes 25427968 | tf_op jit(solution)/shard_map/first_up/pallas_call | solution.py:458
  67.8 10.2 %all-to-all-start.1 = ((bf16[128,88,128]{2,1,0:T(8,128)(2,1)}), bf16[128,88,128]{2,1,0:T(8,128)(2,1)}, u32[]{:S(2)}, u32[]{:S(2)}) async-start(bf16[128,88,128]{2,1,0:T(8,128)(2,1)} %get-tuple-element.20), calls=%async_computation.1 | async-start | bytes 5767168 | tf_op jit(solution)/shard_map/all_to_all | solution.py:460
  78.1 3.9 %copy.19 = bf16[16,8,1664]{2,0,1:T(8,128)(2,1)} copy(bf16[16,8,1664]{0,2,1:T(8,128)(2,1)} %bitcast.2) | data formatting | bytes 851968 | tf_op jit(solution)/shard_map/reshape | solution.py:420
  82.0 19.4 %second_up.1 = (bf16[128,88,128]{2,1,0:T(8,128)(2,1)}, f32[8,128]{1,0:T(8,128)S(1)}) custom-call(s32[520]{0:T(1024)S(1)} %reshape.17.idx_ref, bf16[16,704,128]{2,1,0:T(8,128)(2,1)} %copy-done, bf16[13312,128]{1,0:T(8,128)(2,1)S(1)} %copy-done.2, bf16[104,5,128,128]{3,2,1,0:T(8,128)(2,1)} %refs_9_.1, bf16[13312,16]{1,0:T(8,128)(2,1)} %bitcast.1.occ_rows_ref, ...), custom_call_target="tpu_custom_call" | custom-call | flops 2181038080 | bytes 25427968 | tf_op jit(solution)/shard_map/second_up/pallas_call | solution.py:483
  101.4 13.6 %all-to-all-done.1.refs_8_ = bf16[128,88,128]{2,1,0:T(8,128)(2,1)} async-done(((bf16[128,88,128]{2,1,0:T(8,128)(2,1)}), bf16[128,88,128]{2,1,0:T(8,128)(2,1)}, u32[]{:S(2)}, u32[]{:S(2)}) %all-to-all-start.1) | async-done | bytes 2883616 | tf_op jit(solution)/shard_map/all_to_all | solution.py:460
  115.1 5.8 %all-to-all-start.2 = ((bf16[128,88,128]{2,1,0:T(8,128)(2,1)}), bf16[128,88,128]{2,1,0:T(8,128)(2,1)S(1)}, u32[]{:S(2)}, u32[]{:S(2)}) async-start(bf16[128,88,128]{2,1,0:T(8,128)(2,1)} %get-tuple-element.29), calls=%async_computation.2 | async-start | bytes 5767168 | tf_op jit(solution)/shard_map/all_to_all | solution.py:486
  121.0 2.7 constant_dynamic-slice_fusion.1
  123.6 4.2 %collective-permute-start.6 = (bf16[104,1664]{1,0:T(8,128)(2,1)S(1)}, bf16[104,1664]{1,0:T(8,128)(2,1)S(1)}, u32[]{:S(2)}, u32[]{:S(2)}) collective-permute-start(bf16[104,1664]{1,0:T(8,128)(2,1)S(1)} %get-tuple-element.41), channel_id=1, source_target_pairs={{0,7},{1,0},{2,1},{3,2},{4,3},{5,4},{6,5},{7,6},{8,15},{9,8},{10,9... | collective-permute-start | bytes 1038344 | tf_op jit(solution)/shard_map/ppermute | solution.py:403
  128.2 2.8 collective-permute-start.4
  131.0 1.3 collective-permute-start.3
  132.3 1.3 collective-permute-start.2
  133.6 35.0 %collective-permute-done.6.refs_7_ = bf16[104,1664]{1,0:T(8,128)(2,1)S(1)} collective-permute-done((bf16[104,1664]{1,0:T(8,128)(2,1)S(1)}, bf16[104,1664]{1,0:T(8,128)(2,1)S(1)}, u32[]{:S(2)}, u32[]{:S(2)}) %collective-permute-start.6) | collective-permute-done | bytes 346144 | tf_op jit(solution)/shard_map/ppermute | solution.py:403
  168.7 7.6 %collective-permute-done.5.refs_6_ = bf16[104,1664]{1,0:T(8,128)(2,1)S(1)} collective-permute-done((bf16[104,1664]{1,0:T(8,128)(2,1)S(1)}, bf16[104,1664]{1,0:T(8,128)(2,1)S(1)}, u32[]{:S(2)}, u32[]{:S(2)}) %collective-permute-start.5) | collective-permute-done | bytes 346144 | tf_op jit(solution)/shard_map/ppermute | solution.py:403
  176.3 16.6 %collective-permute-start = (bf16[104,1664]{1,0:T(8,128)(2,1)S(1)}, bf16[104,1664]{1,0:T(8,128)(2,1)S(1)}, u32[]{:S(2)}, u32[]{:S(2)}) collective-permute-start(bf16[104,1664]{1,0:T(8,128)(2,1)S(1)} %get-tuple-element.47), channel_id=1, source_target_pairs={{0,1},{1,2},{2,3},{3,4},{4,5},{5,6},{6,7},{7,0},{8,9},{9,10},{10,1... | collective-permute-start | bytes 1038344 | tf_op jit(solution)/shard_map/ppermute | solution.py:403
  192.9 0.7 pad_add_fusion.idx_ref
  193.6 6.6 %collective-permute-done.refs_1_ = bf16[104,1664]{1,0:T(8,128)(2,1)S(1)} collective-permute-done((bf16[104,1664]{1,0:T(8,128)(2,1)S(1)}, bf16[104,1664]{1,0:T(8,128)(2,1)S(1)}, u32[]{:S(2)}, u32[]{:S(2)}) %collective-permute-start) | collective-permute-done | bytes 346144 | tf_op jit(solution)/shard_map/ppermute | solution.py:403
  200.3 0.7 copy-done.10
  201.0 33.0 %down.1 = (bf16[8,104,1664]{2,1,0:T(8,128)(2,1)}, f32[8,104,1664]{2,1,0:T(8,128)}, f32[8,104,1664]{2,1,0:T(8,128)}, f32[8,128]{1,0:T(8,128)}) custom-call(s32[521]{0:T(1024)} %pad_add_fusion.idx_ref, bf16[104,1664]{1,0:T(8,128)(2,1)} %get-tuple-element.48.refs_0_, bf16[104,1664]{1,0:T(8,128)(2,1)} %copy-done.10, bf16[104,1664]{1,0:T(8,128)(2,1)} %copy-done.9, ...), custom_call_target="tpu_custom_call" | custom-call | flops 2181038080 | bytes 25427968 | tf_op jit(solution)/shard_map/down/pallas_call | solution.py:492
  234.0 0.7 copy-done.3
  234.7 9.9 %joined.1 = (f32[8,104,1664]{2,1,0:T(8,128)S(1)}, f32[8,104,1664]{2,1,0:T(8,128)S(1)}, f32[128,128]{1,0:T(8,128)S(1)}) custom-call(bf16[8,104,1664]{2,1,0:T(8,128)(2,1)} %get-tuple-element.26.a_ref, f32[8,104,1664]{2,1,0:T(8,128)} %get-tuple-element.27.u_ref, f32[8,104,1664]{2,1,0:T(8,128)} %get-tuple-element.28.t_ref, ...), custom_call_target="tpu_custom_call" | custom-call | tf_op jit(solution)/shard_map/joined/pallas_call | solution.py:527
  244.6 19.4 %all_to_all.31 = f32[128,1,128]{2,1,0:T(1,128)S(1)} all-to-all(f32[128,1,128]{2,1,0:T(1,128)S(1)} %bitcast.16), channel_id=1, replica_groups=mesh['up_0'=2,'up_1'=4,'up_2'=2,'dn_0'=2,'dn_1'=4] {'up_0','up_1','up_2'..., dimensions={0} | all-to-all | bytes 131072 | tf_op jit(solution)/shard_map/all_to_all | solution.py:538
  264.0 5.8 %final.1 = (bf16[8,104,1664]{2,1,0:T(8,128)(2,1)}, f32[8,128]{1,0:T(8,128)S(1)}) custom-call(bf16[8,104,1664]{2,1,0:T(8,128)(2,1)S(1)} %copy-done.1, f32[8,104,1664]{2,1,0:T(8,128)S(1)} %get-tuple-element.32.u_ref, f32[8,104,1664]{2,1,0:T(8,128)S(1)} %get-tuple-element.33.g_ref, f32[8,128]{1,0:T(8,128)S(1)} %copy-done.3, f32[128,128]{1,0:T(8,128)S(1)} %bitcast.15), custom_call_target="tpu_custom_call" | custom-call | tf_op jit(solution)/shard_map/final/pallas_call | solution.py:539
  269.8 6.1 %all-to-all-start.4 = ((bf16[8,104,1664]{2,1,0:T(8,128)(2,1)}), bf16[8,104,1664]{2,1,0:T(8,128)(2,1)S(1)}, u32[]{:S(2)}, u32[]{:S(2)}) async-start(bf16[8,104,1664]{2,1,0:T(8,128)(2,1)} %get-tuple-element.35), calls=%async_computation.4 | async-start | bytes 5537792 | tf_op jit(solution)/shard_map/all_to_all | solution.py:549
  276.5 32.0 %all-to-all-done.4 = bf16[8,104,1664]{2,1,0:T(8,128)(2,1)S(1)} async-done(((bf16[8,104,1664]{2,1,0:T(8,128)(2,1)}), bf16[8,104,1664]{2,1,0:T(8,128)(2,1)S(1)}, u32[]{:S(2)}, u32[]{:S(2)}) %all-to-all-start.4) | async-done | bytes 2768928 | tf_op jit(solution)/shard_map/all_to_all | solution.py:549
  308.5 1.5 copy.25
  (39 shorter events, 1.4 us)
Async XLA Ops:
  7.1 5.9 %copy-start.11 = (s32[104,5]{0,1:T(8,128)S(1)}, s32[104,5]{0,1:T(8,128)}, u32[]{:S(2)}) copy-start(s32[104,5]{0,1:T(8,128)} %param.7) | copy-start | bytes 6244
  7.1 5.9 %copy-start.12 = (s32[104,5]{0,1:T(8,128)S(1)}, s32[104,5]{0,1:T(8,128)}, u32[]{:S(2)}) copy-start(s32[104,5]{0,1:T(8,128)} %param.8) | copy-start | bytes 6244
  7.1 43.7 %all-to-all-start = ((bf16[16,704,128]{2,1,0:T(8,128)(2,1)}), bf16[16,704,128]{2,1,0:T(8,128)(2,1)S(1)}, u32[]{:S(2)}, u32[]{:S(2)}) async-start(bf16[16,704,128]{2,1,0:T(8,128)(2,1)} %pack.1), calls=%async_computation | async-start | bytes 5767168 | tf_op jit(solution)/shard_map/all_to_all | solution.py:428
  50.8 17.0 %copy-start = (bf16[16,704,128]{2,1,0:T(8,128)(2,1)}, bf16[16,704,128]{2,1,0:T(8,128)(2,1)S(1)}, u32[]{:S(2)}) copy-start(bf16[16,704,128]{2,1,0:T(8,128)(2,1)S(1)} %all-to-all-done.a_ref) | copy-start | bytes 8650756
  67.8 14.2 %copy-start.2 = (bf16[13312,128]{1,0:T(8,128)(2,1)S(1)}, bf16[13312,128]{1,0:T(8,128)(2,1)}, u32[]{:S(2)}) copy-start(bf16[13312,128]{1,0:T(8,128)(2,1)} %get-tuple-element.21.flat_ref) | copy-start | bytes 10223620
  67.8 47.3 %all-to-all-start.1 = ((bf16[128,88,128]{2,1,0:T(8,128)(2,1)}), bf16[128,88,128]{2,1,0:T(8,128)(2,1)}, u32[]{:S(2)}, u32[]{:S(2)}) async-start(bf16[128,88,128]{2,1,0:T(8,128)(2,1)} %get-tuple-element.20), calls=%async_computation.1 | async-start | bytes 5767168 | tf_op jit(solution)/shard_map/all_to_all | solution.py:460
  115.1 118.9 %all-to-all-start.2 = ((bf16[128,88,128]{2,1,0:T(8,128)(2,1)}), bf16[128,88,128]{2,1,0:T(8,128)(2,1)S(1)}, u32[]{:S(2)}, u32[]{:S(2)}) async-start(bf16[128,88,128]{2,1,0:T(8,128)(2,1)} %get-tuple-element.29), calls=%async_computation.2 | async-start | bytes 5767168 | tf_op jit(solution)/shard_map/all_to_all | solution.py:486
  123.6 45.0 %collective-permute-start.6 = (bf16[104,1664]{1,0:T(8,128)(2,1)S(1)}, bf16[104,1664]{1,0:T(8,128)(2,1)S(1)}, u32[]{:S(2)}, u32[]{:S(2)}) collective-permute-start(bf16[104,1664]{1,0:T(8,128)(2,1)S(1)} %get-tuple-element.41), channel_id=1, source_target_pairs={{0,7},{1,0},{2,1},{3,2},{4,3},{5,4},{6,5},{7,6},{8,15},{9,8},{10,9... | collective-permute-start | bytes 1038344 | tf_op jit(solution)/shard_map/ppermute | solution.py:403
  127.9 48.4 %collective-permute-start.5 = (bf16[104,1664]{1,0:T(8,128)(2,1)S(1)}, bf16[104,1664]{1,0:T(8,128)(2,1)S(1)}, u32[]{:S(2)}, u32[]{:S(2)}) collective-permute-start(bf16[104,1664]{1,0:T(8,128)(2,1)S(1)} %get-tuple-element.42), channel_id=1, source_target_pairs={{0,6},{1,7},{2,0},{3,1},{4,2},{5,3},{6,4},{7,5},{8,14},{9,15},{10,... | collective-permute-start | bytes 1038344 | tf_op jit(solution)/shard_map/ppermute | solution.py:403
  128.2 65.4 %collective-permute-start.4 = (bf16[104,1664]{1,0:T(8,128)(2,1)S(1)}, bf16[104,1664]{1,0:T(8,128)(2,1)S(1)}, u32[]{:S(2)}, u32[]{:S(2)}) collective-permute-start(bf16[104,1664]{1,0:T(8,128)(2,1)S(1)} %get-tuple-element.43), channel_id=1, source_target_pairs={{0,5},{1,6},{2,7},{3,0},{4,1},{5,2},{6,3},{7,4},{8,13},{9,14},{10,... | collective-permute-start | bytes 1038344 | tf_op jit(solution)/shard_map/ppermute | solution.py:403
  131.0 62.6 %collective-permute-start.3 = (bf16[104,1664]{1,0:T(8,128)(2,1)S(1)}, bf16[104,1664]{1,0:T(8,128)(2,1)S(1)}, u32[]{:S(2)}, u32[]{:S(2)}) collective-permute-start(bf16[104,1664]{1,0:T(8,128)(2,1)S(1)} %get-tuple-element.44), channel_id=1, source_target_pairs={{0,4},{1,5},{2,6},{3,7},{4,0},{5,1},{6,2},{7,3},{8,12},{9,13},{10,... | collective-permute-start | bytes 1038344 | tf_op jit(solution)/shard_map/ppermute | solution.py:403
  132.3 61.3 %collective-permute-start.2 = (bf16[104,1664]{1,0:T(8,128)(2,1)S(1)}, bf16[104,1664]{1,0:T(8,128)(2,1)S(1)}, u32[]{:S(2)}, u32[]{:S(2)}) collective-permute-start(bf16[104,1664]{1,0:T(8,128)(2,1)S(1)} %get-tuple-element.45), channel_id=1, source_target_pairs={{0,3},{1,4},{2,5},{3,6},{4,7},{5,0},{6,1},{7,2},{8,11},{9,12},{10,... | collective-permute-start | bytes 1038344 | tf_op jit(solution)/shard_map/ppermute | solution.py:403
  168.7 31.6 %copy-start.4 = (bf16[104,1664]{1,0:T(8,128)(2,1)}, bf16[104,1664]{1,0:T(8,128)(2,1)S(1)}, u32[]{:S(2)}) copy-start(bf16[104,1664]{1,0:T(8,128)(2,1)S(1)} %collective-permute-done.6.refs_7_) | copy-start | bytes 1038340
  168.7 25.0 %collective-permute-start.1 = (bf16[104,1664]{1,0:T(8,128)(2,1)S(1)}, bf16[104,1664]{1,0:T(8,128)(2,1)S(1)}, u32[]{:S(2)}, u32[]{:S(2)}) collective-permute-start(bf16[104,1664]{1,0:T(8,128)(2,1)S(1)} %get-tuple-element.46), channel_id=1, source_target_pairs={{0,2},{1,3},{2,4},{3,5},{4,6},{5,7},{6,0},{7,1},{8,10},{9,11},{10,... | collective-permute-start | bytes 1038344 | tf_op jit(solution)/shard_map/ppermute | solution.py:403
  176.3 24.0 %copy-start.5 = (bf16[104,1664]{1,0:T(8,128)(2,1)}, bf16[104,1664]{1,0:T(8,128)(2,1)S(1)}, u32[]{:S(2)}) copy-start(bf16[104,1664]{1,0:T(8,128)(2,1)S(1)} %collective-permute-done.5.refs_6_) | copy-start | bytes 1038340
  176.3 24.0 %collective-permute-start = (bf16[104,1664]{1,0:T(8,128)(2,1)S(1)}, bf16[104,1664]{1,0:T(8,128)(2,1)S(1)}, u32[]{:S(2)}, u32[]{:S(2)}) collective-permute-start(bf16[104,1664]{1,0:T(8,128)(2,1)S(1)} %get-tuple-element.47), channel_id=1, source_target_pairs={{0,1},{1,2},{2,3},{3,4},{4,5},{5,6},{6,7},{7,0},{8,9},{9,10},{10,1... | collective-permute-start | bytes 1038344 | tf_op jit(solution)/shard_map/ppermute | solution.py:403
  193.6 6.7 %copy-start.6 = (bf16[104,1664]{1,0:T(8,128)(2,1)}, bf16[104,1664]{1,0:T(8,128)(2,1)S(1)}, u32[]{:S(2)}) copy-start(bf16[104,1664]{1,0:T(8,128)(2,1)S(1)} %collective-permute-done.4.refs_5_) | copy-start | bytes 1038340
  193.6 6.7 %copy-start.7 = (bf16[104,1664]{1,0:T(8,128)(2,1)}, bf16[104,1664]{1,0:T(8,128)(2,1)S(1)}, u32[]{:S(2)}) copy-start(bf16[104,1664]{1,0:T(8,128)(2,1)S(1)} %collective-permute-done.3.refs_4_) | copy-start | bytes 1038340
  193.6 6.7 %copy-start.8 = (bf16[104,1664]{1,0:T(8,128)(2,1)}, bf16[104,1664]{1,0:T(8,128)(2,1)S(1)}, u32[]{:S(2)}) copy-start(bf16[104,1664]{1,0:T(8,128)(2,1)S(1)} %collective-permute-done.2.refs_3_) | copy-start | bytes 1038340
  193.6 6.7 %copy-start.9 = (bf16[104,1664]{1,0:T(8,128)(2,1)}, bf16[104,1664]{1,0:T(8,128)(2,1)S(1)}, u32[]{:S(2)}) copy-start(bf16[104,1664]{1,0:T(8,128)(2,1)S(1)} %collective-permute-done.1.refs_2_) | copy-start | bytes 1038340
  200.2 0.7 copy-start.10
  234.0 0.7 copy-start.3
  234.7 29.3 %copy-start.1 = (bf16[8,104,1664]{2,1,0:T(8,128)(2,1)S(1)}, bf16[8,104,1664]{2,1,0:T(8,128)(2,1)}, u32[]{:S(2)}) copy-start(bf16[8,104,1664]{2,1,0:T(8,128)(2,1)} %get-tuple-element.26.a_ref) | copy-start | bytes 8306692
  269.8 38.7 %all-to-all-start.4 = ((bf16[8,104,1664]{2,1,0:T(8,128)(2,1)}), bf16[8,104,1664]{2,1,0:T(8,128)(2,1)S(1)}, u32[]{:S(2)}, u32[]{:S(2)}) async-start(bf16[8,104,1664]{2,1,0:T(8,128)(2,1)} %get-tuple-element.35), calls=%async_computation.4 | async-start | bytes 5537792 | tf_op jit(solution)/shard_map/all_to_all | solution.py:549

commit v4 on v3

--- a/solution.py
+++ b/solution.py
@@ -39,8 +39,8 @@
     return pltpu.with_memory_space_constraint(x, pltpu.HBM)
 
 
-def tile_spec():
-    return pl.BlockSpec((G, KT, T, T), lambda i, *_: (i, 0, 0, 0))
+def tile_specs():
+    return [pl.BlockSpec((G, 1, T, T), lambda i, *_, k=k: (i, k, 0, 0)) for k in range(KT)]
 
 
 def lane_of(shape):
@@ -55,9 +55,13 @@
     return jnp.sum(x.reshape(x.shape[0] // 8, 8, x.shape[1]), axis=0)
 
 
-def hop_nat(i, g, idx_ref, tiles_ref, xs):
-    row = i * G + g
-    left = jnp.concatenate([tiles_ref[g, k] for k in range(KT)], axis=1)
+def tile_fetch(tiles_ref, tiles, sems, k):
+    rows = pl.ds(k * G, G)
+    return pltpu.make_async_copy(tiles_ref.at[rows], tiles.at[rows], sems.at[k])
+
+
+def hop_nat(row, lefts, idx_ref, xs):
+    left = jnp.concatenate(lefts, axis=1)
     right = [xs[pl.ds(pl.multiple_of(idx_ref[row * KT + k] * T, T), T), :] for k in range(KT)]
     return jnp.dot(left, jnp.concatenate(right, axis=0), preferred_element_type=f32)
 
@@ -95,37 +99,57 @@
 S = W - WH
 
 
-def pack_kernel(a_ref, out_ref):
+PARTS = 4
+ENDS = [-(-W * NU * (k + 1) // PARTS // T) * T for k in range(PARTS)]
+
+
+def pack_kernel(a_ref, out_ref, near, sems):
+    i = pl.program_id(0)
     lane = lane_of((1, T))
+
+    def fetch(k):
+        lanes = pl.ds(ENDS[k - 1] if k else 0, ENDS[k] - (ENDS[k - 1] if k else 0))
+        return pltpu.make_async_copy(a_ref.at[:, lanes], near.at[:, lanes], sems.at[k])
 
     def cut(u, block):
         q, o = divmod(u * W, T)
         rows = slice(block * H, (block + 1) * H)
-        x = turned(a_ref[rows, q * T : (q + 1) * T].astype(f32), -o)
+        x = turned(near[rows, q * T : (q + 1) * T], -o)
         if o + W > T:
-            y = turned(a_ref[rows, (q + 1) * T : (q + 2) * T].astype(f32), -o)
+            y = turned(near[rows, (q + 1) * T : (q + 2) * T], -o)
             x = jnp.where(lane < T - o, x, y)
         return x
 
-    for u in range(NU):
-        tails = [cut(u, HEAD // H + h) for h in range(2)]
-        for block in range(HEAD // H):
-            x = cut(u, block)
-            if block < 2 * STRIPS:
-                x = with_strip(x, tails[block % 2], block // 2, lane)
-            out_ref[u, block * H : (block + 1) * H, :] = x.astype(bf16)
+    @pl.when(i == 0)
+    def _():
+        for k in range(PARTS):
+            fetch(k).start()
+
+    for k in range(PARTS):
+
+        @pl.when(i == k)
+        def _():
+            fetch(k).wait()
+            for n in range(NU // PARTS):
+                u = k * (NU // PARTS) + n
+                tails = [cut(u, HEAD // H + h) for h in range(2)]
+                for block in range(HEAD // H):
+                    x = cut(u, block)
+                    if block < 2 * STRIPS:
+                        x = with_strip(x, tails[block % 2], block // 2, lane)
+                    out_ref[n, block * H : (block + 1) * H, :] = x
 
 
 def packed(values, t, lane):
-    x = values[pl.ds(pl.multiple_of(t * W, 8), WH), :]
-    tail = values[pl.ds(pl.multiple_of(t * W + WH, 8), S), :]
+    tail = values[pl.ds(pl.multiple_of(t * W, 8), S), :]
+    x = values[pl.ds(pl.multiple_of(t * W + S, 8), WH), :]
     found = [with_strip(x[S * k : S * (k + 1)], tail, k, lane) for k in range(STRIPS)]
     return jnp.concatenate(found + [x[S * STRIPS :]], axis=0)
 
 
 def unpacked(x, lane):
     tail = from_strips([x[S * k : S * (k + 1)] for k in range(STRIPS)], lane)
-    return jnp.concatenate([x, tail], axis=0)
+    return jnp.concatenate([tail, x], axis=0)
 
 
 FREE = S * (STRIPS - 1)
@@ -135,9 +159,9 @@
 def spread(a_ref, lane, keep):
     def put(s, c):
         for block in range(HEAD // H):
-            keep(pl.multiple_of(s * ROWS + block * H, H), a_ref[s, block * H : (block + 1) * H, :].astype(f32))
+            keep(pl.multiple_of(s * ROWS + block * H, H), a_ref[s, block * H : (block + 1) * H, :])
         for h in range(2):
-            strips = [a_ref[s, (2 * k + h) * H : (2 * k + h + 1) * H, :].astype(f32) for k in range(STRIPS)]
+            strips = [a_ref[s, (2 * k + h) * H : (2 * k + h + 1) * H, :] for k in range(STRIPS)]
             keep(pl.multiple_of(s * ROWS + HEAD + h * H, H), from_strips(strips, lane))
         return c
 
@@ -145,51 +169,56 @@
 
 
 def keep_both(xs, at, n, x):
-    x = x.astype(bf16)
     xs[pl.ds(at, n), :] = x
     xs[pl.ds(NT * T + at, n), :] = -x
 
 
-def first_up_kernel(idx_ref, a_ref, tiles_ref, mean_ref, p_ref, flat_ref, sums_ref, xs, some_p, acc):
+def counted(x, lane):
+    return total_of(jnp.where(lane < W, x, 0.0))
+
+
+def first_up_kernel(idx_ref, a_ref, tiles_ref, mean_ref, p_ref, sums_ref, xs, tiles, some_p, acc, held, sems):
     i = pl.program_id(0)
     lane = lane_of((1, T))
 
     @pl.when(i == 0)
     def _():
+        for k in range(STEPS):
+            tile_fetch(tiles_ref, tiles, sems, k).start()
         acc[...] = jnp.zeros_like(acc)
-        spread(a_ref, lane, lambda at, x: keep_both(xs, at, H, jnp.where(lane < W, x, 0.0)))
+        spread(a_ref, lane, lambda at, x: keep_both(xs, at, H, x))
+
+    tile_fetch(tiles_ref, tiles, sems, i).wait()
 
     for g in range(G):
-        rows = pl.ds(pl.multiple_of((i * G + g) * T, T), T)
-        p = hop_nat(i, g, idx_ref, tiles_ref, xs).astype(bf16)
-        flat_ref[g * T : (g + 1) * T, :] = p
-        p = p.astype(f32)
+        row = i * G + g
+        rows = pl.ds(pl.multiple_of(row * T, T), T)
+        p = hop_nat(row, [tiles[row, k] for k in range(KT)], idx_ref, xs).astype(bf16).astype(f32)
         some_p[g * T : (g + 1) * T, :] = p
         a = xs[rows, :].astype(f32)
         acc[0] += fold8(p * a)
         acc[1] += fold8(a * a)
+
+    @pl.when(i == 0)
+    def _():
+        ratio = 2.0 * counted(acc[0], lane) / jnp.maximum(counted(acc[1], lane), 1e-30)
+        held[...] = jnp.broadcast_to((ratio + mean_ref[0:1, 0:1]).astype(bf16).astype(f32), held.shape)
+
+    center = held[0:1, :]
     for t in range(NU):
-        p_ref[i * NU + t] = packed(some_p, t, lane).astype(bf16)
+        x = packed(some_p, t, lane)
+        marked = jnp.where(lane >= FREE_LANE, center, x[FREE : FREE + S])
+        p_ref[t] = jnp.concatenate([x[:FREE], marked, x[FREE + S :]], axis=0).astype(bf16)
 
     @pl.when(i == STEPS - 1)
     def _():
-        energy = total_of(acc[0])
-        center = (2.0 * energy / jnp.maximum(total_of(acc[1]), 1e-30) + mean_ref[0:1, 0:1]).astype(bf16)
         sub = lax.broadcasted_iota(jnp.int32, (8, T), 0)
-        sums_ref[...] = jnp.where(sub == 0, energy, center.astype(f32))
-        fill = jnp.broadcast_to(center, (S, T))
-        free = lane_of((S, T)) >= FREE_LANE
-
-        def mark(s, c):
-            for k in range(8):
-                at = s * 8 + k
-                p_ref[at, FREE : FREE + S, :] = jnp.where(free, fill, p_ref[at, FREE : FREE + S, :])
-            return c
-
-        lax.fori_loop(0, NU * ND // 8, mark, 0)
-
-
-def second_up_kernel(idx_ref, a_ref, flat_ref, tiles_ref, occ_rows_ref, occ_cols_ref, sums_ref, q_ref, out_ref, xs, some_q, acc):
+        sums_ref[...] = jnp.where(sub == 0, counted(acc[0], lane), center)
+
+
+def second_up_kernel(idx_ref, a_ref, p_ref, *refs):
+    tiles, refs = refs[:KT], refs[KT:]
+    occ_rows_ref, occ_cols_ref, sums_ref, q_ref, out_ref, xs, some_q, flat, acc = refs
     i = pl.program_id(0)
     lane = lane_of((1, T))
 
@@ -198,18 +227,24 @@
         acc[...] = jnp.zeros_like(acc)
         center = sums_ref[1:2, :]
 
+        def open_p(s, c):
+            flat[pl.ds(pl.multiple_of(s * W, 8), W), :] = unpacked(p_ref[s], lane).astype(f32)
+            return c
+
+        lax.fori_loop(0, NU * ND, open_p, 0)
+
         def keep(at, a):
-            a = jnp.where(lane < W, a, 0.0)
+            a = a.astype(f32)
             rows = pl.ds(at, H)
             diag = coupling * jnp.dot(occ_rows_ref[rows, :], occ_cols_ref[...], preferred_element_type=f32)
             acc[...] += fold8(diag * a * a)
-            keep_both(xs, at, H, flat_ref[rows, :].astype(f32) + (diag - center) * a)
+            keep_both(xs, at, H, (flat[rows, :] + (diag - center) * a).astype(bf16))
 
         spread(a_ref, lane, keep)
-        out_ref[...] = jnp.broadcast_to(sums_ref[0:1, :] + total_of(acc[...]), out_ref.shape)
+        out_ref[...] = jnp.broadcast_to(sums_ref[0:1, :] + counted(acc[...], lane), out_ref.shape)
 
     for g in range(G):
-        some_q[g * T : (g + 1) * T, :] = hop_nat(i, g, idx_ref, tiles_ref, xs)
+        some_q[g * T : (g + 1) * T, :] = hop_nat(i * G + g, [tile_ref[g, 0] for tile_ref in tiles], idx_ref, xs)
     for t in range(NU):
         q_ref[t] = packed(some_q, t, lane).astype(bf16)
 
@@ -234,18 +269,14 @@
 def down_kernel(idx_ref, *refs):
     pieces, refs = refs[:ND], refs[ND:]
     p_ref, tiles_ref, occ_rows_ref, occ_cols_ref = refs[:4]
-    a_ref, u_ref, t_ref, sums_ref, tiles, xs, some_r, some_u, some_t, acc, sems = refs[4:]
+    a_ref, u_ref, brief_ref, t_ref, sums_ref, tiles, xs, some_r, some_u, some_t, acc, sems = refs[4:]
     i = pl.program_id(0)
     lane = lane_of((1, T))
 
-    def fetch(k):
-        rows = pl.ds(k * G, G)
-        return pltpu.make_async_copy(tiles_ref.at[rows], tiles.at[rows], sems.at[k])
-
     @pl.when(i == 0)
     def _():
         for k in range(STEPS):
-            fetch(k).start()
+            tile_fetch(tiles_ref, tiles, sems, k).start()
         acc[...] = jnp.zeros_like(acc)
         down = idx_ref[NT * KT]
         for s in range(ND):
@@ -257,12 +288,14 @@
 
     @pl.when(i < STEPS)
     def _():
-        fetch(i).wait()
+        tile_fetch(tiles_ref, tiles, sems, i).wait()
         for g in range(G):
             row = i * G + g
             r = hop_turned(row, idx_ref, tiles, xs)
             some_r[row] = r
-            acc[2] += fold8(r * xs[row].astype(f32))
+            a = xs[row]
+            a_ref[0, :, g * T : (g + 1) * T] = a
+            acc[2] += fold8(r * a.astype(f32))
 
     @pl.when(i == STEPS)
     def _():
@@ -272,12 +305,11 @@
                 for u, _end in pieces_in(o):
                     if u in rolled:
                         continue
-                    x = p_ref[u * ND + d].astype(f32)
-                    centers[u] = jnp.sum(
-                        jnp.where(lane == FREE_LANE, x[FREE : FREE + 1, :], 0.0), axis=1, keepdims=True
-                    )
+                    x = p_ref[u * ND + d]
+                    mark = x[FREE : FREE + S, :].astype(f32)[0:1, :]
+                    centers[u] = jnp.sum(jnp.where(lane == FREE_LANE, mark, 0.0), axis=1, keepdims=True)
                     rolled[u] = turned(unpacked(x, lane), u * W)
-                p = assembled(rolled, o, lane)
+                p = assembled(rolled, o, lane).astype(f32)
                 center = assembled(centers, o, lane)
                 at = d * G + o
                 a = xs[at].astype(f32)
@@ -294,16 +326,15 @@
 
         lax.fori_loop(0, ND, first, 0)
         center = total_of(acc[0]) / jnp.maximum(total_of(acc[1]), 1e-30)
-        sub = lax.broadcasted_iota(jnp.int32, (8, T), 0)
-        sums_ref[...] = jnp.where(sub == 0, center, total_of(acc[2]))
 
         def second(d, c):
             for o in range(G):
                 at = d * G + o
-                a = xs[at]
-                a_ref[d, :, o * T : (o + 1) * T] = a
                 w = some_u[at]
-                u = w - center * a.astype(f32)
+                a = xs[at].astype(f32)
+                u = w - center * a
+                acc[3] += fold8(u * u)
+                acc[4] += fold8(u * a)
                 some_u[at] = u
                 some_t[at] += center * (some_r[at] - w - u)
                 x = (u + xs[NT + at].astype(f32)).astype(bf16)
@@ -312,19 +343,39 @@
             return c
 
         lax.fori_loop(0, ND, second, 0)
+        sub = lax.broadcasted_iota(jnp.int32, (8, T), 0)
+        found = center
+        for k, n in enumerate([2, 3, 4, 1]):
+            found = jnp.where(sub == k + 1, total_of(acc[n]), found)
+        sums_ref[...] = jnp.broadcast_to(found, sums_ref.shape)
 
     @pl.when(i >= STEPS)
     def _():
         for g in range(G):
             row = (i - STEPS) * G + g
             lanes = slice(g * T, (g + 1) * T)
-            u_ref[0, :, lanes] = some_u[row]
+            u = some_u[row]
+            u_ref[0, :, lanes] = u
+            brief_ref[0, :, lanes] = u.astype(bf16)
             t_ref[0, :, lanes] = some_t[row] + hop_turned(row, idx_ref, tiles, xs)
 
 
-def joined_kernel(a_ref, u_ref, t_ref, q_ref, up_ref, down_ref, g_ref, u_out_ref, sums_ref, acc):
+def joined_kernel(*refs):
+    far_refs, (q_ref, up_ref, down_ref, g_ref, sums_ref, a_ref, u_ref, t_ref, sems, acc) = refs[:3], refs[3:]
     i = pl.program_id(0)
     lane = lane_of((1, T))
+
+    def fetch(n, d):
+        return pltpu.make_async_copy(far_refs[n].at[d], (a_ref, u_ref, t_ref)[n].at[d], sems.at[n, d])
+
+    @pl.when(i == 0)
+    def _():
+        for d in range(ND):
+            for n in range(3):
+                fetch(n, d).start()
+
+    for n in range(3):
+        fetch(n, i).wait()
 
     @pl.when(i == 0)
     def _():
@@ -334,21 +385,24 @@
     for o in range(G):
         for u, _end in pieces_in(o):
             if u not in rolled:
-                rolled[u] = turned(unpacked(q_ref[u * ND + i].astype(f32), lane), u * W)
+                rolled[u] = turned(unpacked(q_ref[u * ND + i], lane), u * W)
         lanes = slice(o * T, (o + 1) * T)
-        a = a_ref[0, :, lanes].astype(f32)
-        u = u_ref[0, :, lanes]
-        g = assembled(rolled, o, lane) + t_ref[0, :, lanes]
+        a = a_ref[i, :, lanes].astype(f32)
+        u = u_ref[i, :, lanes].astype(f32)
+        g = assembled(rolled, o, lane).astype(f32) + t_ref[i, :, lanes]
         g_ref[i, :, lanes] = g
-        u_out_ref[i, :, lanes] = u
-        for k, product in enumerate([u * u, u * a, a * a, g * g, g * u, g * a]):
+        for k, product in enumerate([g * g, g * u, g * a]):
             acc[k] += fold8(product)
 
     @pl.when(i == ND - 1)
     def _():
-        row = jnp.where(lane == 6, up_ref[0:1, :] + down_ref[1:2, :], down_ref[0:1, :])
-        for k in range(6):
-            row = jnp.where(lane == k, total_of(acc[k]), row)
+        row = down_ref[0:1, :]
+        for k, value in enumerate(
+            [down_ref[2:3, :], down_ref[3:4, :], down_ref[4:5, :]]
+            + [total_of(acc[k]) for k in range(3)]
+            + [up_ref[0:1, :] + down_ref[1:2, :]]
+        ):
+            row = jnp.where(lane == k, value, row)
         sums_ref[...] = jnp.broadcast_to(row, sums_ref.shape)
 
 
@@ -358,10 +412,11 @@
 
     @pl.when(i == 0)
     def _():
-        uu, ua, aa, gg, gu, ga, energy, center = [shared_ref[:, k : k + 1] for k in range(8)]
+        table = shared_ref[...].T
+        uu, ua, aa, gg, gu, ga, energy, center = [table[k : k + 1, :] for k in range(8)]
 
         def total(x):
-            return jnp.sum(x, axis=0, keepdims=True)
+            return jnp.sum(x, axis=1, keepdims=True)
 
         norm = total(aa)
         scale2 = 1.0 / jnp.maximum(norm, 1.0)
@@ -410,6 +465,7 @@
     index = (tile_columns + NT * tile_signs).astype(jnp.int32).reshape(-1)
     up = lax.axis_index(UP)
     down = lax.axis_index(DN)
+    index = jnp.concatenate([index, down.astype(jnp.int32)[None]])
     occ = occupation.astype(bf16)
     occ_rows = occ.T
     a_cols = lax.dynamic_slice_in_dim(occ, down * cols + up * W, W, 1)
@@ -421,8 +477,12 @@
 
     parts = pl.pallas_call(
         pack_kernel,
+        grid=(PARTS,),
+        in_specs=[pl.BlockSpec(memory_space=pl.ANY)],
+        out_specs=pl.BlockSpec((NU // PARTS, HEAD, T), lambda i: (i, 0, 0)),
         out_shape=pltpu.HBM((NU, HEAD, T), bf16),
-        compiler_params=pltpu.CompilerParams(vmem_limit_bytes=24 * MIB),
+        scratch_shapes=[pltpu.VMEM(start_vector.shape, bf16), pltpu.SemaphoreType.DMA((PARTS,))],
+        compiler_params=params(24),
         name="pack",
     )(far(start_vector))
     a_up = lax.all_to_all(parts, UP, 0, 0, tiled=True)
@@ -442,20 +502,29 @@
         grid_spec=pltpu.PrefetchScalarGridSpec(
             num_scalar_prefetch=1,
             grid=(STEPS,),
-            in_specs=[whole((NU, HEAD, T)), tile_spec(), whole((8, T))],
-            out_specs=[whole(packs), pl.BlockSpec((G * T, T), lambda i, *_: (i, 0)), whole((8, T))],
-            scratch_shapes=[xs_tall, some, pltpu.VMEM((2, 8, T), f32)],
+            in_specs=[whole((NU, HEAD, T)), pl.BlockSpec(memory_space=pl.ANY), whole((8, T))],
+            out_specs=[
+                pl.BlockSpec((NU, WH, T), lambda i, *_: (i, 0, 0)),
+                whole((8, T)),
+            ],
+            scratch_shapes=[
+                xs_tall,
+                pltpu.VMEM((NT, KT, T, T), bf16),
+                some,
+                pltpu.VMEM((2, 8, T), f32),
+                pltpu.VMEM((8, T), f32),
+                pltpu.SemaphoreType.DMA((STEPS,)),
+            ],
         ),
         out_shape=[
             pltpu.HBM(packs, bf16),
-            pltpu.HBM(tall, bf16),
             jax.ShapeDtypeStruct((8, T), f32),
         ],
-        compiler_params=params(28),
+        compiler_params=params(44),
         cost_estimate=cost,
         name="first_up",
     )
-    p, flat, sums = first_up(index, a_up, far(hop_tiles), mean)
+    p, sums = first_up(index, a_up, far(hop_tiles), mean)
 
     p_dn = lax.all_to_all(p, ALL, 0, 0, tiled=True)
 
@@ -466,21 +535,21 @@
             grid=(STEPS,),
             in_specs=[
                 whole((NU, HEAD, T)),
-                whole(tall),
-                tile_spec(),
+                whole(packs),
+                *tile_specs(),
                 whole(occ_rows.shape),
                 whole(a_cols.shape),
                 whole((8, T)),
             ],
             out_specs=[pl.BlockSpec((NU, WH, T), lambda i, *_: (i, 0, 0)), whole((8, T))],
-            scratch_shapes=[xs_tall, some, pltpu.VMEM((8, T), f32)],
+            scratch_shapes=[xs_tall, some, pltpu.VMEM(tall, f32), pltpu.VMEM((8, T), f32)],
         ),
         out_shape=[pltpu.HBM(packs, bf16), jax.ShapeDtypeStruct((8, T), f32)],
-        compiler_params=params(32),
+        compiler_params=params(40),
         cost_estimate=cost,
         name="second_up",
     )
-    q, up_dots = second_up(index, far(a_up), flat, far(hop_tiles), far(occ_rows), a_cols, sums)
+    q, up_dots = second_up(index, far(a_up), far(p), *[far(hop_tiles)] * KT, far(occ_rows), a_cols, sums)
 
     p_dn, q, b_cols = lax.optimization_barrier((p_dn, q, b_cols))
     q_dn = lax.all_to_all(q, ALL, 0, 0, tiled=True)
@@ -489,7 +558,8 @@
     kept = pltpu.VMEM(wide, f32)
     cut = pltpu.VMEM((NT, W, T), f32)
     late = pl.BlockSpec((1, W, cols), lambda i, *_: (jnp.maximum(i - STEPS, 0), 0, 0))
-    a_dn, u, t, down_dots = pl.pallas_call(
+    early = pl.BlockSpec((1, W, cols), lambda i, *_: (jnp.minimum(i, STEPS - 1), 0, 0))
+    a_dn, u, brief_u, t, down_dots = pl.pallas_call(
         down_kernel,
         grid_spec=pltpu.PrefetchScalarGridSpec(
             num_scalar_prefetch=1,
@@ -501,39 +571,46 @@
                 whole(b_rows.shape),
                 whole(b_cols.shape),
             ],
-            out_specs=[whole(wide), late, late, whole((8, T))],
+            out_specs=[early, late, late, late, whole((8, T))],
             scratch_shapes=[
                 pltpu.VMEM((NT, KT, T, T), bf16),
                 pltpu.VMEM((2 * NT, W, T), bf16),
                 cut,
                 cut,
                 cut,
-                pltpu.VMEM((3, 8, T), f32),
+                pltpu.VMEM((5, 8, T), f32),
                 pltpu.SemaphoreType.DMA((STEPS,)),
             ],
         ),
         out_shape=[
             pltpu.HBM(wide, bf16),
             pltpu.HBM(wide, f32),
+            pltpu.HBM(wide, bf16),
             pltpu.HBM(wide, f32),
             jax.ShapeDtypeStruct((8, T), f32),
         ],
         compiler_params=params(56),
         cost_estimate=cost,
         name="down",
-    )(jnp.concatenate([index, down[None]]), *[far(x) for x in pieces], p_dn, far(hop_tiles), b_rows, b_cols)
+    )(index, *[far(x) for x in pieces], p_dn, far(hop_tiles), b_rows, b_cols)
 
     block = pl.BlockSpec((1, W, cols), lambda i, *_: (i, 0, 0))
-    g, u, partial = pl.pallas_call(
+    g, partial = pl.pallas_call(
         joined_kernel,
         grid=(ND,),
-        in_specs=[block, block, block, whole(packs), whole((8, T)), whole((8, T))],
-        out_specs=[near, near, whole((NU * ND, T))],
-        out_shape=[kept, kept, jax.ShapeDtypeStruct((NU * ND, T), f32)],
-        scratch_shapes=[pltpu.VMEM((6, 8, T), f32)],
-        compiler_params=params(20),
+        in_specs=[pl.BlockSpec(memory_space=pl.ANY)] * 3 + [whole(packs), whole((8, T)), whole((8, T))],
+        out_specs=[near, whole((NU * ND, T))],
+        out_shape=[kept, jax.ShapeDtypeStruct((NU * ND, T), f32)],
+        scratch_shapes=[
+            pltpu.VMEM(wide, bf16),
+            pltpu.VMEM(wide, bf16),
+            pltpu.VMEM(wide, f32),
+            pltpu.SemaphoreType.DMA((3, ND)),
+            pltpu.VMEM((3, 8, T), f32),
+        ],
+        compiler_params=params(24),
         name="joined",
-    )(far(a_dn), far(u), far(t), q_dn, up_dots, down_dots)
+    )(far(a_dn), far(brief_u), far(t), q_dn, far(up_dots), far(down_dots))
 
     shared = lax.all_to_all(partial, ALL, 0, 0, tiled=True)
     v, scalars = pl.pallas_call(
@@ -545,7 +622,7 @@
         scratch_shapes=[pltpu.VMEM((8, T), f32)],
         compiler_params=params(16),
         name="final",
-    )(a_dn, u, g, down_dots, shared)
+    )(a_dn, u, g, far(down_dots), shared)
     final = lax.all_to_all(v, DN, 0, 0, tiled=True).reshape(rows, cols)
     return final, scalars[0, 0:2], scalars[0, 2:4]
 

time: 312 us -> 303 us (0.971)
  waiting for transfers between devices: 118 us -> 108 us
    all_to_all x1, waiting for transfers between devices: 13.6 us -> 2.99 us  [body(): p_dn = lax.all_to_all(p, ALL, 0, 0, tiled=True)]
    unnamed x29 -> x35, local copies, waits for them, and re-layouts: 8.16 us -> 9.92 us
  transfers between devices with their start and end apart: 11 -> 11, of which waited for: 6 -> 6; matrix products, arithmetic and copies ran while one was open for 7% -> 6% of each run, Pallas kernels for 17% -> 21%
where the time goes in v4:
time: 303 us; the launch traced here: 301 us
  waiting for transfers between devices  108 us (36%)
  Pallas kernels  92.4 us (30%)
  starting transfers between devices  55.5 us (18%)
  blocking collectives  19.4 us (6%)
  local copies, waits for them, and re-layouts  18 us (6%)
  other arithmetic  5.88 us (2%)
    ppermute x7, waiting for transfers between devices, swapped_down(): piece = lax.ppermute(piece, DN, [(k, (k + s) % ND) for k in range(ND)])  50 us
    pallas_call x1, Pallas kernels, body(): pl.pallas_call(down_kernel, grid_spec=pltpu.PrefetchScalarGridSpec(num_sc...  33.6 us
    all_to_all x1, waiting for transfers between devices, body(): final = lax.all_to_all(v, DN, 0, 0, tiled=True).reshape(rows, cols)  32 us
    pallas_call x1, Pallas kernels, body(): second_up(index, far(a_up), far(p), *[far(hop_tiles)] * KT, far(occ_rows)...  29.4 us
    ppermute x7, starting transfers between devices, swapped_down(): piece = lax.ppermute(piece, DN, [(k, (k + s) % ND) for k in range(ND)])  26.6 us
    all_to_all x1, waiting for transfers between devices, body(): a_up = lax.all_to_all(parts, UP, 0, 0, tiled=True)  23.4 us
    all_to_all x1, blocking collectives, body(): shared = lax.all_to_all(partial, ALL, 0, 0, tiled=True)  19.4 us
    pallas_call x1, Pallas kernels, body(): p, sums = first_up(index, a_up, far(hop_tiles), mean)  11.4 us
  transfers between devices with their start and end apart: 11, of which 6 were waited for; matrix products, arithmetic and copies ran while one was open for 6% of the time, Pallas kernels for 21%

profile of v4, /device:TPU:24, one launch (start us, length us, event | category | flops | bytes accessed | tf_op | source)
XLA Modules:
  0.0 301.1 jit_solution(15111159721801204828)
XLA Ops:
  0.6 5.3 %pack.1 = bf16[16,704,128]{2,1,0:T(8,128)(2,1)} custom-call(bf16[832,1664]{1,0:T(8,128)(2,1)} %a_ref.1), custom_call_target="tpu_custom_call" | custom-call | tf_op jit(solution)/shard_map/pack/pallas_call | solution.py:478
  5.9 5.8 %all-to-all-start = ((bf16[16,704,128]{2,1,0:T(8,128)(2,1)}), bf16[16,704,128]{2,1,0:T(8,128)(2,1)S(1)}, u32[]{:S(2)}, u32[]{:S(2)}) async-start(bf16[16,704,128]{2,1,0:T(8,128)(2,1)} %pack.1), calls=%async_computation | async-start | bytes 5767168 | tf_op jit(solution)/shard_map/all_to_all | solution.py:488
  12.1 5.2 %copy.16 = s32[16,13312]{0,1:T(8,128)} copy(s32[16,13312]{1,0:T(8,128)} %param.9) | data formatting | bytes 1703936 | tf_op args[4]
  17.3 5.2 %convert_reduce_fusion = (f32[16]{0:T(128)S(1)}, bf16[16,13312]{0,1:T(8,128)(2,1)S(1)}) fusion(s32[16,13312]{0,1:T(8,128)} %copy.16), kind=kLoop, calls=%fused_computation | loop fusion | flops 638960 | bytes 1278016 | tf_op jit(solution)/shard_map/reduce_sum | solution.py:473
  22.4 1.8 copy-done.4
  24.2 0.6 dynamic-slice_bitcast_fusion
  24.9 0.6 multiply_reduce_fusion
  26.2 23.4 %all-to-all-done.a_ref = bf16[16,704,128]{2,1,0:T(8,128)(2,1)S(1)} async-done(((bf16[16,704,128]{2,1,0:T(8,128)(2,1)}), bf16[16,704,128]{2,1,0:T(8,128)(2,1)S(1)}, u32[]{:S(2)}, u32[]{:S(2)}) %all-to-all-start) | async-done | bytes 2883616 | tf_op jit(solution)/shard_map/all_to_all | solution.py:488
  49.6 11.4 %first_up.1 = (bf16[128,88,128]{2,1,0:T(8,128)(2,1)}, f32[8,128]{1,0:T(8,128)S(1)}) custom-call(s32[521]{0:T(1024)S(1)} %pad_add_fusion.idx_ref, bf16[16,704,128]{2,1,0:T(8,128)(2,1)S(1)} %all-to-all-done.a_ref, bf16[104,5,128,128]{3,2,1,0:T(8,128)(2,1)} %refs_9_.1, f32[8,128]{1,0:T(8,128)S(1)} %broadcast_in_dim.7.mean_ref), custom_call_target="tpu_custom_call" | custom-call | flops 2181038080 | bytes 25427968 | tf_op jit(solution)/shard_map/first_up/pallas_call | solution.py:527
  60.9 10.2 %all-to-all-start.1 = ((bf16[128,88,128]{2,1,0:T(8,128)(2,1)}), bf16[128,88,128]{2,1,0:T(8,128)(2,1)}, u32[]{:S(2)}, u32[]{:S(2)}) async-start(bf16[128,88,128]{2,1,0:T(8,128)(2,1)} %get-tuple-element.19.p_ref), calls=%async_computation.1 | async-start | bytes 5767168 | tf_op jit(solution)/shard_map/all_to_all | solution.py:529
  71.2 3.9 %copy.19 = bf16[16,8,1664]{2,0,1:T(8,128)(2,1)} copy(bf16[16,8,1664]{0,2,1:T(8,128)(2,1)} %bitcast.19) | data formatting | bytes 851968 | tf_op jit(solution)/shard_map/reshape | solution.py:476
  75.2 29.4 %second_up.1 = (bf16[128,88,128]{2,1,0:T(8,128)(2,1)}, f32[8,128]{1,0:T(8,128)S(1)}) custom-call(s32[521]{0:T(1024)S(1)} %pad_add_fusion.idx_ref, bf16[16,704,128]{2,1,0:T(8,128)(2,1)} %copy-done, bf16[128,88,128]{2,1,0:T(8,128)(2,1)} %get-tuple-element.19.p_ref, bf16[104,5,128,128]{3,2,1,0:T(8,128)(2,1)} %refs_9_.1, bf16[104,5,128,128]{3,2,1,0:T(8,128)(2,1)} %refs_9_.1, ...), custom_call_target="tpu_custom_call" | custom-call | flops 2181038080 | bytes 25427968 | tf_op jit(solution)/shard_map/second_up/pallas_call | solution.py:552
  104.6 0.6 copy-done.3
  105.2 3.0 all-to-all-done.1.refs_8_
  108.2 6.8 %all-to-all-start.2 = ((bf16[128,88,128]{2,1,0:T(8,128)(2,1)}), bf16[128,88,128]{2,1,0:T(8,128)(2,1)S(1)}, u32[]{:S(2)}, u32[]{:S(2)}) async-start(bf16[128,88,128]{2,1,0:T(8,128)(2,1)} %get-tuple-element.28), calls=%async_computation.2 | async-start | bytes 5767168 | tf_op jit(solution)/shard_map/all_to_all | solution.py:555
  115.1 2.7 constant_dynamic-slice_fusion.1
  117.8 4.2 %collective-permute-start.6 = (bf16[104,1664]{1,0:T(8,128)(2,1)S(1)}, bf16[104,1664]{1,0:T(8,128)(2,1)S(1)}, u32[]{:S(2)}, u32[]{:S(2)}) collective-permute-start(bf16[104,1664]{1,0:T(8,128)(2,1)S(1)} %get-tuple-element.39), channel_id=1, source_target_pairs={{0,7},{1,0},{2,1},{3,2},{4,3},{5,4},{6,5},{7,6},{8,15},{9,8},{10,9... | collective-permute-start | bytes 1038344 | tf_op jit(solution)/shard_map/ppermute | solution.py:458
  122.3 2.8 collective-permute-start.4
  125.1 1.3 collective-permute-start.3
  126.4 1.3 collective-permute-start.2
  127.8 35.0 %collective-permute-done.6.refs_7_ = bf16[104,1664]{1,0:T(8,128)(2,1)S(1)} collective-permute-done((bf16[104,1664]{1,0:T(8,128)(2,1)S(1)}, bf16[104,1664]{1,0:T(8,128)(2,1)S(1)}, u32[]{:S(2)}, u32[]{:S(2)}) %collective-permute-start.6) | collective-permute-done | bytes 346144 | tf_op jit(solution)/shard_map/ppermute | solution.py:458
  162.8 7.6 %collective-permute-done.5.refs_6_ = bf16[104,1664]{1,0:T(8,128)(2,1)S(1)} collective-permute-done((bf16[104,1664]{1,0:T(8,128)(2,1)S(1)}, bf16[104,1664]{1,0:T(8,128)(2,1)S(1)}, u32[]{:S(2)}, u32[]{:S(2)}) %collective-permute-start.5) | collective-permute-done | bytes 346144 | tf_op jit(solution)/shard_map/ppermute | solution.py:458
  170.4 16.6 %collective-permute-start = (bf16[104,1664]{1,0:T(8,128)(2,1)S(1)}, bf16[104,1664]{1,0:T(8,128)(2,1)S(1)}, u32[]{:S(2)}, u32[]{:S(2)}) collective-permute-start(bf16[104,1664]{1,0:T(8,128)(2,1)S(1)} %get-tuple-element.45), channel_id=1, source_target_pairs={{0,1},{1,2},{2,3},{3,4},{4,5},{5,6},{6,7},{7,0},{8,9},{9,10},{10,1... | collective-permute-start | bytes 1038344 | tf_op jit(solution)/shard_map/ppermute | solution.py:458
  187.1 7.3 %collective-permute-done.refs_1_ = bf16[104,1664]{1,0:T(8,128)(2,1)S(1)} collective-permute-done((bf16[104,1664]{1,0:T(8,128)(2,1)S(1)}, bf16[104,1664]{1,0:T(8,128)(2,1)S(1)}, u32[]{:S(2)}, u32[]{:S(2)}) %collective-permute-start) | collective-permute-done | bytes 346144 | tf_op jit(solution)/shard_map/ppermute | solution.py:458
  194.4 0.7 copy-done.11
  195.1 33.6 %down.1 = (bf16[8,104,1664]{2,1,0:T(8,128)(2,1)}, f32[8,104,1664]{2,1,0:T(8,128)}, bf16[8,104,1664]{2,1,0:T(8,128)(2,1)}, f32[8,104,1664]{2,1,0:T(8,128)}, f32[8,128]{1,0:T(8,128)}) custom-call(s32[521]{0:T(1024)} %copy-done.2, bf16[104,1664]{1,0:T(8,128)(2,1)} %get-tuple-element.46.refs_0_, bf16[104,1664]{1,0:T(8,128)(2,1)} %copy-done.11, ...), custom_call_target="tpu_custom_call" | custom-call | flops 2181038080 | bytes 25427968 | tf_op jit(solution)/shard_map/down/pallas_call | solution.py:562
  228.8 6.6 %joined.1 = (f32[8,104,1664]{2,1,0:T(8,128)S(1)}, f32[128,128]{1,0:T(8,128)S(1)}) custom-call(bf16[8,104,1664]{2,1,0:T(8,128)(2,1)} %get-tuple-element.24.refs_0_.a_ref, bf16[8,104,1664]{2,1,0:T(8,128)(2,1)} %get-tuple-element.26.refs_1_, f32[8,104,1664]{2,1,0:T(8,128)} %get-tuple-element.27.refs_2_, bf16[128,88,128]{2,1,0:T(8,128)(2,1)S(1)} %all-to-all-done.2.refs_3_, ...), custom_call_target="tpu_custom_call" | custom-call | tf_op jit(solution)/shard_map/joined/pallas_call | solution.py:598
  235.4 19.4 %all_to_all.31 = f32[128,1,128]{2,1,0:T(1,128)S(1)} all-to-all(f32[128,1,128]{2,1,0:T(1,128)S(1)} %bitcast.18), channel_id=1, replica_groups=mesh['up_0'=2,'up_1'=4,'up_2'=2,'dn_0'=2,'dn_1'=4] {'up_0','up_1','up_2'..., dimensions={0} | all-to-all | bytes 131072 | tf_op jit(solution)/shard_map/all_to_all | solution.py:615
  254.8 6.1 %final.1 = (bf16[8,104,1664]{2,1,0:T(8,128)(2,1)}, f32[8,128]{1,0:T(8,128)S(1)}) custom-call(bf16[8,104,1664]{2,1,0:T(8,128)(2,1)S(1)} %copy-done.1, f32[8,104,1664]{2,1,0:T(8,128)S(1)} %bitcast.16, f32[8,104,1664]{2,1,0:T(8,128)S(1)} %get-tuple-element.31.g_ref, f32[8,128]{1,0:T(8,128)} %get-tuple-element.30.refs_5_.center_ref, f32[128,128]{1,0:T(8,128)S(1)} %bitcast.17), custom_call_target="tpu_custom_call" | custom-call | tf_op jit(solution)/shard_map/final/pallas_call | solution.py:616
  260.8 6.1 %all-to-all-start.4 = ((bf16[8,104,1664]{2,1,0:T(8,128)(2,1)}), bf16[8,104,1664]{2,1,0:T(8,128)(2,1)S(1)}, u32[]{:S(2)}, u32[]{:S(2)}) async-start(bf16[8,104,1664]{2,1,0:T(8,128)(2,1)} %get-tuple-element.33), calls=%async_computation.4 | async-start | bytes 5537792 | tf_op jit(solution)/shard_map/all_to_all | solution.py:626
  267.5 32.0 %all-to-all-done.4 = bf16[8,104,1664]{2,1,0:T(8,128)(2,1)S(1)} async-done(((bf16[8,104,1664]{2,1,0:T(8,128)(2,1)}), bf16[8,104,1664]{2,1,0:T(8,128)(2,1)S(1)}, u32[]{:S(2)}, u32[]{:S(2)}) %all-to-all-start.4) | async-done | bytes 2768928 | tf_op jit(solution)/shard_map/all_to_all | solution.py:626
  299.5 1.5 copy.25
  (46 shorter events, 1.4 us)
Async XLA Ops:
  5.9 5.8 %copy-start.12 = (s32[104,5]{0,1:T(8,128)S(1)}, s32[104,5]{0,1:T(8,128)}, u32[]{:S(2)}) copy-start(s32[104,5]{0,1:T(8,128)} %param.7) | copy-start | bytes 6244
  5.9 5.8 %copy-start.13 = (s32[104,5]{0,1:T(8,128)S(1)}, s32[104,5]{0,1:T(8,128)}, u32[]{:S(2)}) copy-start(s32[104,5]{0,1:T(8,128)} %param.8) | copy-start | bytes 6244
  5.9 43.6 %all-to-all-start = ((bf16[16,704,128]{2,1,0:T(8,128)(2,1)}), bf16[16,704,128]{2,1,0:T(8,128)(2,1)S(1)}, u32[]{:S(2)}, u32[]{:S(2)}) async-start(bf16[16,704,128]{2,1,0:T(8,128)(2,1)} %pack.1), calls=%async_computation | async-start | bytes 5767168 | tf_op jit(solution)/shard_map/all_to_all | solution.py:488
  22.4 1.8 copy-start.4
  26.2 49.0 %copy-start.2 = (s32[521]{0:T(1024)}, s32[521]{0:T(1024)S(1)}, u32[]{:S(2)}) copy-start(s32[521]{0:T(1024)S(1)} %pad_add_fusion.idx_ref) | copy-start | bytes 6256
  49.5 11.4 %copy-start = (bf16[16,704,128]{2,1,0:T(8,128)(2,1)}, bf16[16,704,128]{2,1,0:T(8,128)(2,1)S(1)}, u32[]{:S(2)}) copy-start(bf16[16,704,128]{2,1,0:T(8,128)(2,1)S(1)} %all-to-all-done.a_ref) | copy-start | bytes 8650756
  60.9 47.3 %all-to-all-start.1 = ((bf16[128,88,128]{2,1,0:T(8,128)(2,1)}), bf16[128,88,128]{2,1,0:T(8,128)(2,1)}, u32[]{:S(2)}, u32[]{:S(2)}) async-start(bf16[128,88,128]{2,1,0:T(8,128)(2,1)} %get-tuple-element.19.p_ref), calls=%async_computation.1 | async-start | bytes 5767168 | tf_op jit(solution)/shard_map/all_to_all | solution.py:529
  104.6 0.6 copy-start.3
  108.2 120.5 %all-to-all-start.2 = ((bf16[128,88,128]{2,1,0:T(8,128)(2,1)}), bf16[128,88,128]{2,1,0:T(8,128)(2,1)S(1)}, u32[]{:S(2)}, u32[]{:S(2)}) async-start(bf16[128,88,128]{2,1,0:T(8,128)(2,1)} %get-tuple-element.28), calls=%async_computation.2 | async-start | bytes 5767168 | tf_op jit(solution)/shard_map/all_to_all | solution.py:555
  117.8 45.0 %collective-permute-start.6 = (bf16[104,1664]{1,0:T(8,128)(2,1)S(1)}, bf16[104,1664]{1,0:T(8,128)(2,1)S(1)}, u32[]{:S(2)}, u32[]{:S(2)}) collective-permute-start(bf16[104,1664]{1,0:T(8,128)(2,1)S(1)} %get-tuple-element.39), channel_id=1, source_target_pairs={{0,7},{1,0},{2,1},{3,2},{4,3},{5,4},{6,5},{7,6},{8,15},{9,8},{10,9... | collective-permute-start | bytes 1038344 | tf_op jit(solution)/shard_map/ppermute | solution.py:458
  122.0 48.4 %collective-permute-start.5 = (bf16[104,1664]{1,0:T(8,128)(2,1)S(1)}, bf16[104,1664]{1,0:T(8,128)(2,1)S(1)}, u32[]{:S(2)}, u32[]{:S(2)}) collective-permute-start(bf16[104,1664]{1,0:T(8,128)(2,1)S(1)} %get-tuple-element.40), channel_id=1, source_target_pairs={{0,6},{1,7},{2,0},{3,1},{4,2},{5,3},{6,4},{7,5},{8,14},{9,15},{10,... | collective-permute-start | bytes 1038344 | tf_op jit(solution)/shard_map/ppermute | solution.py:458
  122.3 64.7 %collective-permute-start.4 = (bf16[104,1664]{1,0:T(8,128)(2,1)S(1)}, bf16[104,1664]{1,0:T(8,128)(2,1)S(1)}, u32[]{:S(2)}, u32[]{:S(2)}) collective-permute-start(bf16[104,1664]{1,0:T(8,128)(2,1)S(1)} %get-tuple-element.41), channel_id=1, source_target_pairs={{0,5},{1,6},{2,7},{3,0},{4,1},{5,2},{6,3},{7,4},{8,13},{9,14},{10,... | collective-permute-start | bytes 1038344 | tf_op jit(solution)/shard_map/ppermute | solution.py:458
  125.1 62.0 %collective-permute-start.3 = (bf16[104,1664]{1,0:T(8,128)(2,1)S(1)}, bf16[104,1664]{1,0:T(8,128)(2,1)S(1)}, u32[]{:S(2)}, u32[]{:S(2)}) collective-permute-start(bf16[104,1664]{1,0:T(8,128)(2,1)S(1)} %get-tuple-element.42), channel_id=1, source_target_pairs={{0,4},{1,5},{2,6},{3,7},{4,0},{5,1},{6,2},{7,3},{8,12},{9,13},{10,... | collective-permute-start | bytes 1038344 | tf_op jit(solution)/shard_map/ppermute | solution.py:458
  126.4 60.7 %collective-permute-start.2 = (bf16[104,1664]{1,0:T(8,128)(2,1)S(1)}, bf16[104,1664]{1,0:T(8,128)(2,1)S(1)}, u32[]{:S(2)}, u32[]{:S(2)}) collective-permute-start(bf16[104,1664]{1,0:T(8,128)(2,1)S(1)} %get-tuple-element.43), channel_id=1, source_target_pairs={{0,3},{1,4},{2,5},{3,6},{4,7},{5,0},{6,1},{7,2},{8,11},{9,12},{10,... | collective-permute-start | bytes 1038344 | tf_op jit(solution)/shard_map/ppermute | solution.py:458
  162.8 31.6 %copy-start.5 = (bf16[104,1664]{1,0:T(8,128)(2,1)}, bf16[104,1664]{1,0:T(8,128)(2,1)S(1)}, u32[]{:S(2)}) copy-start(bf16[104,1664]{1,0:T(8,128)(2,1)S(1)} %collective-permute-done.6.refs_7_) | copy-start | bytes 1038340
  162.8 24.3 %collective-permute-start.1 = (bf16[104,1664]{1,0:T(8,128)(2,1)S(1)}, bf16[104,1664]{1,0:T(8,128)(2,1)S(1)}, u32[]{:S(2)}, u32[]{:S(2)}) collective-permute-start(bf16[104,1664]{1,0:T(8,128)(2,1)S(1)} %get-tuple-element.44), channel_id=1, source_target_pairs={{0,2},{1,3},{2,4},{3,5},{4,6},{5,7},{6,0},{7,1},{8,10},{9,11},{10,... | collective-permute-start | bytes 1038344 | tf_op jit(solution)/shard_map/ppermute | solution.py:458
  170.4 24.0 %copy-start.6 = (bf16[104,1664]{1,0:T(8,128)(2,1)}, bf16[104,1664]{1,0:T(8,128)(2,1)S(1)}, u32[]{:S(2)}) copy-start(bf16[104,1664]{1,0:T(8,128)(2,1)S(1)} %collective-permute-done.5.refs_6_) | copy-start | bytes 1038340
  170.4 23.9 %collective-permute-start = (bf16[104,1664]{1,0:T(8,128)(2,1)S(1)}, bf16[104,1664]{1,0:T(8,128)(2,1)S(1)}, u32[]{:S(2)}, u32[]{:S(2)}) collective-permute-start(bf16[104,1664]{1,0:T(8,128)(2,1)S(1)} %get-tuple-element.45), channel_id=1, source_target_pairs={{0,1},{1,2},{2,3},{3,4},{4,5},{5,6},{6,7},{7,0},{8,9},{9,10},{10,1... | collective-permute-start | bytes 1038344 | tf_op jit(solution)/shard_map/ppermute | solution.py:458
  187.0 7.3 %copy-start.7 = (bf16[104,1664]{1,0:T(8,128)(2,1)}, bf16[104,1664]{1,0:T(8,128)(2,1)S(1)}, u32[]{:S(2)}) copy-start(bf16[104,1664]{1,0:T(8,128)(2,1)S(1)} %collective-permute-done.4.refs_5_) | copy-start | bytes 1038340
  187.1 7.3 %copy-start.8 = (bf16[104,1664]{1,0:T(8,128)(2,1)}, bf16[104,1664]{1,0:T(8,128)(2,1)S(1)}, u32[]{:S(2)}) copy-start(bf16[104,1664]{1,0:T(8,128)(2,1)S(1)} %collective-permute-done.3.refs_4_) | copy-start | bytes 1038340
  187.1 7.3 %copy-start.9 = (bf16[104,1664]{1,0:T(8,128)(2,1)}, bf16[104,1664]{1,0:T(8,128)(2,1)S(1)}, u32[]{:S(2)}) copy-start(bf16[104,1664]{1,0:T(8,128)(2,1)S(1)} %collective-permute-done.2.refs_3_) | copy-start | bytes 1038340
  187.1 7.3 %copy-start.10 = (bf16[104,1664]{1,0:T(8,128)(2,1)}, bf16[104,1664]{1,0:T(8,128)(2,1)S(1)}, u32[]{:S(2)}) copy-start(bf16[104,1664]{1,0:T(8,128)(2,1)S(1)} %collective-permute-done.1.refs_2_) | copy-start | bytes 1038340
  194.4 0.7 copy-start.11
  228.7 26.0 %slice-start = ((s8[5537792]{0:T(1024)(128)(4,1)}), s8[4194304]{0:T(1024)(128)(4,1)S(1)}, s32[]{:S(2)}) async-start(s8[5537792]{0:T(1024)(128)(4,1)} %bitcast.15), calls=%async_computation.5 | async-start | bytes 8388608
  228.8 26.0 %copy-start.1 = (bf16[8,104,1664]{2,1,0:T(8,128)(2,1)S(1)}, bf16[8,104,1664]{2,1,0:T(8,128)(2,1)}, u32[]{:S(2)}) copy-start(bf16[8,104,1664]{2,1,0:T(8,128)(2,1)} %get-tuple-element.24.refs_0_.a_ref) | copy-start | bytes 8306692
  228.8 26.0 %slice-start.1 = ((s8[5537792]{0:T(1024)(128)(4,1)}), s8[1343488]{0:T(1024)(128)(4,1)S(1)}, s32[]{:S(2)}) async-start(s8[5537792]{0:T(1024)(128)(4,1)} %bitcast.15), calls=%async_computation.6 | async-start | bytes 2686976
  260.8 38.7 %all-to-all-start.4 = ((bf16[8,104,1664]{2,1,0:T(8,128)(2,1)}), bf16[8,104,1664]{2,1,0:T(8,128)(2,1)S(1)}, u32[]{:S(2)}, u32[]{:S(2)}) async-start(bf16[8,104,1664]{2,1,0:T(8,128)(2,1)} %get-tuple-element.33), calls=%async_computation.4 | async-start | bytes 5537792 | tf_op jit(solution)/shard_map/all_to_all | solution.py:626

commit v5 on v4

--- a/solution.py
+++ b/solution.py
@@ -23,6 +23,7 @@
 W = 104
 NU = 16
 ND = 8
+NZ = 4
 MIB = 1024 * 1024
 
 
@@ -103,13 +104,16 @@
 ENDS = [-(-W * NU * (k + 1) // PARTS // T) * T for k in range(PARTS)]
 
 
-def pack_kernel(a_ref, out_ref, near, sems):
+def pack_kernel(a_ref, out_ref, near, ready, sems, out_sems):
     i = pl.program_id(0)
     lane = lane_of((1, T))
 
     def fetch(k):
         lanes = pl.ds(ENDS[k - 1] if k else 0, ENDS[k] - (ENDS[k - 1] if k else 0))
         return pltpu.make_async_copy(a_ref.at[:, lanes], near.at[:, lanes], sems.at[k])
+
+    def send(u):
+        return pltpu.make_async_copy(ready.at[u], out_ref.at[u], out_sems.at[u])
 
     def cut(u, block):
         q, o = divmod(u * W, T)
@@ -137,7 +141,13 @@
                     x = cut(u, block)
                     if block < 2 * STRIPS:
                         x = with_strip(x, tails[block % 2], block // 2, lane)
-                    out_ref[n, block * H : (block + 1) * H, :] = x
+                    ready[u, block * H : (block + 1) * H, :] = x
+                send(u).start()
+
+    @pl.when(i == PARTS - 1)
+    def _():
+        for u in range(NU):
+            send(u).wait()
 
 
 def packed(values, t, lane):
@@ -165,7 +175,7 @@
             keep(pl.multiple_of(s * ROWS + HEAD + h * H, H), from_strips(strips, lane))
         return c
 
-    lax.fori_loop(0, NU, put, 0)
+    lax.fori_loop(0, NU, put, 0, unroll=2)
 
 
 def keep_both(xs, at, n, x):
@@ -279,8 +289,9 @@
             tile_fetch(tiles_ref, tiles, sems, k).start()
         acc[...] = jnp.zeros_like(acc)
         down = idx_ref[NT * KT]
+        y, z = down // NZ, lax.rem(down, NZ)
         for s in range(ND):
-            source = lax.rem(down + ND - s, ND)
+            source = (y if s < NZ else 1 - y) * NZ + lax.rem(z + NZ - s % NZ, NZ)
             for o in range(G):
                 x = pieces[s][:, o * T : (o + 1) * T]
                 xs[source * G + o] = x
@@ -406,7 +417,7 @@
         sums_ref[...] = jnp.broadcast_to(row, sums_ref.shape)
 
 
-def final_kernel(a_ref, u_ref, g_ref, center_ref, shared_ref, v_ref, out_ref, coef):
+def final_kernel(a_ref, u_ref, g_ref, center_ref, shared_ref, v_ref, out_ref, coef, ready, sems):
     i = pl.program_id(0)
     lane = lane_of((1, T))
 
@@ -446,17 +457,30 @@
         out_ref[...] = jnp.broadcast_to(row, out_ref.shape)
 
     ca, cu, cg = coef[0:1, 4:5], coef[0:1, 5:6], coef[0:1, 6:7]
-    v_ref[0] = (cg * g_ref[i] + cu * u_ref[i] + ca * a_ref[0].astype(f32)).astype(bf16)
+    ready[i] = (cg * g_ref[i] + cu * u_ref[i] + ca * a_ref[i].astype(f32)).astype(bf16)
+
+    def send(d):
+        return pltpu.make_async_copy(ready.at[d], v_ref.at[d], sems.at[d])
+
+    send(i).start()
+
+    @pl.when(i == ND - 1)
+    def _():
+        for d in range(ND):
+            send(d).wait()
 
 
 def swapped_down(start_vector):
-    down = lax.axis_index(DN)
+    y, z = lax.axis_index("dn_0"), lax.axis_index("dn_1")
     pieces = []
-    for s in range(ND):
-        piece = lax.dynamic_slice_in_dim(start_vector, (down + s) % ND * W, W, 0)
-        if s:
-            piece = lax.ppermute(piece, DN, [(k, (k + s) % ND) for k in range(ND)])
-        pieces.append(piece)
+    for b in range(2):
+        for s in range(NZ):
+            to = (y if b == 0 else 1 - y) * NZ + (z + s) % NZ
+            piece = lax.dynamic_slice_in_dim(start_vector, to * W, W, 0)
+            if b or s:
+                swaps = [(k, (k // NZ ^ b) * NZ + (k + s) % NZ) for k in range(ND)]
+                piece = lax.ppermute(piece, DN, swaps)
+            pieces.append(piece)
     return pieces
 
 
@@ -479,9 +503,14 @@
         pack_kernel,
         grid=(PARTS,),
         in_specs=[pl.BlockSpec(memory_space=pl.ANY)],
-        out_specs=pl.BlockSpec((NU // PARTS, HEAD, T), lambda i: (i, 0, 0)),
+        out_specs=pl.BlockSpec(memory_space=pl.ANY),
         out_shape=pltpu.HBM((NU, HEAD, T), bf16),
-        scratch_shapes=[pltpu.VMEM(start_vector.shape, bf16), pltpu.SemaphoreType.DMA((PARTS,))],
+        scratch_shapes=[
+            pltpu.VMEM(start_vector.shape, bf16),
+            pltpu.VMEM((NU, HEAD, T), bf16),
+            pltpu.SemaphoreType.DMA((PARTS,)),
+            pltpu.SemaphoreType.DMA((NU,)),
+        ],
         compiler_params=params(24),
         name="pack",
     )(far(start_vector))
@@ -616,10 +645,10 @@
     v, scalars = pl.pallas_call(
         final_kernel,
         grid=(ND,),
-        in_specs=[block, near, near, whole((8, T)), whole((NU * ND, T))],
-        out_specs=[block, whole((8, T))],
+        in_specs=[near, near, near, whole((8, T)), whole((NU * ND, T))],
+        out_specs=[pl.BlockSpec(memory_space=pl.ANY), whole((8, T))],
         out_shape=[pltpu.HBM(wide, bf16), jax.ShapeDtypeStruct((8, T), f32)],
-        scratch_shapes=[pltpu.VMEM((8, T), f32)],
+        scratch_shapes=[pltpu.VMEM((8, T), f32), pltpu.VMEM(wide, bf16), pltpu.SemaphoreType.DMA((ND,))],
         compiler_params=params(16),
         name="final",
     )(a_dn, u, g, far(down_dots), shared)

time: 303 us -> 289 us (0.954)
  starting transfers between devices: 55.5 us -> 43 us
  waiting for transfers between devices: 108 us -> 115 us
  blocking collectives: 19.4 us -> 13.8 us
    ppermute x7, starting transfers between devices: 26.6 us -> 15.1 us  [swapped_down(): piece = lax.ppermute(piece, DN, swaps)]
    ppermute x7, waiting for transfers between devices: 50 us -> 55.7 us  [swapped_down(): piece = lax.ppermute(piece, DN, swaps)]
    all_to_all x1, blocking collectives: 19.4 us -> 13.8 us  [body(): shared = lax.all_to_all(partial, ALL, 0, 0, tiled=True)]
  transfers between devices with their start and end apart: 11 -> 11, of which waited for: 6 -> 9; matrix products, arithmetic and copies ran while one was open for 6% -> 7% of each run, Pallas kernels for 21% -> 22%
where the time goes in v5:
time: 289 us; the launch traced here: 287 us
  waiting for transfers between devices  115 us (40%)
  Pallas kernels  90 us (31%)
  starting transfers between devices  43 us (15%)
  local copies, waits for them, and re-layouts  18 us (6%)
  blocking collectives  13.8 us (5%)
  other arithmetic  5.88 us (2%)
    ppermute x7, waiting for transfers between devices, swapped_down(): piece = lax.ppermute(piece, DN, swaps)  55.7 us
    pallas_call x1, Pallas kernels, body(): pl.pallas_call(down_kernel, grid_spec=pltpu.PrefetchScalarGridSpec(num_sc...  33.6 us
    all_to_all x1, waiting for transfers between devices, body(): final = lax.all_to_all(v, DN, 0, 0, tiled=True).reshape(rows, cols)  32 us
    pallas_call x1, Pallas kernels, body(): second_up(index, far(a_up), far(p), *[far(hop_tiles)] * KT, far(occ_rows)...  28.4 us
    all_to_all x1, waiting for transfers between devices, body(): a_up = lax.all_to_all(parts, UP, 0, 0, tiled=True)  23.4 us
    ppermute x7, starting transfers between devices, swapped_down(): piece = lax.ppermute(piece, DN, swaps)  15.1 us
    all_to_all x1, blocking collectives, body(): shared = lax.all_to_all(partial, ALL, 0, 0, tiled=True)  13.8 us
    pallas_call x1, Pallas kernels, body(): p, sums = first_up(index, a_up, far(hop_tiles), mean)  11 us
  transfers between devices with their start and end apart: 11, of which 9 were waited for; matrix products, arithmetic and copies ran while one was open for 7% of the time, Pallas kernels for 22%

profile of v5, /device:TPU:24, one launch (start us, length us, event | category | flops | bytes accessed | tf_op | source)
XLA Modules:
  0.0 287.4 jit_solution(16546996027704229124)
XLA Ops:
  0.6 5.1 %pack.1 = bf16[16,704,128]{2,1,0:T(8,128)(2,1)} custom-call(bf16[832,1664]{1,0:T(8,128)(2,1)} %a_ref.1), custom_call_target="tpu_custom_call" | custom-call | tf_op jit(solution)/shard_map/pack/pallas_call | solution.py:502
  5.8 5.8 %all-to-all-start = ((bf16[16,704,128]{2,1,0:T(8,128)(2,1)}), bf16[16,704,128]{2,1,0:T(8,128)(2,1)S(1)}, u32[]{:S(2)}, u32[]{:S(2)}) async-start(bf16[16,704,128]{2,1,0:T(8,128)(2,1)} %pack.1), calls=%async_computation | async-start | bytes 5767168 | tf_op jit(solution)/shard_map/all_to_all | solution.py:517
  11.9 5.2 %copy.16 = s32[16,13312]{0,1:T(8,128)} copy(s32[16,13312]{1,0:T(8,128)} %param.9) | data formatting | bytes 1703936 | tf_op args[4]
  17.1 5.2 %convert_reduce_fusion = (f32[16]{0:T(128)S(1)}, bf16[16,13312]{0,1:T(8,128)(2,1)S(1)}) fusion(s32[16,13312]{0,1:T(8,128)} %copy.16), kind=kLoop, calls=%fused_computation | loop fusion | flops 638960 | bytes 1278016 | tf_op jit(solution)/shard_map/reduce_sum | solution.py:497
  22.3 1.8 copy-done.4
  26.0 23.4 %all-to-all-done.a_ref = bf16[16,704,128]{2,1,0:T(8,128)(2,1)S(1)} async-done(((bf16[16,704,128]{2,1,0:T(8,128)(2,1)}), bf16[16,704,128]{2,1,0:T(8,128)(2,1)S(1)}, u32[]{:S(2)}, u32[]{:S(2)}) %all-to-all-start) | async-done | bytes 2883616 | tf_op jit(solution)/shard_map/all_to_all | solution.py:517
  49.4 11.0 %first_up.1 = (bf16[128,88,128]{2,1,0:T(8,128)(2,1)}, f32[8,128]{1,0:T(8,128)S(1)}) custom-call(s32[521]{0:T(1024)S(1)} %pad_add_fusion.idx_ref, bf16[16,704,128]{2,1,0:T(8,128)(2,1)S(1)} %all-to-all-done.a_ref, bf16[104,5,128,128]{3,2,1,0:T(8,128)(2,1)} %refs_9_.1, f32[8,128]{1,0:T(8,128)S(1)} %broadcast_in_dim.7.mean_ref), custom_call_target="tpu_custom_call" | custom-call | flops 2181038080 | bytes 25427968 | tf_op jit(solution)/shard_map/first_up/pallas_call | solution.py:556
  60.4 10.2 %all-to-all-start.1 = ((bf16[128,88,128]{2,1,0:T(8,128)(2,1)}), bf16[128,88,128]{2,1,0:T(8,128)(2,1)}, u32[]{:S(2)}, u32[]{:S(2)}) async-start(bf16[128,88,128]{2,1,0:T(8,128)(2,1)} %get-tuple-element.19.p_ref), calls=%async_computation.1 | async-start | bytes 5767168 | tf_op jit(solution)/shard_map/all_to_all | solution.py:558
  70.7 3.9 %copy.19 = bf16[16,8,1664]{2,0,1:T(8,128)(2,1)} copy(bf16[16,8,1664]{0,2,1:T(8,128)(2,1)} %bitcast.19) | data formatting | bytes 851968 | tf_op jit(solution)/shard_map/reshape | solution.py:500
  74.6 28.4 %second_up.1 = (bf16[128,88,128]{2,1,0:T(8,128)(2,1)}, f32[8,128]{1,0:T(8,128)S(1)}) custom-call(s32[521]{0:T(1024)S(1)} %pad_add_fusion.idx_ref, bf16[16,704,128]{2,1,0:T(8,128)(2,1)} %copy-done, bf16[128,88,128]{2,1,0:T(8,128)(2,1)} %get-tuple-element.19.p_ref, bf16[104,5,128,128]{3,2,1,0:T(8,128)(2,1)} %refs_9_.1, bf16[104,5,128,128]{3,2,1,0:T(8,128)(2,1)} %refs_9_.1, ...), custom_call_target="tpu_custom_call" | custom-call | flops 2181038080 | bytes 25427968 | tf_op jit(solution)/shard_map/second_up/pallas_call | solution.py:581
  103.6 4.0 %all-to-all-done.1.refs_8_ = bf16[128,88,128]{2,1,0:T(8,128)(2,1)} async-done(((bf16[128,88,128]{2,1,0:T(8,128)(2,1)}), bf16[128,88,128]{2,1,0:T(8,128)(2,1)}, u32[]{:S(2)}, u32[]{:S(2)}) %all-to-all-start.1) | async-done | bytes 2883616 | tf_op jit(solution)/shard_map/all_to_all | solution.py:558
  107.7 5.8 %all-to-all-start.2 = ((bf16[128,88,128]{2,1,0:T(8,128)(2,1)}), bf16[128,88,128]{2,1,0:T(8,128)(2,1)S(1)}, u32[]{:S(2)}, u32[]{:S(2)}) async-start(bf16[128,88,128]{2,1,0:T(8,128)(2,1)} %get-tuple-element.28), calls=%async_computation.2 | async-start | bytes 5767168 | tf_op jit(solution)/shard_map/all_to_all | solution.py:584
  113.6 2.7 constant_dynamic-slice_fusion.1
  116.2 4.2 %collective-permute-start.6 = (bf16[104,1664]{1,0:T(8,128)(2,1)S(1)}, bf16[104,1664]{1,0:T(8,128)(2,1)S(1)}, u32[]{:S(2)}, u32[]{:S(2)}) collective-permute-start(bf16[104,1664]{1,0:T(8,128)(2,1)S(1)} %get-tuple-element.39), channel_id=1, source_target_pairs={{0,7},{1,4},{2,5},{3,6},{4,3},{5,0},{6,1},{7,2},{8,15},{9,12},{10,... | collective-permute-start | bytes 1038344 | tf_op jit(solution)/shard_map/ppermute | solution.py:482
  120.5 2.0 collective-permute-start.5
  122.4 1.9 collective-permute-start.4
  124.3 2.2 collective-permute-start.3
  126.5 2.1 collective-permute-start.2
  128.6 27.5 %collective-permute-done.6.refs_7_ = bf16[104,1664]{1,0:T(8,128)(2,1)S(1)} collective-permute-done((bf16[104,1664]{1,0:T(8,128)(2,1)S(1)}, bf16[104,1664]{1,0:T(8,128)(2,1)S(1)}, u32[]{:S(2)}, u32[]{:S(2)}) %collective-permute-start.6) | collective-permute-done | bytes 346144 | tf_op jit(solution)/shard_map/ppermute | solution.py:482
  156.1 2.7 collective-permute-start.1
  158.8 7.3 %collective-permute-done.5.refs_6_ = bf16[104,1664]{1,0:T(8,128)(2,1)S(1)} collective-permute-done((bf16[104,1664]{1,0:T(8,128)(2,1)S(1)}, bf16[104,1664]{1,0:T(8,128)(2,1)S(1)}, u32[]{:S(2)}, u32[]{:S(2)}) %collective-permute-start.5) | collective-permute-done | bytes 346144 | tf_op jit(solution)/shard_map/ppermute | solution.py:482
  166.1 6.9 %collective-permute-done.4.refs_5_ = bf16[104,1664]{1,0:T(8,128)(2,1)S(1)} collective-permute-done((bf16[104,1664]{1,0:T(8,128)(2,1)S(1)}, bf16[104,1664]{1,0:T(8,128)(2,1)S(1)}, u32[]{:S(2)}, u32[]{:S(2)}) %collective-permute-start.4) | collective-permute-done | bytes 346144 | tf_op jit(solution)/shard_map/ppermute | solution.py:482
  173.0 3.9 %collective-permute-done.3.refs_4_ = bf16[104,1664]{1,0:T(8,128)(2,1)S(1)} collective-permute-done((bf16[104,1664]{1,0:T(8,128)(2,1)S(1)}, bf16[104,1664]{1,0:T(8,128)(2,1)S(1)}, u32[]{:S(2)}, u32[]{:S(2)}) %collective-permute-start.3) | collective-permute-done | bytes 346144 | tf_op jit(solution)/shard_map/ppermute | solution.py:482
  176.9 2.9 %collective-permute-done.1.refs_2_ = bf16[104,1664]{1,0:T(8,128)(2,1)S(1)} collective-permute-done((bf16[104,1664]{1,0:T(8,128)(2,1)S(1)}, bf16[104,1664]{1,0:T(8,128)(2,1)S(1)}, u32[]{:S(2)}, u32[]{:S(2)}) %collective-permute-start.1) | collective-permute-done | bytes 346144 | tf_op jit(solution)/shard_map/ppermute | solution.py:482
  179.8 7.3 %collective-permute-done.refs_1_ = bf16[104,1664]{1,0:T(8,128)(2,1)S(1)} collective-permute-done((bf16[104,1664]{1,0:T(8,128)(2,1)S(1)}, bf16[104,1664]{1,0:T(8,128)(2,1)S(1)}, u32[]{:S(2)}, u32[]{:S(2)}) %collective-permute-start) | collective-permute-done | bytes 346144 | tf_op jit(solution)/shard_map/ppermute | solution.py:482
  187.8 33.6 %down.1 = (bf16[8,104,1664]{2,1,0:T(8,128)(2,1)}, f32[8,104,1664]{2,1,0:T(8,128)}, bf16[8,104,1664]{2,1,0:T(8,128)(2,1)}, f32[8,104,1664]{2,1,0:T(8,128)}, f32[8,128]{1,0:T(8,128)}) custom-call(s32[521]{0:T(1024)} %copy-done.2, bf16[104,1664]{1,0:T(8,128)(2,1)} %get-tuple-element.46.refs_0_, bf16[104,1664]{1,0:T(8,128)(2,1)} %copy-done.11, ...), custom_call_target="tpu_custom_call" | custom-call | flops 2181038080 | bytes 25427968 | tf_op jit(solution)/shard_map/down/pallas_call | solution.py:591
  221.4 6.6 %joined.1 = (f32[8,104,1664]{2,1,0:T(8,128)S(1)}, f32[128,128]{1,0:T(8,128)S(1)}) custom-call(bf16[8,104,1664]{2,1,0:T(8,128)(2,1)} %get-tuple-element.24.refs_0_.a_ref, bf16[8,104,1664]{2,1,0:T(8,128)(2,1)} %get-tuple-element.26.refs_1_, f32[8,104,1664]{2,1,0:T(8,128)} %get-tuple-element.27.refs_2_, bf16[128,88,128]{2,1,0:T(8,128)(2,1)S(1)} %all-to-all-done.2.refs_3_, ...), custom_call_target="tpu_custom_call" | custom-call | tf_op jit(solution)/shard_map/joined/pallas_call | solution.py:627
  228.0 13.8 %all_to_all.31 = f32[128,1,128]{2,1,0:T(1,128)S(1)} all-to-all(f32[128,1,128]{2,1,0:T(1,128)S(1)} %bitcast.18), channel_id=1, replica_groups=mesh['up_0'=2,'up_1'=4,'up_2'=2,'dn_0'=2,'dn_1'=4] {'up_0','up_1','up_2'..., dimensions={0} | all-to-all | bytes 131072 | tf_op jit(solution)/shard_map/all_to_all | solution.py:644
  241.9 5.3 %final.1 = (bf16[8,104,1664]{2,1,0:T(8,128)(2,1)}, f32[8,128]{1,0:T(8,128)S(1)}) custom-call(bf16[8,104,1664]{2,1,0:T(8,128)(2,1)S(1)} %copy-done.1, f32[8,104,1664]{2,1,0:T(8,128)S(1)} %bitcast.16, f32[8,104,1664]{2,1,0:T(8,128)S(1)} %get-tuple-element.31.g_ref, f32[8,128]{1,0:T(8,128)} %get-tuple-element.30.refs_5_.center_ref, f32[128,128]{1,0:T(8,128)S(1)} %bitcast.17), custom_call_target="tpu_custom_call" | custom-call | tf_op jit(solution)/shard_map/final/pallas_call | solution.py:645
  247.1 6.1 %all-to-all-start.4 = ((bf16[8,104,1664]{2,1,0:T(8,128)(2,1)}), bf16[8,104,1664]{2,1,0:T(8,128)(2,1)S(1)}, u32[]{:S(2)}, u32[]{:S(2)}) async-start(bf16[8,104,1664]{2,1,0:T(8,128)(2,1)} %get-tuple-element.33), calls=%async_computation.4 | async-start | bytes 5537792 | tf_op jit(solution)/shard_map/all_to_all | solution.py:655
  253.9 32.0 %all-to-all-done.4 = bf16[8,104,1664]{2,1,0:T(8,128)(2,1)S(1)} async-done(((bf16[8,104,1664]{2,1,0:T(8,128)(2,1)}), bf16[8,104,1664]{2,1,0:T(8,128)(2,1)S(1)}, u32[]{:S(2)}, u32[]{:S(2)}) %all-to-all-start.4) | async-done | bytes 2768928 | tf_op jit(solution)/shard_map/all_to_all | solution.py:655
  285.9 1.5 copy.25
  (46 shorter events, 3.6 us)
Async XLA Ops:
  5.8 5.8 %copy-start.12 = (s32[104,5]{0,1:T(8,128)S(1)}, s32[104,5]{0,1:T(8,128)}, u32[]{:S(2)}) copy-start(s32[104,5]{0,1:T(8,128)} %param.7) | copy-start | bytes 6244
  5.8 5.8 %copy-start.13 = (s32[104,5]{0,1:T(8,128)S(1)}, s32[104,5]{0,1:T(8,128)}, u32[]{:S(2)}) copy-start(s32[104,5]{0,1:T(8,128)} %param.8) | copy-start | bytes 6244
  5.8 43.6 %all-to-all-start = ((bf16[16,704,128]{2,1,0:T(8,128)(2,1)}), bf16[16,704,128]{2,1,0:T(8,128)(2,1)S(1)}, u32[]{:S(2)}, u32[]{:S(2)}) async-start(bf16[16,704,128]{2,1,0:T(8,128)(2,1)} %pack.1), calls=%async_computation | async-start | bytes 5767168 | tf_op jit(solution)/shard_map/all_to_all | solution.py:517
  22.3 1.8 copy-start.4
  26.0 48.6 %copy-start.2 = (s32[521]{0:T(1024)}, s32[521]{0:T(1024)S(1)}, u32[]{:S(2)}) copy-start(s32[521]{0:T(1024)S(1)} %pad_add_fusion.idx_ref) | copy-start | bytes 6256
  49.4 11.0 %copy-start = (bf16[16,704,128]{2,1,0:T(8,128)(2,1)}, bf16[16,704,128]{2,1,0:T(8,128)(2,1)S(1)}, u32[]{:S(2)}) copy-start(bf16[16,704,128]{2,1,0:T(8,128)(2,1)S(1)} %all-to-all-done.a_ref) | copy-start | bytes 8650756
  60.4 47.3 %all-to-all-start.1 = ((bf16[128,88,128]{2,1,0:T(8,128)(2,1)}), bf16[128,88,128]{2,1,0:T(8,128)(2,1)}, u32[]{:S(2)}, u32[]{:S(2)}) async-start(bf16[128,88,128]{2,1,0:T(8,128)(2,1)} %get-tuple-element.19.p_ref), calls=%async_computation.1 | async-start | bytes 5767168 | tf_op jit(solution)/shard_map/all_to_all | solution.py:558
  103.0 0.6 copy-start.3
  107.7 113.7 %all-to-all-start.2 = ((bf16[128,88,128]{2,1,0:T(8,128)(2,1)}), bf16[128,88,128]{2,1,0:T(8,128)(2,1)S(1)}, u32[]{:S(2)}, u32[]{:S(2)}) async-start(bf16[128,88,128]{2,1,0:T(8,128)(2,1)} %get-tuple-element.28), calls=%async_computation.2 | async-start | bytes 5767168 | tf_op jit(solution)/shard_map/all_to_all | solution.py:584
  116.2 39.9 %collective-permute-start.6 = (bf16[104,1664]{1,0:T(8,128)(2,1)S(1)}, bf16[104,1664]{1,0:T(8,128)(2,1)S(1)}, u32[]{:S(2)}, u32[]{:S(2)}) collective-permute-start(bf16[104,1664]{1,0:T(8,128)(2,1)S(1)} %get-tuple-element.39), channel_id=1, source_target_pairs={{0,7},{1,4},{2,5},{3,6},{4,3},{5,0},{6,1},{7,2},{8,15},{9,12},{10,... | collective-permute-start | bytes 1038344 | tf_op jit(solution)/shard_map/ppermute | solution.py:482
  120.5 45.6 %collective-permute-start.5 = (bf16[104,1664]{1,0:T(8,128)(2,1)S(1)}, bf16[104,1664]{1,0:T(8,128)(2,1)S(1)}, u32[]{:S(2)}, u32[]{:S(2)}) collective-permute-start(bf16[104,1664]{1,0:T(8,128)(2,1)S(1)} %get-tuple-element.40), channel_id=1, source_target_pairs={{0,6},{1,7},{2,4},{3,5},{4,2},{5,3},{6,0},{7,1},{8,14},{9,15},{10,... | collective-permute-start | bytes 1038344 | tf_op jit(solution)/shard_map/ppermute | solution.py:482
  122.4 50.6 %collective-permute-start.4 = (bf16[104,1664]{1,0:T(8,128)(2,1)S(1)}, bf16[104,1664]{1,0:T(8,128)(2,1)S(1)}, u32[]{:S(2)}, u32[]{:S(2)}) collective-permute-start(bf16[104,1664]{1,0:T(8,128)(2,1)S(1)} %get-tuple-element.41), channel_id=1, source_target_pairs={{0,5},{1,6},{2,7},{3,4},{4,1},{5,2},{6,3},{7,0},{8,13},{9,14},{10,... | collective-permute-start | bytes 1038344 | tf_op jit(solution)/shard_map/ppermute | solution.py:482
  124.3 52.6 %collective-permute-start.3 = (bf16[104,1664]{1,0:T(8,128)(2,1)S(1)}, bf16[104,1664]{1,0:T(8,128)(2,1)S(1)}, u32[]{:S(2)}, u32[]{:S(2)}) collective-permute-start(bf16[104,1664]{1,0:T(8,128)(2,1)S(1)} %get-tuple-element.42), channel_id=1, source_target_pairs={{0,4},{1,5},{2,6},{3,7},{4,0},{5,1},{6,2},{7,3},{8,12},{9,13},{10,... | collective-permute-start | bytes 1038344 | tf_op jit(solution)/shard_map/ppermute | solution.py:482
  126.5 50.4 %collective-permute-start.2 = (bf16[104,1664]{1,0:T(8,128)(2,1)S(1)}, bf16[104,1664]{1,0:T(8,128)(2,1)S(1)}, u32[]{:S(2)}, u32[]{:S(2)}) collective-permute-start(bf16[104,1664]{1,0:T(8,128)(2,1)S(1)} %get-tuple-element.43), channel_id=1, source_target_pairs={{0,3},{1,0},{2,1},{3,2},{4,7},{5,4},{6,5},{7,6},{8,11},{9,8},{10,9... | collective-permute-start | bytes 1038344 | tf_op jit(solution)/shard_map/ppermute | solution.py:482
  156.1 30.9 %copy-start.5 = (bf16[104,1664]{1,0:T(8,128)(2,1)}, bf16[104,1664]{1,0:T(8,128)(2,1)S(1)}, u32[]{:S(2)}) copy-start(bf16[104,1664]{1,0:T(8,128)(2,1)S(1)} %collective-permute-done.6.refs_7_) | copy-start | bytes 1038340
  156.1 23.6 %collective-permute-start.1 = (bf16[104,1664]{1,0:T(8,128)(2,1)S(1)}, bf16[104,1664]{1,0:T(8,128)(2,1)S(1)}, u32[]{:S(2)}, u32[]{:S(2)}) collective-permute-start(bf16[104,1664]{1,0:T(8,128)(2,1)S(1)} %get-tuple-element.44), channel_id=1, source_target_pairs={{0,2},{1,3},{2,0},{3,1},{4,6},{5,7},{6,4},{7,5},{8,10},{9,11},{10,... | collective-permute-start | bytes 1038344 | tf_op jit(solution)/shard_map/ppermute | solution.py:482
  166.1 21.0 %copy-start.6 = (bf16[104,1664]{1,0:T(8,128)(2,1)}, bf16[104,1664]{1,0:T(8,128)(2,1)S(1)}, u32[]{:S(2)}) copy-start(bf16[104,1664]{1,0:T(8,128)(2,1)S(1)} %collective-permute-done.5.refs_6_) | copy-start | bytes 1038340
  166.1 20.9 %collective-permute-start = (bf16[104,1664]{1,0:T(8,128)(2,1)S(1)}, bf16[104,1664]{1,0:T(8,128)(2,1)S(1)}, u32[]{:S(2)}, u32[]{:S(2)}) collective-permute-start(bf16[104,1664]{1,0:T(8,128)(2,1)S(1)} %get-tuple-element.45), channel_id=1, source_target_pairs={{0,1},{1,2},{2,3},{3,0},{4,5},{5,6},{6,7},{7,4},{8,9},{9,10},{10,1... | collective-permute-start | bytes 1038344 | tf_op jit(solution)/shard_map/ppermute | solution.py:482
  173.0 14.1 %copy-start.7 = (bf16[104,1664]{1,0:T(8,128)(2,1)}, bf16[104,1664]{1,0:T(8,128)(2,1)S(1)}, u32[]{:S(2)}) copy-start(bf16[104,1664]{1,0:T(8,128)(2,1)S(1)} %collective-permute-done.4.refs_5_) | copy-start | bytes 1038340
  176.9 10.2 %copy-start.8 = (bf16[104,1664]{1,0:T(8,128)(2,1)}, bf16[104,1664]{1,0:T(8,128)(2,1)S(1)}, u32[]{:S(2)}) copy-start(bf16[104,1664]{1,0:T(8,128)(2,1)S(1)} %collective-permute-done.3.refs_4_) | copy-start | bytes 1038340
  176.9 10.2 %copy-start.9 = (bf16[104,1664]{1,0:T(8,128)(2,1)}, bf16[104,1664]{1,0:T(8,128)(2,1)S(1)}, u32[]{:S(2)}) copy-start(bf16[104,1664]{1,0:T(8,128)(2,1)S(1)} %collective-permute-done.2.refs_3_) | copy-start | bytes 1038340
  179.8 7.3 %copy-start.10 = (bf16[104,1664]{1,0:T(8,128)(2,1)}, bf16[104,1664]{1,0:T(8,128)(2,1)S(1)}, u32[]{:S(2)}) copy-start(bf16[104,1664]{1,0:T(8,128)(2,1)S(1)} %collective-permute-done.1.refs_2_) | copy-start | bytes 1038340
  187.1 0.7 copy-start.11
  221.4 20.5 %slice-start = ((s8[5537792]{0:T(1024)(128)(4,1)}), s8[4194304]{0:T(1024)(128)(4,1)S(1)}, s32[]{:S(2)}) async-start(s8[5537792]{0:T(1024)(128)(4,1)} %bitcast.15), calls=%async_computation.5 | async-start | bytes 8388608
  221.4 20.4 %copy-start.1 = (bf16[8,104,1664]{2,1,0:T(8,128)(2,1)S(1)}, bf16[8,104,1664]{2,1,0:T(8,128)(2,1)}, u32[]{:S(2)}) copy-start(bf16[8,104,1664]{2,1,0:T(8,128)(2,1)} %get-tuple-element.24.refs_0_.a_ref) | copy-start | bytes 8306692
  221.4 20.4 %slice-start.1 = ((s8[5537792]{0:T(1024)(128)(4,1)}), s8[1343488]{0:T(1024)(128)(4,1)S(1)}, s32[]{:S(2)}) async-start(s8[5537792]{0:T(1024)(128)(4,1)} %bitcast.15), calls=%async_computation.6 | async-start | bytes 2686976
  247.1 38.7 %all-to-all-start.4 = ((bf16[8,104,1664]{2,1,0:T(8,128)(2,1)}), bf16[8,104,1664]{2,1,0:T(8,128)(2,1)S(1)}, u32[]{:S(2)}, u32[]{:S(2)}) async-start(bf16[8,104,1664]{2,1,0:T(8,128)(2,1)} %get-tuple-element.33), calls=%async_computation.4 | async-start | bytes 5537792 | tf_op jit(solution)/shard_map/all_to_all | solution.py:655

commit v6 on v5

--- a/solution.py
+++ b/solution.py
@@ -105,7 +105,6 @@
 
 
 def pack_kernel(a_ref, out_ref, near, ready, sems, out_sems):
-    i = pl.program_id(0)
     lane = lane_of((1, T))
 
     def fetch(k):
@@ -124,30 +123,22 @@
             x = jnp.where(lane < T - o, x, y)
         return x
 
-    @pl.when(i == 0)
-    def _():
-        for k in range(PARTS):
-            fetch(k).start()
-
     for k in range(PARTS):
-
-        @pl.when(i == k)
-        def _():
-            fetch(k).wait()
-            for n in range(NU // PARTS):
-                u = k * (NU // PARTS) + n
-                tails = [cut(u, HEAD // H + h) for h in range(2)]
-                for block in range(HEAD // H):
-                    x = cut(u, block)
-                    if block < 2 * STRIPS:
-                        x = with_strip(x, tails[block % 2], block // 2, lane)
-                    ready[u, block * H : (block + 1) * H, :] = x
-                send(u).start()
-
-    @pl.when(i == PARTS - 1)
-    def _():
-        for u in range(NU):
-            send(u).wait()
+        fetch(k).start()
+
+    for k in range(PARTS):
+        fetch(k).wait()
+        for n in range(NU // PARTS):
+            u = k * (NU // PARTS) + n
+            tails = [cut(u, HEAD // H + h) for h in range(2)]
+            for block in range(HEAD // H):
+                x = cut(u, block)
+                if block < 2 * STRIPS:
+                    x = with_strip(x, tails[block % 2], block // 2, lane)
+                ready[u, block * H : (block + 1) * H, :] = x
+            send(u).start()
+    for u in range(NU):
+        send(u).wait()
 
 
 def packed(values, t, lane):
@@ -373,101 +364,94 @@
 
 def joined_kernel(*refs):
     far_refs, (q_ref, up_ref, down_ref, g_ref, sums_ref, a_ref, u_ref, t_ref, sems, acc) = refs[:3], refs[3:]
-    i = pl.program_id(0)
     lane = lane_of((1, T))
 
     def fetch(n, d):
         return pltpu.make_async_copy(far_refs[n].at[d], (a_ref, u_ref, t_ref)[n].at[d], sems.at[n, d])
 
-    @pl.when(i == 0)
-    def _():
-        for d in range(ND):
-            for n in range(3):
-                fetch(n, d).start()
-
-    for n in range(3):
-        fetch(n, i).wait()
-
-    @pl.when(i == 0)
-    def _():
-        acc[...] = jnp.zeros_like(acc)
-
-    rolled = {}
-    for o in range(G):
-        for u, _end in pieces_in(o):
-            if u not in rolled:
-                rolled[u] = turned(unpacked(q_ref[u * ND + i], lane), u * W)
-        lanes = slice(o * T, (o + 1) * T)
-        a = a_ref[i, :, lanes].astype(f32)
-        u = u_ref[i, :, lanes].astype(f32)
-        g = assembled(rolled, o, lane).astype(f32) + t_ref[i, :, lanes]
-        g_ref[i, :, lanes] = g
-        for k, product in enumerate([g * g, g * u, g * a]):
-            acc[k] += fold8(product)
-
-    @pl.when(i == ND - 1)
-    def _():
-        row = down_ref[0:1, :]
-        for k, value in enumerate(
-            [down_ref[2:3, :], down_ref[3:4, :], down_ref[4:5, :]]
-            + [total_of(acc[k]) for k in range(3)]
-            + [up_ref[0:1, :] + down_ref[1:2, :]]
-        ):
-            row = jnp.where(lane == k, value, row)
-        sums_ref[...] = jnp.broadcast_to(row, sums_ref.shape)
+    for d in range(ND):
+        for n in range(3):
+            fetch(n, d).start()
+
+    acc[...] = jnp.zeros_like(acc)
+
+    def join(i, c):
+        for n in range(3):
+            fetch(n, i).wait()
+        rolled = {}
+        for o in range(G):
+            for u, _end in pieces_in(o):
+                if u not in rolled:
+                    rolled[u] = turned(unpacked(q_ref[u * ND + i], lane), u * W)
+            lanes = slice(o * T, (o + 1) * T)
+            a = a_ref[i, :, lanes].astype(f32)
+            u = u_ref[i, :, lanes].astype(f32)
+            g = assembled(rolled, o, lane).astype(f32) + t_ref[i, :, lanes]
+            g_ref[i, :, lanes] = g
+            for k, product in enumerate([g * g, g * u, g * a]):
+                acc[k] += fold8(product)
+        return c
+
+    lax.fori_loop(0, ND, join, 0)
+    row = down_ref[0:1, :]
+    for k, value in enumerate(
+        [down_ref[2:3, :], down_ref[3:4, :], down_ref[4:5, :]]
+        + [total_of(acc[k]) for k in range(3)]
+        + [up_ref[0:1, :] + down_ref[1:2, :]]
+    ):
+        row = jnp.where(lane == k, value, row)
+    sums_ref[...] = jnp.broadcast_to(row, sums_ref.shape)
 
 
 def final_kernel(a_ref, u_ref, g_ref, center_ref, shared_ref, v_ref, out_ref, coef, ready, sems):
-    i = pl.program_id(0)
     lane = lane_of((1, T))
 
-    @pl.when(i == 0)
-    def _():
-        table = shared_ref[...].T
-        uu, ua, aa, gg, gu, ga, energy, center = [table[k : k + 1, :] for k in range(8)]
-
-        def total(x):
-            return jnp.sum(x, axis=1, keepdims=True)
-
-        norm = total(aa)
-        scale2 = 1.0 / jnp.maximum(norm, 1.0)
-        alpha1 = total(energy) * scale2
-        off = center - alpha1
-        hh = total(gg + 4.0 * off * (gu + off * (uu + off * ua)) + off * off * (2.0 * ga + off * off * aa))
-        hu = total(gu + off * (2.0 * uu + ga + off * (3.0 * ua + off * aa)))
-        ha = total(ga + off * (2.0 * ua + off * aa))
-        uu = total(uu + off * (2.0 * ua + off * aa))
-        ua = total(ua + off * aa)
-        square1 = jnp.maximum(scale2 * uu, 1.0)
-        ratio2 = scale2 / square1
-        alpha2 = ratio2 * (hu + alpha1 * uu - square1 * ua)
-        move = alpha2 - alpha1
-        nn = hh + square1 * square1 * norm + move * move * uu
-        nn = nn - 2.0 * square1 * ha - 2.0 * move * hu + 2.0 * square1 * move * ua
-        square2 = jnp.maximum(ratio2 * nn, 1.0)
-        beta1, beta2 = jnp.sqrt(square1), jnp.sqrt(square2)
-        cg = jnp.sqrt(ratio2) / beta2
-        off = center_ref[0:1, 0:1] - alpha1
-        row = jnp.zeros((1, T), f32)
-        for k, value in enumerate(
-            [alpha1, alpha2, beta1, beta2, cg * (off * (off - move) - square1), cg * (2.0 * off - move), cg]
-        ):
-            row = jnp.where(lane == k, value, row)
-        coef[...] = jnp.broadcast_to(row, coef.shape)
-        out_ref[...] = jnp.broadcast_to(row, out_ref.shape)
+    table = shared_ref[...].T
+    uu, ua, aa, gg, gu, ga, energy, center = [table[k : k + 1, :] for k in range(8)]
+
+    def total(x):
+        return jnp.sum(x, axis=1, keepdims=True)
+
+    norm = total(aa)
+    scale2 = 1.0 / jnp.maximum(norm, 1.0)
+    alpha1 = total(energy) * scale2
+    off = center - alpha1
+    hh = total(gg + 4.0 * off * (gu + off * (uu + off * ua)) + off * off * (2.0 * ga + off * off * aa))
+    hu = total(gu + off * (2.0 * uu + ga + off * (3.0 * ua + off * aa)))
+    ha = total(ga + off * (2.0 * ua + off * aa))
+    uu = total(uu + off * (2.0 * ua + off * aa))
+    ua = total(ua + off * aa)
+    square1 = jnp.maximum(scale2 * uu, 1.0)
+    ratio2 = scale2 / square1
+    alpha2 = ratio2 * (hu + alpha1 * uu - square1 * ua)
+    move = alpha2 - alpha1
+    nn = hh + square1 * square1 * norm + move * move * uu
+    nn = nn - 2.0 * square1 * ha - 2.0 * move * hu + 2.0 * square1 * move * ua
+    square2 = jnp.maximum(ratio2 * nn, 1.0)
+    beta1, beta2 = jnp.sqrt(square1), jnp.sqrt(square2)
+    cg = jnp.sqrt(ratio2) / beta2
+    off = center_ref[0:1, 0:1] - alpha1
+    row = jnp.zeros((1, T), f32)
+    for k, value in enumerate(
+        [alpha1, alpha2, beta1, beta2, cg * (off * (off - move) - square1), cg * (2.0 * off - move), cg]
+    ):
+        row = jnp.where(lane == k, value, row)
+    coef[...] = jnp.broadcast_to(row, coef.shape)
+    out_ref[...] = jnp.broadcast_to(row, out_ref.shape)
 
     ca, cu, cg = coef[0:1, 4:5], coef[0:1, 5:6], coef[0:1, 6:7]
-    ready[i] = (cg * g_ref[i] + cu * u_ref[i] + ca * a_ref[i].astype(f32)).astype(bf16)
 
     def send(d):
         return pltpu.make_async_copy(ready.at[d], v_ref.at[d], sems.at[d])
 
-    send(i).start()
-
-    @pl.when(i == ND - 1)
-    def _():
-        for d in range(ND):
-            send(d).wait()
+    def combine(d, c):
+        ready[d] = (cg * g_ref[d] + cu * u_ref[d] + ca * a_ref[d].astype(f32)).astype(bf16)
+        send(d).start()
+        return c
+
+    lax.fori_loop(0, ND, combine, 0)
+    for d in range(ND):
+        send(d).wait()
 
 
 def swapped_down(start_vector):
@@ -501,7 +485,6 @@
 
     parts = pl.pallas_call(
         pack_kernel,
-        grid=(PARTS,),
         in_specs=[pl.BlockSpec(memory_space=pl.ANY)],
         out_specs=pl.BlockSpec(memory_space=pl.ANY),
         out_shape=pltpu.HBM((NU, HEAD, T), bf16),
@@ -511,7 +494,7 @@
             pltpu.SemaphoreType.DMA((PARTS,)),
             pltpu.SemaphoreType.DMA((NU,)),
         ],
-        compiler_params=params(24),
+        compiler_params=pltpu.CompilerParams(vmem_limit_bytes=24 * MIB),
         name="pack",
     )(far(start_vector))
     a_up = lax.all_to_all(parts, UP, 0, 0, tiled=True)
@@ -626,7 +609,7 @@
     block = pl.BlockSpec((1, W, cols), lambda i, *_: (i, 0, 0))
     g, partial = pl.pallas_call(
         joined_kernel,
-        grid=(ND,),
+        grid=(1,),
         in_specs=[pl.BlockSpec(memory_space=pl.ANY)] * 3 + [whole(packs), whole((8, T)), whole((8, T))],
         out_specs=[near, whole((NU * ND, T))],
         out_shape=[kept, jax.ShapeDtypeStruct((NU * ND, T), f32)],
@@ -644,7 +627,7 @@
     shared = lax.all_to_all(partial, ALL, 0, 0, tiled=True)
     v, scalars = pl.pallas_call(
         final_kernel,
-        grid=(ND,),
+        grid=(1,),
         in_specs=[near, near, near, whole((8, T)), whole((NU * ND, T))],
         out_specs=[pl.BlockSpec(memory_space=pl.ANY), whole((8, T))],
         out_shape=[pltpu.HBM(wide, bf16), jax.ShapeDtypeStruct((8, T), f32)],

time: 289 us -> 289 us (level)
  no operation moved by 1% of the time
where the time goes in v6:
time: 289 us; the launch traced here: 287 us
  waiting for transfers between devices  115 us (40%)
  Pallas kernels  89.5 us (31%)
  starting transfers between devices  43 us (15%)
  local copies, waits for them, and re-layouts  18 us (6%)
  blocking collectives  13.8 us (5%)
  other arithmetic  5.88 us (2%)
    ppermute x7, waiting for transfers between devices, swapped_down(): piece = lax.ppermute(piece, DN, swaps)  55.7 us
    pallas_call x1, Pallas kernels, body(): pl.pallas_call(down_kernel, grid_spec=pltpu.PrefetchScalarGridSpec(num_sc...  33.6 us
    all_to_all x1, waiting for transfers between devices, body(): final = lax.all_to_all(v, DN, 0, 0, tiled=True).reshape(rows, cols)  32 us
    pallas_call x1, Pallas kernels, body(): second_up(index, far(a_up), far(p), *[far(hop_tiles)] * KT, far(occ_rows)...  28.4 us
    all_to_all x1, waiting for transfers between devices, body(): a_up = lax.all_to_all(parts, UP, 0, 0, tiled=True)  23.4 us
    ppermute x7, starting transfers between devices, swapped_down(): piece = lax.ppermute(piece, DN, swaps)  15.1 us
    all_to_all x1, blocking collectives, body(): shared = lax.all_to_all(partial, ALL, 0, 0, tiled=True)  13.8 us
    pallas_call x1, Pallas kernels, body(): p, sums = first_up(index, a_up, far(hop_tiles), mean)  11 us
  transfers between devices with their start and end apart: 11, of which 9 were waited for; matrix products, arithmetic and copies ran while one was open for 7% of the time, Pallas kernels for 22%

profile of v6, /device:TPU:24, one launch (start us, length us, event | category | flops | bytes accessed | tf_op | source)
XLA Modules:
  0.0 286.9 jit_solution(724803173656466369)
XLA Ops:
  0.6 5.1 %pack.1 = bf16[16,704,128]{2,1,0:T(8,128)(2,1)} custom-call(bf16[832,1664]{1,0:T(8,128)(2,1)} %a_ref.1), custom_call_target="tpu_custom_call" | custom-call | tf_op jit(solution)/shard_map/pack/pallas_call | solution.py:486
  5.7 5.8 %all-to-all-start = ((bf16[16,704,128]{2,1,0:T(8,128)(2,1)}), bf16[16,704,128]{2,1,0:T(8,128)(2,1)S(1)}, u32[]{:S(2)}, u32[]{:S(2)}) async-start(bf16[16,704,128]{2,1,0:T(8,128)(2,1)} %pack.1), calls=%async_computation | async-start | bytes 5767168 | tf_op jit(solution)/shard_map/all_to_all | solution.py:500
  11.8 5.2 %copy.16 = s32[16,13312]{0,1:T(8,128)} copy(s32[16,13312]{1,0:T(8,128)} %param.9) | data formatting | bytes 1703936 | tf_op args[4]
  17.1 5.2 %convert_reduce_fusion = (f32[16]{0:T(128)S(1)}, bf16[16,13312]{0,1:T(8,128)(2,1)S(1)}) fusion(s32[16,13312]{0,1:T(8,128)} %copy.16), kind=kLoop, calls=%fused_computation | loop fusion | flops 638960 | bytes 1278016 | tf_op jit(solution)/shard_map/reduce_sum | solution.py:481
  22.2 1.8 copy-done.4
  26.0 23.4 %all-to-all-done.a_ref = bf16[16,704,128]{2,1,0:T(8,128)(2,1)S(1)} async-done(((bf16[16,704,128]{2,1,0:T(8,128)(2,1)}), bf16[16,704,128]{2,1,0:T(8,128)(2,1)S(1)}, u32[]{:S(2)}, u32[]{:S(2)}) %all-to-all-start) | async-done | bytes 2883616 | tf_op jit(solution)/shard_map/all_to_all | solution.py:500
  49.3 11.0 %first_up.1 = (bf16[128,88,128]{2,1,0:T(8,128)(2,1)}, f32[8,128]{1,0:T(8,128)S(1)}) custom-call(s32[521]{0:T(1024)S(1)} %pad_add_fusion.idx_ref, bf16[16,704,128]{2,1,0:T(8,128)(2,1)S(1)} %all-to-all-done.a_ref, bf16[104,5,128,128]{3,2,1,0:T(8,128)(2,1)} %refs_9_.1, f32[8,128]{1,0:T(8,128)S(1)} %broadcast_in_dim.7.mean_ref), custom_call_target="tpu_custom_call" | custom-call | flops 2181038080 | bytes 25427968 | tf_op jit(solution)/shard_map/first_up/pallas_call | solution.py:539
  60.3 10.2 %all-to-all-start.1 = ((bf16[128,88,128]{2,1,0:T(8,128)(2,1)}), bf16[128,88,128]{2,1,0:T(8,128)(2,1)}, u32[]{:S(2)}, u32[]{:S(2)}) async-start(bf16[128,88,128]{2,1,0:T(8,128)(2,1)} %get-tuple-element.19.p_ref), calls=%async_computation.1 | async-start | bytes 5767168 | tf_op jit(solution)/shard_map/all_to_all | solution.py:541
  70.6 3.9 %copy.19 = bf16[16,8,1664]{2,0,1:T(8,128)(2,1)} copy(bf16[16,8,1664]{0,2,1:T(8,128)(2,1)} %bitcast.19) | data formatting | bytes 851968 | tf_op jit(solution)/shard_map/reshape | solution.py:484
  74.6 28.4 %second_up.1 = (bf16[128,88,128]{2,1,0:T(8,128)(2,1)}, f32[8,128]{1,0:T(8,128)S(1)}) custom-call(s32[521]{0:T(1024)S(1)} %pad_add_fusion.idx_ref, bf16[16,704,128]{2,1,0:T(8,128)(2,1)} %copy-done, bf16[128,88,128]{2,1,0:T(8,128)(2,1)} %get-tuple-element.19.p_ref, bf16[104,5,128,128]{3,2,1,0:T(8,128)(2,1)} %refs_9_.1, bf16[104,5,128,128]{3,2,1,0:T(8,128)(2,1)} %refs_9_.1, ...), custom_call_target="tpu_custom_call" | custom-call | flops 2181038080 | bytes 25427968 | tf_op jit(solution)/shard_map/second_up/pallas_call | solution.py:564
  103.6 4.0 %all-to-all-done.1.refs_8_ = bf16[128,88,128]{2,1,0:T(8,128)(2,1)} async-done(((bf16[128,88,128]{2,1,0:T(8,128)(2,1)}), bf16[128,88,128]{2,1,0:T(8,128)(2,1)}, u32[]{:S(2)}, u32[]{:S(2)}) %all-to-all-start.1) | async-done | bytes 2883616 | tf_op jit(solution)/shard_map/all_to_all | solution.py:541
  107.6 5.8 %all-to-all-start.2 = ((bf16[128,88,128]{2,1,0:T(8,128)(2,1)}), bf16[128,88,128]{2,1,0:T(8,128)(2,1)S(1)}, u32[]{:S(2)}, u32[]{:S(2)}) async-start(bf16[128,88,128]{2,1,0:T(8,128)(2,1)} %get-tuple-element.28), calls=%async_computation.2 | async-start | bytes 5767168 | tf_op jit(solution)/shard_map/all_to_all | solution.py:567
  113.5 2.7 constant_dynamic-slice_fusion.1
  116.2 4.2 %collective-permute-start.6 = (bf16[104,1664]{1,0:T(8,128)(2,1)S(1)}, bf16[104,1664]{1,0:T(8,128)(2,1)S(1)}, u32[]{:S(2)}, u32[]{:S(2)}) collective-permute-start(bf16[104,1664]{1,0:T(8,128)(2,1)S(1)} %get-tuple-element.39), channel_id=1, source_target_pairs={{0,7},{1,4},{2,5},{3,6},{4,3},{5,0},{6,1},{7,2},{8,15},{9,12},{10,... | collective-permute-start | bytes 1038344 | tf_op jit(solution)/shard_map/ppermute | solution.py:466
  120.4 2.0 collective-permute-start.5
  122.4 1.9 collective-permute-start.4
  124.3 2.2 collective-permute-start.3
  126.5 2.1 collective-permute-start.2
  128.6 27.5 %collective-permute-done.6.refs_7_ = bf16[104,1664]{1,0:T(8,128)(2,1)S(1)} collective-permute-done((bf16[104,1664]{1,0:T(8,128)(2,1)S(1)}, bf16[104,1664]{1,0:T(8,128)(2,1)S(1)}, u32[]{:S(2)}, u32[]{:S(2)}) %collective-permute-start.6) | collective-permute-done | bytes 346144 | tf_op jit(solution)/shard_map/ppermute | solution.py:466
  156.1 2.7 collective-permute-start.1
  158.8 7.3 %collective-permute-done.5.refs_6_ = bf16[104,1664]{1,0:T(8,128)(2,1)S(1)} collective-permute-done((bf16[104,1664]{1,0:T(8,128)(2,1)S(1)}, bf16[104,1664]{1,0:T(8,128)(2,1)S(1)}, u32[]{:S(2)}, u32[]{:S(2)}) %collective-permute-start.5) | collective-permute-done | bytes 346144 | tf_op jit(solution)/shard_map/ppermute | solution.py:466
  166.0 6.9 %collective-permute-done.4.refs_5_ = bf16[104,1664]{1,0:T(8,128)(2,1)S(1)} collective-permute-done((bf16[104,1664]{1,0:T(8,128)(2,1)S(1)}, bf16[104,1664]{1,0:T(8,128)(2,1)S(1)}, u32[]{:S(2)}, u32[]{:S(2)}) %collective-permute-start.4) | collective-permute-done | bytes 346144 | tf_op jit(solution)/shard_map/ppermute | solution.py:466
  172.9 3.9 %collective-permute-done.3.refs_4_ = bf16[104,1664]{1,0:T(8,128)(2,1)S(1)} collective-permute-done((bf16[104,1664]{1,0:T(8,128)(2,1)S(1)}, bf16[104,1664]{1,0:T(8,128)(2,1)S(1)}, u32[]{:S(2)}, u32[]{:S(2)}) %collective-permute-start.3) | collective-permute-done | bytes 346144 | tf_op jit(solution)/shard_map/ppermute | solution.py:466
  176.8 2.9 %collective-permute-done.1.refs_2_ = bf16[104,1664]{1,0:T(8,128)(2,1)S(1)} collective-permute-done((bf16[104,1664]{1,0:T(8,128)(2,1)S(1)}, bf16[104,1664]{1,0:T(8,128)(2,1)S(1)}, u32[]{:S(2)}, u32[]{:S(2)}) %collective-permute-start.1) | collective-permute-done | bytes 346144 | tf_op jit(solution)/shard_map/ppermute | solution.py:466
  179.7 7.3 %collective-permute-done.refs_1_ = bf16[104,1664]{1,0:T(8,128)(2,1)S(1)} collective-permute-done((bf16[104,1664]{1,0:T(8,128)(2,1)S(1)}, bf16[104,1664]{1,0:T(8,128)(2,1)S(1)}, u32[]{:S(2)}, u32[]{:S(2)}) %collective-permute-start) | collective-permute-done | bytes 346144 | tf_op jit(solution)/shard_map/ppermute | solution.py:466
  187.7 33.6 %down.1 = (bf16[8,104,1664]{2,1,0:T(8,128)(2,1)}, f32[8,104,1664]{2,1,0:T(8,128)}, bf16[8,104,1664]{2,1,0:T(8,128)(2,1)}, f32[8,104,1664]{2,1,0:T(8,128)}, f32[8,128]{1,0:T(8,128)}) custom-call(s32[521]{0:T(1024)} %copy-done.2, bf16[104,1664]{1,0:T(8,128)(2,1)} %get-tuple-element.46.refs_0_, bf16[104,1664]{1,0:T(8,128)(2,1)} %copy-done.11, ...), custom_call_target="tpu_custom_call" | custom-call | flops 2181038080 | bytes 25427968 | tf_op jit(solution)/shard_map/down/pallas_call | solution.py:574
  221.4 6.3 %joined.1 = (f32[8,104,1664]{2,1,0:T(8,128)S(1)}, f32[128,128]{1,0:T(8,128)S(1)}) custom-call(bf16[8,104,1664]{2,1,0:T(8,128)(2,1)} %get-tuple-element.24.refs_0_.a_ref, bf16[8,104,1664]{2,1,0:T(8,128)(2,1)} %get-tuple-element.26.refs_1_, f32[8,104,1664]{2,1,0:T(8,128)} %get-tuple-element.27.refs_2_, bf16[128,88,128]{2,1,0:T(8,128)(2,1)S(1)} %all-to-all-done.2.refs_3_, ...), custom_call_target="tpu_custom_call" | custom-call | tf_op jit(solution)/shard_map/joined/pallas_call | solution.py:610
  227.7 13.8 %all_to_all.31 = f32[128,1,128]{2,1,0:T(1,128)S(1)} all-to-all(f32[128,1,128]{2,1,0:T(1,128)S(1)} %bitcast.18), channel_id=1, replica_groups=mesh['up_0'=2,'up_1'=4,'up_2'=2,'dn_0'=2,'dn_1'=4] {'up_0','up_1','up_2'..., dimensions={0} | all-to-all | bytes 131072 | tf_op jit(solution)/shard_map/all_to_all | solution.py:627
  241.5 5.1 %final.1 = (bf16[8,104,1664]{2,1,0:T(8,128)(2,1)}, f32[8,128]{1,0:T(8,128)S(1)}) custom-call(bf16[8,104,1664]{2,1,0:T(8,128)(2,1)S(1)} %copy-done.1, f32[8,104,1664]{2,1,0:T(8,128)S(1)} %bitcast.16, f32[8,104,1664]{2,1,0:T(8,128)S(1)} %get-tuple-element.31.g_ref, f32[8,128]{1,0:T(8,128)} %get-tuple-element.30.refs_5_.center_ref, f32[128,128]{1,0:T(8,128)S(1)} %bitcast.17), custom_call_target="tpu_custom_call" | custom-call | tf_op jit(solution)/shard_map/final/pallas_call | solution.py:628
  246.6 6.1 %all-to-all-start.4 = ((bf16[8,104,1664]{2,1,0:T(8,128)(2,1)}), bf16[8,104,1664]{2,1,0:T(8,128)(2,1)S(1)}, u32[]{:S(2)}, u32[]{:S(2)}) async-start(bf16[8,104,1664]{2,1,0:T(8,128)(2,1)} %get-tuple-element.33), calls=%async_computation.4 | async-start | bytes 5537792 | tf_op jit(solution)/shard_map/all_to_all | solution.py:638
  253.4 32.0 %all-to-all-done.4 = bf16[8,104,1664]{2,1,0:T(8,128)(2,1)S(1)} async-done(((bf16[8,104,1664]{2,1,0:T(8,128)(2,1)}), bf16[8,104,1664]{2,1,0:T(8,128)(2,1)S(1)}, u32[]{:S(2)}, u32[]{:S(2)}) %all-to-all-start.4) | async-done | bytes 2768928 | tf_op jit(solution)/shard_map/all_to_all | solution.py:638
  285.4 1.5 copy.25
  (46 shorter events, 3.6 us)
Async XLA Ops:
  5.7 5.8 %copy-start.12 = (s32[104,5]{0,1:T(8,128)S(1)}, s32[104,5]{0,1:T(8,128)}, u32[]{:S(2)}) copy-start(s32[104,5]{0,1:T(8,128)} %param.7) | copy-start | bytes 6244
  5.7 5.8 %copy-start.13 = (s32[104,5]{0,1:T(8,128)S(1)}, s32[104,5]{0,1:T(8,128)}, u32[]{:S(2)}) copy-start(s32[104,5]{0,1:T(8,128)} %param.8) | copy-start | bytes 6244
  5.7 43.6 %all-to-all-start = ((bf16[16,704,128]{2,1,0:T(8,128)(2,1)}), bf16[16,704,128]{2,1,0:T(8,128)(2,1)S(1)}, u32[]{:S(2)}, u32[]{:S(2)}) async-start(bf16[16,704,128]{2,1,0:T(8,128)(2,1)} %pack.1), calls=%async_computation | async-start | bytes 5767168 | tf_op jit(solution)/shard_map/all_to_all | solution.py:500
  22.2 1.8 copy-start.4
  26.0 48.6 %copy-start.2 = (s32[521]{0:T(1024)}, s32[521]{0:T(1024)S(1)}, u32[]{:S(2)}) copy-start(s32[521]{0:T(1024)S(1)} %pad_add_fusion.idx_ref) | copy-start | bytes 6256
  49.3 11.0 %copy-start = (bf16[16,704,128]{2,1,0:T(8,128)(2,1)}, bf16[16,704,128]{2,1,0:T(8,128)(2,1)S(1)}, u32[]{:S(2)}) copy-start(bf16[16,704,128]{2,1,0:T(8,128)(2,1)S(1)} %all-to-all-done.a_ref) | copy-start | bytes 8650756
  60.3 47.3 %all-to-all-start.1 = ((bf16[128,88,128]{2,1,0:T(8,128)(2,1)}), bf16[128,88,128]{2,1,0:T(8,128)(2,1)}, u32[]{:S(2)}, u32[]{:S(2)}) async-start(bf16[128,88,128]{2,1,0:T(8,128)(2,1)} %get-tuple-element.19.p_ref), calls=%async_computation.1 | async-start | bytes 5767168 | tf_op jit(solution)/shard_map/all_to_all | solution.py:541
  103.0 0.6 copy-start.3
  107.6 113.7 %all-to-all-start.2 = ((bf16[128,88,128]{2,1,0:T(8,128)(2,1)}), bf16[128,88,128]{2,1,0:T(8,128)(2,1)S(1)}, u32[]{:S(2)}, u32[]{:S(2)}) async-start(bf16[128,88,128]{2,1,0:T(8,128)(2,1)} %get-tuple-element.28), calls=%async_computation.2 | async-start | bytes 5767168 | tf_op jit(solution)/shard_map/all_to_all | solution.py:567
  116.2 39.9 %collective-permute-start.6 = (bf16[104,1664]{1,0:T(8,128)(2,1)S(1)}, bf16[104,1664]{1,0:T(8,128)(2,1)S(1)}, u32[]{:S(2)}, u32[]{:S(2)}) collective-permute-start(bf16[104,1664]{1,0:T(8,128)(2,1)S(1)} %get-tuple-element.39), channel_id=1, source_target_pairs={{0,7},{1,4},{2,5},{3,6},{4,3},{5,0},{6,1},{7,2},{8,15},{9,12},{10,... | collective-permute-start | bytes 1038344 | tf_op jit(solution)/shard_map/ppermute | solution.py:466
  120.4 45.6 %collective-permute-start.5 = (bf16[104,1664]{1,0:T(8,128)(2,1)S(1)}, bf16[104,1664]{1,0:T(8,128)(2,1)S(1)}, u32[]{:S(2)}, u32[]{:S(2)}) collective-permute-start(bf16[104,1664]{1,0:T(8,128)(2,1)S(1)} %get-tuple-element.40), channel_id=1, source_target_pairs={{0,6},{1,7},{2,4},{3,5},{4,2},{5,3},{6,0},{7,1},{8,14},{9,15},{10,... | collective-permute-start | bytes 1038344 | tf_op jit(solution)/shard_map/ppermute | solution.py:466
  122.4 50.6 %collective-permute-start.4 = (bf16[104,1664]{1,0:T(8,128)(2,1)S(1)}, bf16[104,1664]{1,0:T(8,128)(2,1)S(1)}, u32[]{:S(2)}, u32[]{:S(2)}) collective-permute-start(bf16[104,1664]{1,0:T(8,128)(2,1)S(1)} %get-tuple-element.41), channel_id=1, source_target_pairs={{0,5},{1,6},{2,7},{3,4},{4,1},{5,2},{6,3},{7,0},{8,13},{9,14},{10,... | collective-permute-start | bytes 1038344 | tf_op jit(solution)/shard_map/ppermute | solution.py:466
  124.3 52.6 %collective-permute-start.3 = (bf16[104,1664]{1,0:T(8,128)(2,1)S(1)}, bf16[104,1664]{1,0:T(8,128)(2,1)S(1)}, u32[]{:S(2)}, u32[]{:S(2)}) collective-permute-start(bf16[104,1664]{1,0:T(8,128)(2,1)S(1)} %get-tuple-element.42), channel_id=1, source_target_pairs={{0,4},{1,5},{2,6},{3,7},{4,0},{5,1},{6,2},{7,3},{8,12},{9,13},{10,... | collective-permute-start | bytes 1038344 | tf_op jit(solution)/shard_map/ppermute | solution.py:466
  126.5 50.4 %collective-permute-start.2 = (bf16[104,1664]{1,0:T(8,128)(2,1)S(1)}, bf16[104,1664]{1,0:T(8,128)(2,1)S(1)}, u32[]{:S(2)}, u32[]{:S(2)}) collective-permute-start(bf16[104,1664]{1,0:T(8,128)(2,1)S(1)} %get-tuple-element.43), channel_id=1, source_target_pairs={{0,3},{1,0},{2,1},{3,2},{4,7},{5,4},{6,5},{7,6},{8,11},{9,8},{10,9... | collective-permute-start | bytes 1038344 | tf_op jit(solution)/shard_map/ppermute | solution.py:466
  156.1 30.9 %copy-start.5 = (bf16[104,1664]{1,0:T(8,128)(2,1)}, bf16[104,1664]{1,0:T(8,128)(2,1)S(1)}, u32[]{:S(2)}) copy-start(bf16[104,1664]{1,0:T(8,128)(2,1)S(1)} %collective-permute-done.6.refs_7_) | copy-start | bytes 1038340
  156.1 23.6 %collective-permute-start.1 = (bf16[104,1664]{1,0:T(8,128)(2,1)S(1)}, bf16[104,1664]{1,0:T(8,128)(2,1)S(1)}, u32[]{:S(2)}, u32[]{:S(2)}) collective-permute-start(bf16[104,1664]{1,0:T(8,128)(2,1)S(1)} %get-tuple-element.44), channel_id=1, source_target_pairs={{0,2},{1,3},{2,0},{3,1},{4,6},{5,7},{6,4},{7,5},{8,10},{9,11},{10,... | collective-permute-start | bytes 1038344 | tf_op jit(solution)/shard_map/ppermute | solution.py:466
  166.0 21.0 %copy-start.6 = (bf16[104,1664]{1,0:T(8,128)(2,1)}, bf16[104,1664]{1,0:T(8,128)(2,1)S(1)}, u32[]{:S(2)}) copy-start(bf16[104,1664]{1,0:T(8,128)(2,1)S(1)} %collective-permute-done.5.refs_6_) | copy-start | bytes 1038340
  166.0 20.9 %collective-permute-start = (bf16[104,1664]{1,0:T(8,128)(2,1)S(1)}, bf16[104,1664]{1,0:T(8,128)(2,1)S(1)}, u32[]{:S(2)}, u32[]{:S(2)}) collective-permute-start(bf16[104,1664]{1,0:T(8,128)(2,1)S(1)} %get-tuple-element.45), channel_id=1, source_target_pairs={{0,1},{1,2},{2,3},{3,0},{4,5},{5,6},{6,7},{7,4},{8,9},{9,10},{10,1... | collective-permute-start | bytes 1038344 | tf_op jit(solution)/shard_map/ppermute | solution.py:466
  172.9 14.1 %copy-start.7 = (bf16[104,1664]{1,0:T(8,128)(2,1)}, bf16[104,1664]{1,0:T(8,128)(2,1)S(1)}, u32[]{:S(2)}) copy-start(bf16[104,1664]{1,0:T(8,128)(2,1)S(1)} %collective-permute-done.4.refs_5_) | copy-start | bytes 1038340
  176.8 10.2 %copy-start.8 = (bf16[104,1664]{1,0:T(8,128)(2,1)}, bf16[104,1664]{1,0:T(8,128)(2,1)S(1)}, u32[]{:S(2)}) copy-start(bf16[104,1664]{1,0:T(8,128)(2,1)S(1)} %collective-permute-done.3.refs_4_) | copy-start | bytes 1038340
  176.8 10.2 %copy-start.9 = (bf16[104,1664]{1,0:T(8,128)(2,1)}, bf16[104,1664]{1,0:T(8,128)(2,1)S(1)}, u32[]{:S(2)}) copy-start(bf16[104,1664]{1,0:T(8,128)(2,1)S(1)} %collective-permute-done.2.refs_3_) | copy-start | bytes 1038340
  179.7 7.3 %copy-start.10 = (bf16[104,1664]{1,0:T(8,128)(2,1)}, bf16[104,1664]{1,0:T(8,128)(2,1)S(1)}, u32[]{:S(2)}) copy-start(bf16[104,1664]{1,0:T(8,128)(2,1)S(1)} %collective-permute-done.1.refs_2_) | copy-start | bytes 1038340
  187.0 0.7 copy-start.11
  221.3 20.2 %slice-start = ((s8[5537792]{0:T(1024)(128)(4,1)}), s8[4194304]{0:T(1024)(128)(4,1)S(1)}, s32[]{:S(2)}) async-start(s8[5537792]{0:T(1024)(128)(4,1)} %bitcast.15), calls=%async_computation.5 | async-start | bytes 8388608
  221.4 20.2 %copy-start.1 = (bf16[8,104,1664]{2,1,0:T(8,128)(2,1)S(1)}, bf16[8,104,1664]{2,1,0:T(8,128)(2,1)}, u32[]{:S(2)}) copy-start(bf16[8,104,1664]{2,1,0:T(8,128)(2,1)} %get-tuple-element.24.refs_0_.a_ref) | copy-start | bytes 8306692
  221.4 20.2 %slice-start.1 = ((s8[5537792]{0:T(1024)(128)(4,1)}), s8[1343488]{0:T(1024)(128)(4,1)S(1)}, s32[]{:S(2)}) async-start(s8[5537792]{0:T(1024)(128)(4,1)} %bitcast.15), calls=%async_computation.6 | async-start | bytes 2686976
  246.6 38.7 %all-to-all-start.4 = ((bf16[8,104,1664]{2,1,0:T(8,128)(2,1)}), bf16[8,104,1664]{2,1,0:T(8,128)(2,1)S(1)}, u32[]{:S(2)}, u32[]{:S(2)}) async-start(bf16[8,104,1664]{2,1,0:T(8,128)(2,1)} %get-tuple-element.33), calls=%async_computation.4 | async-start | bytes 5537792 | tf_op jit(solution)/shard_map/all_to_all | solution.py:638
